TPU v7x, 256 devices: a whole 4x4x8 slice. The times are simulated.
256 devices in a mesh: sec: 16 (over x_lo, y, core), strip: 16 (over z, x_hi).
Axes of the slice: x: 4 (x_hi: 2, x_lo: 2; x = x_hi * 2 + x_lo), y: 4, z: 8, core: 2. Of those that a mesh axis runs over, the one named last changes fastest.
Arguments:
- images: bfloat16 [16, 2048, 1024], P('sec', 'strip'), may hold values from -6 to 6
- row_weights: float32 [16, 4, 2048], P('sec', None, 'strip'), may hold values from 0.05 to 0.5
- row_shift: int32 [16, 16], P('sec', 'strip'), may hold values from -4 to 4
- col_weights: bfloat16 [16, 4, 1024], P('sec'), may hold values from 0.049804688 to 0.5
- col_shift: int32 [16], P('sec'), may hold values from -32 to 32
- pair_on: int32 [16, 3], replicated, may hold values 0 or 1
Outputs:
- grad_warped: float32 [16, 2048, 1024], P('sec', 'strip')
- displacement: float32 [2, 16, 2048, 1024], P(None, 'sec', 'strip')
All inputs are finite; a program needn't handle non-finite values.
Results may differ from a plain program's by a relative error of at most 0.0047.
Values may be sent and summed in bfloat16 or wider, within the bound.
No kernel may reach another device: no remote copies, remote signals or barrier semaphores. Data moves between devices by JAX's collectives and lax.ppermute only.
A program may use at most 64 MiB of HBM per device.

v0:
```python
import jax
import jax.numpy as jnp
from jax import lax
from jax.sharding import PartitionSpec as P

TAP_COUNT = 4
MAX_SHIFT = 4
RADIUS = 4
PAIR_REACH = 3


variance_bias = 0.25


def padded_2(block, sides, width):
    for axis, dim in sides:
        count = lax.axis_size(axis)
        forward = [(i, i + 1) for i in range(count - 1)]
        backward = [(target, source) for source, target in forward]
        low = lax.ppermute(
            lax.slice_in_dim(block, block.shape[dim] - width, None, axis=dim), axis, forward
        )
        high = lax.ppermute(lax.slice_in_dim(block, 0, width, axis=dim), axis, backward)
        block = jnp.concatenate([low, block, high], axis=dim)
    return block


def passed_along(value, axis, steps):
    count = lax.axis_size(axis)
    initial, last = (max(0, -steps), min(count, count - steps))
    return lax.ppermute(value, axis, [(source, source + steps) for source in range(initial, last)])


def box_rows(field, out_rows):
    running = field[..., 0:out_rows, :]
    for step_row in range(1, 2 * RADIUS + 1):
        running = running + field[..., step_row : step_row + out_rows, :]
    return running


def box_cols(field):
    col_count = field.shape[-1]
    widths = [(0, 0)] * (field.ndim - 1) + [(RADIUS, RADIUS)]
    padded = jnp.pad(field, widths)
    running = padded[..., 0:col_count]
    for step_col in range(1, 2 * RADIUS + 1):
        running = running + padded[..., step_col : step_col + col_count]
    return running


def box_sum(field, out_rows):
    return box_cols(box_rows(field, out_rows))


def pair_grads(left_rim, right_rim, weight, depth, row_count):
    box_cells = float((2 * RADIUS + 1) ** 2)
    left_field = left_rim.astype(jnp.float32)
    right_field = right_rim.astype(jnp.float32)
    mean_left = box_sum(left_field, row_count) / box_cells
    mean_right = box_sum(right_field, row_count) / box_cells
    var_left = (
        box_sum(left_field * left_field, row_count) / box_cells
        - mean_left * mean_left
        + variance_bias
    )
    var_right = (
        box_sum(right_field * right_field, row_count) / box_cells
        - mean_right * mean_right
        + variance_bias
    )
    covariance = box_sum(left_field * right_field, row_count) / box_cells - mean_left * mean_right
    denom_root = jnp.sqrt(var_left * var_right)
    ncc_value = covariance / denom_root
    g_cov = -weight / denom_root
    g_left = weight * ncc_value / (2.0 * var_left)
    g_right = weight * ncc_value / (2.0 * var_right)
    h_left = -g_cov * mean_right - 2.0 * g_left * mean_left
    h_right = -g_cov * mean_left - 2.0 * g_right * mean_right
    stacked = jnp.stack([g_cov, g_left, g_right, h_left, h_right])
    widened = padded_2(stacked.astype(jnp.bfloat16), (("strip", 1),), RADIUS).astype(stacked.dtype)
    boxed = box_sum(widened, row_count)
    mid_left = left_field[depth : depth + row_count]
    mid_right = right_field[depth : depth + row_count]
    grad_left = (boxed[3] + 2.0 * mid_left * boxed[1] + mid_right * boxed[0]) / box_cells
    grad_right = (boxed[4] + 2.0 * mid_right * boxed[2] + mid_left * boxed[0]) / box_cells
    return (grad_left, grad_right)


def per_device(images, row_weights, row_shift, col_weights, col_shift, pair_on):
    sec_count, row_count, col_count = images.shape
    sec_pos = lax.axis_index("sec")
    total_sections = sec_count * lax.axis_size("sec")
    source_depth = MAX_SHIFT + 2
    source = padded_2(images, (("strip", 1),), source_depth)

    def warp_rows(source_sec, weights, shift_value):
        running = jnp.zeros((row_count, col_count), jnp.float32)
        for tap_index in range(TAP_COUNT):
            window = lax.dynamic_slice_in_dim(
                source_sec, source_depth - 1 + tap_index + shift_value, row_count, 0
            )
            running = running + weights[tap_index][:, None] * window.astype(jnp.float32)
        return running.astype(jnp.bfloat16)

    row_warped = jax.vmap(warp_rows)(source, row_weights, row_shift[:, 0])
    row_ids = lax.broadcasted_iota(jnp.int32, (col_count, col_count), 0)
    col_ids = lax.broadcasted_iota(jnp.int32, (col_count, col_count), 1)

    def column_matrix(weights, shift_value):
        offsets = row_ids - col_ids - shift_value + 1
        matrix = jnp.zeros((col_count, col_count), jnp.bfloat16)
        for tap_index in range(TAP_COUNT):
            matrix = jnp.where(offsets == tap_index, weights[tap_index][None, :], matrix)
        return matrix

    matrices = jax.vmap(column_matrix)(col_weights, col_shift)
    warped = jnp.einsum(
        "srw,swv->srv", row_warped, matrices, preferred_element_type=jnp.float32
    ).astype(jnp.bfloat16)
    depth = RADIUS
    rimmed = padded_2(warped, (("strip", 1),), depth)
    hops = (PAIR_REACH + sec_count - 1) // sec_count
    first_global = sec_pos * sec_count
    padded_on = jnp.concatenate([jnp.zeros((PAIR_REACH, PAIR_REACH), jnp.int32), pair_on], 0)
    on_rows = lax.dynamic_slice_in_dim(padded_on, first_global, sec_count + PAIR_REACH, 0).astype(
        jnp.float32
    )
    pieces = {}
    section = 0
    pieces[section] = rimmed[section]
    for hop in range(1, hops + 1):
        arrived = passed_along(rimmed, "sec", -hop)
        slot_pos = 0
        pieces[hop * sec_count + slot_pos] = arrived[slot_pos]
    gradient_sums = {}
    section = 0
    for distance in range(1, PAIR_REACH + 1):
        global_first = first_global + section
        inside = (global_first >= 0) & (global_first + distance < total_sections)
        grad_left, grad_right = pair_grads(
            pieces[section],
            pieces[section + distance],
            on_rows[section + PAIR_REACH, distance - 1] * inside.astype(jnp.float32),
            depth,
            row_count,
        )
        for target, term in ((section, grad_left), (section + distance, grad_right)):
            if target in gradient_sums:
                gradient_sums[target] = gradient_sums[target] + term
            else:
                gradient_sums[target] = term
    section = 0
    own_grads = [gradient_sums[section]]
    for hop in range(1, hops + 1):
        parcel = jnp.stack([gradient_sums[hop * sec_count]])
        returned = passed_along(parcel, "sec", hop)
        slot_pos = 0
        own_grads[slot_pos] = own_grads[slot_pos] + returned[slot_pos]
    grad_warped = jnp.stack(own_grads)
    middle = rimmed[:, depth - 1 : depth + row_count + 1].astype(jnp.float32)
    slope_rows = (middle[:, 2:] - middle[:, :-2]) * 0.5
    centre = middle[:, 1:-1]
    side_padded = jnp.pad(centre, ((0, 0), (0, 0), (1, 1)))
    slope_cols = (side_padded[:, :, 2:] - side_padded[:, :, :-2]) * 0.5
    products = jnp.stack([grad_warped * slope_rows, grad_warped * slope_cols])
    widened = padded_2(products, (("strip", 2),), RADIUS)
    displacement = -box_sum(widened, row_count) / 9.0
    return (grad_warped, displacement)


def solution(mesh):
    return jax.shard_map(
        per_device,
        mesh=mesh,
        in_specs=(
            P("sec", "strip", None),
            P("sec", None, "strip"),
            P("sec", "strip"),
            P("sec", None, None),
            P("sec"),
            P(),
        ),
        out_specs=(P("sec", "strip", None), P(None, "sec", "strip", None)),
        check_vma=False,
    )
```

profile of v0, /device:TPU:110, one launch (start us, length us, event | category | flops | bytes accessed | tf_op | source)
XLA Modules:
  0.0 180.4 jit_solution(15730013100611856684)
XLA Ops:
  1.4 5.9 %collective-permute-start = (bf16[1,6,1024]{2,1,0:T(8,128)(2,1)S(1)}, bf16[1,6,1024]{2,1,0:T(8,128)(2,1)S(1)}, u32[]{:S(2)}, u32[]{:S(2)}) collective-permute-start(bf16[1,6,1024]{2,1,0:T(8,128)(2,1)S(1)} %get-tuple-element.109), channel_id=1, source_target_pairs={{0,1},{1,2},{2,3},{3,4},{4,5},{5,6},{6,7},{7,8},{8,9},{9,10},{10,1... | collective-permute-start | bytes 36872 | tf_op jit(solution)/shard_map/ppermute | solution.py:20
  7.2 1.9 %collective-permute-start.1 = (bf16[1,6,1024]{2,1,0:T(8,128)(2,1)S(1)}, bf16[1,6,1024]{2,1,0:T(8,128)(2,1)S(1)}, u32[]{:S(2)}, u32[]{:S(2)}) collective-permute-start(bf16[1,6,1024]{2,1,0:T(8,128)(2,1)S(1)} %get-tuple-element.110), channel_id=1, source_target_pairs={{1,0},{2,1},{3,2},{4,3},{5,4},{6,5},{7,6},{8,7},{9,8},{10,9},{11,1... | collective-permute-start | bytes 36872 | tf_op jit(solution)/shard_map/ppermute | solution.py:23
  9.2 0.8 slice_bitcast_fusion.3
  10.0 0.9 slice_reduce_fusion.3
  12.2 4.3 %collective-permute-done.1 = bf16[1,6,1024]{2,1,0:T(8,128)(2,1)S(1)} collective-permute-done((bf16[1,6,1024]{2,1,0:T(8,128)(2,1)S(1)}, bf16[1,6,1024]{2,1,0:T(8,128)(2,1)S(1)}, u32[]{:S(2)}, u32[]{:S(2)}) %collective-permute-start.1) | collective-permute-done | bytes 12320 | tf_op jit(solution)/shard_map/ppermute | solution.py:23
  16.5 1.0 pad_maximum_fusion.2
  17.5 2.3 %fusion.37 = bf16[1,128,1024]{2,1,0:T(8,128)(2,1)S(1)} fusion(s32[]{:T(128)} %bitcast.118, bf16[1024]{0:T(1024)(128)(2,1)S(1)} %get-tuple-element.48, bf16[1024]{0:T(1024)(128)(2,1)S(1)} %get-tuple-element.49, bf16[1024]{0:T(1024)(128)(2,1)S(1)} %get-tuple-element.47, bf16[1024]{0:T(1024)(128)(2,1)S(1)} %get-tuple-element.46, ...), kind=kOutput, calls=%fused_computation.91 | convolution fusion | flops 281673728 | bytes 1320980 | tf_op jit(solution)/shard_map/srw,swv->srv/dot_general | solution.py:117
  19.9 3.3 %collective-permute-start.2 = (bf16[1,4,1024]{2,1,0:T(4,128)(2,1)S(1)}, bf16[1,4,1024]{2,1,0:T(4,128)(2,1)S(1)}, u32[]{:S(2)}, u32[]{:S(2)}) collective-permute-start(bf16[1,4,1024]{2,1,0:T(4,128)(2,1)S(1)} %get-tuple-element.107), channel_id=1, source_target_pairs={{0,1},{1,2},{2,3},{3,4},{4,5},{5,6},{6,7},{7,8},{8,9},{9,10},{10,1... | collective-permute-start | bytes 24584 | tf_op jit(solution)/shard_map/ppermute | solution.py:20
  23.2 4.0 %collective-permute-start.3 = (bf16[1,4,1024]{2,1,0:T(4,128)(2,1)S(1)}, bf16[1,4,1024]{2,1,0:T(4,128)(2,1)S(1)}, u32[]{:S(2)}, u32[]{:S(2)}) collective-permute-start(bf16[1,4,1024]{2,1,0:T(4,128)(2,1)S(1)} %get-tuple-element.108), channel_id=1, source_target_pairs={{1,0},{2,1},{3,2},{4,3},{5,4},{6,5},{7,6},{8,7},{9,8},{10,9},{11,1... | collective-permute-start | bytes 24584 | tf_op jit(solution)/shard_map/ppermute | solution.py:23
  27.4 5.0 %collective-permute-done.3 = bf16[1,4,1024]{2,1,0:T(4,128)(2,1)S(1)} collective-permute-done((bf16[1,4,1024]{2,1,0:T(4,128)(2,1)S(1)}, bf16[1,4,1024]{2,1,0:T(4,128)(2,1)S(1)}, u32[]{:S(2)}, u32[]{:S(2)}) %collective-permute-start.3) | collective-permute-done | bytes 8224 | tf_op jit(solution)/shard_map/ppermute | solution.py:23
  32.5 2.4 %collective-permute-start.7 = (bf16[1,136,1024]{2,1,0:T(8,128)(2,1)S(1)}, bf16[1,136,1024]{2,1,0:T(8,128)(2,1)S(1)}, u32[]{:S(2)}, u32[]{:S(2)}) collective-permute-start(bf16[1,136,1024]{2,1,0:T(8,128)(2,1)S(1)} %get-tuple-element.106), channel_id=1, source_target_pairs={{32,0},{48,16},{64,32},{80,48},{96,64},{112,80},{128,96},{144,112}... | collective-permute-start | bytes 835592 | tf_op jit(solution)/shard_map/ppermute | solution.py:31
  37.3 1.9 %collective-permute-start.10 = (bf16[1,136,1024]{2,1,0:T(8,128)(2,1)S(1)}, bf16[1,136,1024]{2,1,0:T(8,128)(2,1)S(1)}, u32[]{:S(2)}, u32[]{:S(2)}) collective-permute-start(bf16[1,136,1024]{2,1,0:T(8,128)(2,1)S(1)} %get-tuple-element.106), channel_id=1, source_target_pairs={{48,0},{64,16},{80,32},{96,48},{112,64},{128,80},{144,96},{160,112... | collective-permute-start | bytes 835592 | tf_op jit(solution)/shard_map/ppermute | solution.py:31
  39.2 4.7 %collective-permute-start.4 = (bf16[1,136,1024]{2,1,0:T(8,128)(2,1)S(1)}, bf16[1,136,1024]{2,1,0:T(8,128)(2,1)S(1)}, u32[]{:S(2)}, u32[]{:S(2)}) collective-permute-start(bf16[1,136,1024]{2,1,0:T(8,128)(2,1)S(1)} %get-tuple-element.106), channel_id=1, source_target_pairs={{16,0},{32,16},{48,32},{64,48},{80,64},{96,80},{112,96},{128,112},... | collective-permute-start | bytes 835592 | tf_op jit(solution)/shard_map/ppermute | solution.py:31
  44.8 4.0 %collective-permute-done.10 = bf16[1,136,1024]{2,1,0:T(8,128)(2,1)S(1)} collective-permute-done((bf16[1,136,1024]{2,1,0:T(8,128)(2,1)S(1)}, bf16[1,136,1024]{2,1,0:T(8,128)(2,1)S(1)}, u32[]{:S(2)}, u32[]{:S(2)}) %collective-permute-start.10) | collective-permute-done | bytes 278560 | tf_op jit(solution)/shard_map/ppermute | solution.py:31
  49.8 0.7 fusion.203
  50.6 0.7 fusion.210
  51.3 0.7 fusion.209
  52.1 0.7 fusion.196
  52.8 4.8 %bitcast_dynamic-update-slice_fusion.8 = (bf16[5,128,1024]{2,1,0:T(8,128)(2,1)S(1)}, f32[128,1024]{1,0:T(8,128)S(1)}, f32[128,1024]{1,0:T(8,128)S(1)}, f32[128,1...) fusion(f32[]{:T(128)S(6)} %neg.24, f32[128,1024]{1,0:T(8,128)S(1)} %get-tuple-element.123, ...), kind=kLoop, calls=%fused_computation.522 | loop fusion | flops 5898239 | bytes 4980740
  57.6 2.2 %bitcast_dynamic-update-slice_fusion.5 = (bf16[5,128,1024]{2,1,0:T(8,128)(2,1)S(1)}, f32[128,1024]{1,0:T(8,128)S(1)}, f32[128,1024]{1,0:T(8,128)S(1)}, f32[128,1024]{1,0:T(8,128)S(1)}) fusion(f32[128,1024]{1,0:T(8,128)S(1)} %get-tuple-element.58, f32[]{:T(128)S(6)} %neg.26, f32[128,1024]{1,0:T(8,128)S(1)} %get-tuple-element.121, f32[128,1024]{1,0:T(8,128)S(1)} %fusion.204), kind=kLoop, calls=%fused_computation.519 | loop fusion | flops 3145727 | bytes 3407876
  59.9 4.6 %bitcast_dynamic-update-slice_fusion.7 = (bf16[5,128,1024]{2,1,0:T(8,128)(2,1)S(1)}, f32[128,1024]{1,0:T(8,128)S(1)}, bf16[5,128,1024]{2,1,0:T(8,128)(2,1)S(1)},...) fusion(bf16[5,128,1024]{2,1,0:T(8,128)(2,1)S(1)} %get-tuple-ele, ...), kind=kLoop, calls=%fused_computation.521 | loop fusion | flops 7471103 | bytes 8650764
  64.5 1.2 bitcast_dynamic-update-slice_fusion.1
  66.6 0.9 fusion.226
  67.5 1.9 %collective-permute-start.11 = (bf16[5,4,1024]{2,1,0:T(4,128)(2,1)S(1)}, bf16[5,4,1024]{2,1,0:T(4,128)(2,1)S(1)}, u32[]{:S(2)}, u32[]{:S(2)}) collective-permute-start(bf16[5,4,1024]{2,1,0:T(4,128)(2,1)S(1)} %get-tuple-element.76), channel_id=1, source_target_pairs={{0,1},{1,2},{2,3},{3,4},{4,5},{5,6},{6,7},{7,8},{8,9},{9,10},{10,1... | collective-permute-start | bytes 122888 | tf_op jit(solution)/shard_map/ppermute | solution.py:20
  69.4 5.4 %collective-permute-start.12 = (bf16[5,4,1024]{2,1,0:T(4,128)(2,1)S(1)}, bf16[5,4,1024]{2,1,0:T(4,128)(2,1)S(1)}, u32[]{:S(2)}, u32[]{:S(2)}) collective-permute-start(bf16[5,4,1024]{2,1,0:T(4,128)(2,1)S(1)} %get-tuple-element.77), channel_id=1, source_target_pairs={{1,0},{2,1},{3,2},{4,3},{5,4},{6,5},{7,6},{8,7},{9,8},{10,9},{11,1... | collective-permute-start | bytes 122888 | tf_op jit(solution)/shard_map/ppermute | solution.py:23
  74.9 4.0 %collective-permute-start.8 = (bf16[5,4,1024]{2,1,0:T(4,128)(2,1)S(1)}, bf16[5,4,1024]{2,1,0:T(4,128)(2,1)S(1)}, u32[]{:S(2)}, u32[]{:S(2)}) collective-permute-start(bf16[5,4,1024]{2,1,0:T(4,128)(2,1)S(1)} %get-tuple-element.74), channel_id=1, source_target_pairs={{0,1},{1,2},{2,3},{3,4},{4,5},{5,6},{6,7},{7,8},{8,9},{9,10},{10,1... | collective-permute-start | bytes 122888 | tf_op jit(solution)/shard_map/ppermute | solution.py:20
  78.9 3.3 %collective-permute-start.9 = (bf16[5,4,1024]{2,1,0:T(4,128)(2,1)S(1)}, bf16[5,4,1024]{2,1,0:T(4,128)(2,1)S(1)}, u32[]{:S(2)}, u32[]{:S(2)}) collective-permute-start(bf16[5,4,1024]{2,1,0:T(4,128)(2,1)S(1)} %get-tuple-element.75), channel_id=1, source_target_pairs={{1,0},{2,1},{3,2},{4,3},{5,4},{6,5},{7,6},{8,7},{9,8},{10,9},{11,1... | collective-permute-start | bytes 122888 | tf_op jit(solution)/shard_map/ppermute | solution.py:23
  82.3 6.1 %collective-permute-start.5 = (bf16[5,4,1024]{2,1,0:T(4,128)(2,1)S(1)}, bf16[5,4,1024]{2,1,0:T(4,128)(2,1)S(1)}, u32[]{:S(2)}, u32[]{:S(2)}) collective-permute-start(bf16[5,4,1024]{2,1,0:T(4,128)(2,1)S(1)} %get-tuple-element.72), channel_id=1, source_target_pairs={{0,1},{1,2},{2,3},{3,4},{4,5},{5,6},{6,7},{7,8},{8,9},{9,10},{10,1... | collective-permute-start | bytes 122888 | tf_op jit(solution)/shard_map/ppermute | solution.py:20
  88.5 1.9 %collective-permute-start.6 = (bf16[5,4,1024]{2,1,0:T(4,128)(2,1)S(1)}, bf16[5,4,1024]{2,1,0:T(4,128)(2,1)S(1)}, u32[]{:S(2)}, u32[]{:S(2)}) collective-permute-start(bf16[5,4,1024]{2,1,0:T(4,128)(2,1)S(1)} %get-tuple-element.73), channel_id=1, source_target_pairs={{1,0},{2,1},{3,2},{4,3},{5,4},{6,5},{7,6},{8,7},{9,8},{10,9},{11,1... | collective-permute-start | bytes 122888 | tf_op jit(solution)/shard_map/ppermute | solution.py:23
  90.9 2.1 %slice_add_fusion = f32[5,128,1024]{2,1,0:T(8,128)S(1)} fusion(f32[5,136,1024]{2,1,0:T(8,128)S(1)} %maximum_convert_fusion.2), kind=kLoop, calls=%fused_computation.57 | loop fusion | flops 5242880 | bytes 26214400 | tf_op jit(solution)/shard_map/add | solution.py:37
  93.0 5.6 %fusion.31 = f32[5,128,1024]{2,1,0:T(8,128)S(1)} fusion(f32[5,128,1024]{2,1,0:T(8,128)S(1)} %slice_add_fusion), kind=kLoop, calls=%fused_computation.56 | loop fusion | flops 5242880 | bytes 5242880 | tf_op jit(solution)/shard_map/add | solution.py:47
  99.0 1.9 %slice_add_fusion.8 = f32[5,128,1024]{2,1,0:T(8,128)S(1)} fusion(f32[5,136,1024]{2,1,0:T(8,128)S(1)} %maximum_convert_fusion.1), kind=kLoop, calls=%fused_computation.65 | loop fusion | flops 5242880 | bytes 26214400 | tf_op jit(solution)/shard_map/add | solution.py:37
  100.9 5.6 %fusion.23 = f32[5,128,1024]{2,1,0:T(8,128)S(1)} fusion(f32[5,128,1024]{2,1,0:T(8,128)S(1)} %slice_add_fusion.8), kind=kLoop, calls=%fused_computation.48 | loop fusion | flops 5242880 | bytes 5242880 | tf_op jit(solution)/shard_map/add | solution.py:47
  107.0 1.9 %slice_add_fusion.16 = f32[5,128,1024]{2,1,0:T(8,128)S(1)} fusion(f32[5,136,1024]{2,1,0:T(8,128)S(1)} %maximum_convert_fusion), kind=kLoop, calls=%fused_computation.73 | loop fusion | flops 5242880 | bytes 26214400 | tf_op jit(solution)/shard_map/add | solution.py:37
  108.9 5.8 %fusion.15 = f32[5,128,1024]{2,1,0:T(8,128)S(1)} fusion(f32[5,128,1024]{2,1,0:T(8,128)S(1)} %slice_add_fusion.16), kind=kLoop, calls=%fused_computation.40 | loop fusion | flops 5242880 | bytes 5242880 | tf_op jit(solution)/shard_map/add | solution.py:47
  114.7 0.8 fusion.188
  115.6 2.5 %collective-permute-start.13 = (f32[1,128,1024]{2,1,0:T(8,128)S(1)}, f32[1,128,1024]{2,1,0:T(8,128)S(1)}, u32[]{:S(2)}, u32[]{:S(2)}) collective-permute-start(f32[1,128,1024]{2,1,0:T(8,128)S(1)} %get-tuple-element.88), channel_id=1, source_target_pairs={{0,16},{16,32},{32,48},{48,64},{64,80},{80,96},{96,112},{112,128},... | collective-permute-start | bytes 1572872 | tf_op jit(solution)/shard_map/ppermute | solution.py:31
  118.0 3.0 %collective-permute-start.14 = (f32[1,128,1024]{2,1,0:T(8,128)S(1)}, f32[1,128,1024]{2,1,0:T(8,128)S(1)}, u32[]{:S(2)}, u32[]{:S(2)}) collective-permute-start(f32[1,128,1024]{2,1,0:T(8,128)S(1)} %get-tuple-element.89), channel_id=1, source_target_pairs={{0,32},{16,48},{32,64},{48,80},{64,96},{80,112},{96,128},{112,144}... | collective-permute-start | bytes 1572872 | tf_op jit(solution)/shard_map/ppermute | solution.py:31
  121.1 2.5 %collective-permute-start.15 = (f32[1,128,1024]{2,1,0:T(8,128)S(1)}, f32[1,128,1024]{2,1,0:T(8,128)S(1)}, u32[]{:S(2)}, u32[]{:S(2)}) collective-permute-start(f32[1,128,1024]{2,1,0:T(8,128)S(1)} %get-tuple-element.90), channel_id=1, source_target_pairs={{0,48},{16,64},{32,80},{48,96},{64,112},{80,128},{96,144},{112,160... | collective-permute-start | bytes 1572872 | tf_op jit(solution)/shard_map/ppermute | solution.py:31
  123.6 4.9 %collective-permute-done.13 = f32[1,128,1024]{2,1,0:T(8,128)S(1)} collective-permute-done((f32[1,128,1024]{2,1,0:T(8,128)S(1)}, f32[1,128,1024]{2,1,0:T(8,128)S(1)}, u32[]{:S(2)}, u32[]{:S(2)}) %collective-permute-start.13) | collective-permute-done | bytes 524320 | tf_op jit(solution)/shard_map/ppermute | solution.py:31
  128.5 6.4 %collective-permute-done.14 = f32[1,128,1024]{2,1,0:T(8,128)S(1)} collective-permute-done((f32[1,128,1024]{2,1,0:T(8,128)S(1)}, f32[1,128,1024]{2,1,0:T(8,128)S(1)}, u32[]{:S(2)}, u32[]{:S(2)}) %collective-permute-start.14) | collective-permute-done | bytes 524320 | tf_op jit(solution)/shard_map/ppermute | solution.py:31
  134.9 22.9 %collective-permute-done.15 = f32[1,128,1024]{2,1,0:T(8,128)S(1)} collective-permute-done((f32[1,128,1024]{2,1,0:T(8,128)S(1)}, f32[1,128,1024]{2,1,0:T(8,128)S(1)}, u32[]{:S(2)}, u32[]{:S(2)}) %collective-permute-start.15) | collective-permute-done | bytes 524320 | tf_op jit(solution)/shard_map/ppermute | solution.py:31
  157.7 1.1 fusion.179
  159.2 7.5 %collective-permute-start.16 = (f32[2,1,4,1024]{3,2,1,0:T(4,128)S(1)}, f32[2,1,4,1024]{3,2,1,0:T(4,128)S(1)}, u32[]{:S(2)}, u32[]{:S(2)}) collective-permute-start(f32[2,1,4,1024]{3,2,1,0:T(4,128)S(1)} %get-tuple-element.80), channel_id=1, source_target_pairs={{0,1},{1,2},{2,3},{3,4},{4,5},{5,6},{6,7},{7,8},{8,9},{9,10},{10,1... | collective-permute-start | bytes 98312 | tf_op jit(solution)/shard_map/ppermute | solution.py:20
  166.7 1.9 %collective-permute-start.17 = (f32[2,1,4,1024]{3,2,1,0:T(4,128)S(1)}, f32[2,1,4,1024]{3,2,1,0:T(4,128)S(1)}, u32[]{:S(2)}, u32[]{:S(2)}) collective-permute-start(f32[2,1,4,1024]{3,2,1,0:T(4,128)S(1)} %get-tuple-element.81), channel_id=1, source_target_pairs={{1,0},{2,1},{3,2},{4,3},{5,4},{6,5},{7,6},{8,7},{9,8},{10,9},{11,1... | collective-permute-start | bytes 98312 | tf_op jit(solution)/shard_map/ppermute | solution.py:23
  168.7 7.5 %collective-permute-done.17 = f32[2,1,4,1024]{3,2,1,0:T(4,128)S(1)} collective-permute-done((f32[2,1,4,1024]{3,2,1,0:T(4,128)S(1)}, f32[2,1,4,1024]{3,2,1,0:T(4,128)S(1)}, u32[]{:S(2)}, u32[]{:S(2)}) %collective-permute-start.17) | collective-permute-done | bytes 32800 | tf_op jit(solution)/shard_map/ppermute | solution.py:23
  176.4 0.8 fusion.54
  177.2 3.2 %fusion.49 = f32[2,1,128,1024]{3,2,1,0:T(8,128)} fusion(f32[2,1,128,1024]{3,2,1,0:T(8,128)S(1)} %fusion.54), kind=kLoop, calls=%fused_computation.111 | loop fusion | flops 2621440 | bytes 2097152 | tf_op jit(solution)/shard_map/div | solution.py:167
  (41 shorter events, 6.4 us)
Async XLA Ops:
  1.4 10.9 %collective-permute-start = (bf16[1,6,1024]{2,1,0:T(8,128)(2,1)S(1)}, bf16[1,6,1024]{2,1,0:T(8,128)(2,1)S(1)}, u32[]{:S(2)}, u32[]{:S(2)}) collective-permute-start(bf16[1,6,1024]{2,1,0:T(8,128)(2,1)S(1)} %get-tuple-element.109), channel_id=1, source_target_pairs={{0,1},{1,2},{2,3},{3,4},{4,5},{5,6},{6,7},{7,8},{8,9},{9,10},{10,1... | collective-permute-start | bytes 36872 | tf_op jit(solution)/shard_map/ppermute | solution.py:20
  7.2 9.2 %collective-permute-start.1 = (bf16[1,6,1024]{2,1,0:T(8,128)(2,1)S(1)}, bf16[1,6,1024]{2,1,0:T(8,128)(2,1)S(1)}, u32[]{:S(2)}, u32[]{:S(2)}) collective-permute-start(bf16[1,6,1024]{2,1,0:T(8,128)(2,1)S(1)} %get-tuple-element.110), channel_id=1, source_target_pairs={{1,0},{2,1},{3,2},{4,3},{5,4},{6,5},{7,6},{8,7},{9,8},{10,9},{11,1... | collective-permute-start | bytes 36872 | tf_op jit(solution)/shard_map/ppermute | solution.py:23
  17.5 9.7 %copy-start.1 = (s32[16,3]{0,1:T(4,128)S(1)}, s32[16,3]{0,1:T(4,128)}, u32[]{:S(2)}) copy-start(s32[16,3]{0,1:T(4,128)} %param.11) | copy-start | bytes 580
  19.9 7.5 %collective-permute-start.2 = (bf16[1,4,1024]{2,1,0:T(4,128)(2,1)S(1)}, bf16[1,4,1024]{2,1,0:T(4,128)(2,1)S(1)}, u32[]{:S(2)}, u32[]{:S(2)}) collective-permute-start(bf16[1,4,1024]{2,1,0:T(4,128)(2,1)S(1)} %get-tuple-element.107), channel_id=1, source_target_pairs={{0,1},{1,2},{2,3},{3,4},{4,5},{5,6},{6,7},{7,8},{8,9},{9,10},{10,1... | collective-permute-start | bytes 24584 | tf_op jit(solution)/shard_map/ppermute | solution.py:20
  23.2 9.2 %collective-permute-start.3 = (bf16[1,4,1024]{2,1,0:T(4,128)(2,1)S(1)}, bf16[1,4,1024]{2,1,0:T(4,128)(2,1)S(1)}, u32[]{:S(2)}, u32[]{:S(2)}) collective-permute-start(bf16[1,4,1024]{2,1,0:T(4,128)(2,1)S(1)} %get-tuple-element.108), channel_id=1, source_target_pairs={{1,0},{2,1},{3,2},{4,3},{5,4},{6,5},{7,6},{8,7},{9,8},{10,9},{11,1... | collective-permute-start | bytes 24584 | tf_op jit(solution)/shard_map/ppermute | solution.py:23
  32.5 11.9 %collective-permute-start.7 = (bf16[1,136,1024]{2,1,0:T(8,128)(2,1)S(1)}, bf16[1,136,1024]{2,1,0:T(8,128)(2,1)S(1)}, u32[]{:S(2)}, u32[]{:S(2)}) collective-permute-start(bf16[1,136,1024]{2,1,0:T(8,128)(2,1)S(1)} %get-tuple-element.106), channel_id=1, source_target_pairs={{32,0},{48,16},{64,32},{80,48},{96,64},{112,80},{128,96},{144,112}... | collective-permute-start | bytes 835592 | tf_op jit(solution)/shard_map/ppermute | solution.py:31
  37.3 11.5 %collective-permute-start.10 = (bf16[1,136,1024]{2,1,0:T(8,128)(2,1)S(1)}, bf16[1,136,1024]{2,1,0:T(8,128)(2,1)S(1)}, u32[]{:S(2)}, u32[]{:S(2)}) collective-permute-start(bf16[1,136,1024]{2,1,0:T(8,128)(2,1)S(1)} %get-tuple-element.106), channel_id=1, source_target_pairs={{48,0},{64,16},{80,32},{96,48},{112,64},{128,80},{144,96},{160,112... | collective-permute-start | bytes 835592 | tf_op jit(solution)/shard_map/ppermute | solution.py:31
  39.2 10.0 %collective-permute-start.4 = (bf16[1,136,1024]{2,1,0:T(8,128)(2,1)S(1)}, bf16[1,136,1024]{2,1,0:T(8,128)(2,1)S(1)}, u32[]{:S(2)}, u32[]{:S(2)}) collective-permute-start(bf16[1,136,1024]{2,1,0:T(8,128)(2,1)S(1)} %get-tuple-element.106), channel_id=1, source_target_pairs={{16,0},{32,16},{48,32},{64,48},{80,64},{96,80},{112,96},{128,112},... | collective-permute-start | bytes 835592 | tf_op jit(solution)/shard_map/ppermute | solution.py:31
  67.5 21.0 %collective-permute-start.11 = (bf16[5,4,1024]{2,1,0:T(4,128)(2,1)S(1)}, bf16[5,4,1024]{2,1,0:T(4,128)(2,1)S(1)}, u32[]{:S(2)}, u32[]{:S(2)}) collective-permute-start(bf16[5,4,1024]{2,1,0:T(4,128)(2,1)S(1)} %get-tuple-element.76), channel_id=1, source_target_pairs={{0,1},{1,2},{2,3},{3,4},{4,5},{5,6},{6,7},{7,8},{8,9},{9,10},{10,1... | collective-permute-start | bytes 122888 | tf_op jit(solution)/shard_map/ppermute | solution.py:20
  69.4 21.0 %collective-permute-start.12 = (bf16[5,4,1024]{2,1,0:T(4,128)(2,1)S(1)}, bf16[5,4,1024]{2,1,0:T(4,128)(2,1)S(1)}, u32[]{:S(2)}, u32[]{:S(2)}) collective-permute-start(bf16[5,4,1024]{2,1,0:T(4,128)(2,1)S(1)} %get-tuple-element.77), channel_id=1, source_target_pairs={{1,0},{2,1},{3,2},{4,3},{5,4},{6,5},{7,6},{8,7},{9,8},{10,9},{11,1... | collective-permute-start | bytes 122888 | tf_op jit(solution)/shard_map/ppermute | solution.py:23
  74.9 23.7 %collective-permute-start.8 = (bf16[5,4,1024]{2,1,0:T(4,128)(2,1)S(1)}, bf16[5,4,1024]{2,1,0:T(4,128)(2,1)S(1)}, u32[]{:S(2)}, u32[]{:S(2)}) collective-permute-start(bf16[5,4,1024]{2,1,0:T(4,128)(2,1)S(1)} %get-tuple-element.74), channel_id=1, source_target_pairs={{0,1},{1,2},{2,3},{3,4},{4,5},{5,6},{6,7},{7,8},{8,9},{9,10},{10,1... | collective-permute-start | bytes 122888 | tf_op jit(solution)/shard_map/ppermute | solution.py:20
  78.9 19.6 %collective-permute-start.9 = (bf16[5,4,1024]{2,1,0:T(4,128)(2,1)S(1)}, bf16[5,4,1024]{2,1,0:T(4,128)(2,1)S(1)}, u32[]{:S(2)}, u32[]{:S(2)}) collective-permute-start(bf16[5,4,1024]{2,1,0:T(4,128)(2,1)S(1)} %get-tuple-element.75), channel_id=1, source_target_pairs={{1,0},{2,1},{3,2},{4,3},{5,4},{6,5},{7,6},{8,7},{9,8},{10,9},{11,1... | collective-permute-start | bytes 122888 | tf_op jit(solution)/shard_map/ppermute | solution.py:23
  82.3 24.2 %collective-permute-start.5 = (bf16[5,4,1024]{2,1,0:T(4,128)(2,1)S(1)}, bf16[5,4,1024]{2,1,0:T(4,128)(2,1)S(1)}, u32[]{:S(2)}, u32[]{:S(2)}) collective-permute-start(bf16[5,4,1024]{2,1,0:T(4,128)(2,1)S(1)} %get-tuple-element.72), channel_id=1, source_target_pairs={{0,1},{1,2},{2,3},{3,4},{4,5},{5,6},{6,7},{7,8},{8,9},{9,10},{10,1... | collective-permute-start | bytes 122888 | tf_op jit(solution)/shard_map/ppermute | solution.py:20
  88.5 18.1 %collective-permute-start.6 = (bf16[5,4,1024]{2,1,0:T(4,128)(2,1)S(1)}, bf16[5,4,1024]{2,1,0:T(4,128)(2,1)S(1)}, u32[]{:S(2)}, u32[]{:S(2)}) collective-permute-start(bf16[5,4,1024]{2,1,0:T(4,128)(2,1)S(1)} %get-tuple-element.73), channel_id=1, source_target_pairs={{1,0},{2,1},{3,2},{4,3},{5,4},{6,5},{7,6},{8,7},{9,8},{10,9},{11,1... | collective-permute-start | bytes 122888 | tf_op jit(solution)/shard_map/ppermute | solution.py:23
  115.6 12.9 %collective-permute-start.13 = (f32[1,128,1024]{2,1,0:T(8,128)S(1)}, f32[1,128,1024]{2,1,0:T(8,128)S(1)}, u32[]{:S(2)}, u32[]{:S(2)}) collective-permute-start(f32[1,128,1024]{2,1,0:T(8,128)S(1)} %get-tuple-element.88), channel_id=1, source_target_pairs={{0,16},{16,32},{32,48},{48,64},{64,80},{80,96},{96,112},{112,128},... | collective-permute-start | bytes 1572872 | tf_op jit(solution)/shard_map/ppermute | solution.py:31
  118.0 16.8 %collective-permute-start.14 = (f32[1,128,1024]{2,1,0:T(8,128)S(1)}, f32[1,128,1024]{2,1,0:T(8,128)S(1)}, u32[]{:S(2)}, u32[]{:S(2)}) collective-permute-start(f32[1,128,1024]{2,1,0:T(8,128)S(1)} %get-tuple-element.89), channel_id=1, source_target_pairs={{0,32},{16,48},{32,64},{48,80},{64,96},{80,112},{96,128},{112,144}... | collective-permute-start | bytes 1572872 | tf_op jit(solution)/shard_map/ppermute | solution.py:31
  121.1 36.7 %collective-permute-start.15 = (f32[1,128,1024]{2,1,0:T(8,128)S(1)}, f32[1,128,1024]{2,1,0:T(8,128)S(1)}, u32[]{:S(2)}, u32[]{:S(2)}) collective-permute-start(f32[1,128,1024]{2,1,0:T(8,128)S(1)} %get-tuple-element.90), channel_id=1, source_target_pairs={{0,48},{16,64},{32,80},{48,96},{64,112},{80,128},{96,144},{112,160... | collective-permute-start | bytes 1572872 | tf_op jit(solution)/shard_map/ppermute | solution.py:31
  158.8 17.6 %copy-start = (f32[1,128,1024]{2,1,0:T(8,128)}, f32[1,128,1024]{2,1,0:T(8,128)S(1)}, u32[]{:S(2)}) copy-start(f32[1,128,1024]{2,1,0:T(8,128)S(1)} %get-tuple-element.51) | copy-start | bytes 1572868
  159.2 9.5 %collective-permute-start.16 = (f32[2,1,4,1024]{3,2,1,0:T(4,128)S(1)}, f32[2,1,4,1024]{3,2,1,0:T(4,128)S(1)}, u32[]{:S(2)}, u32[]{:S(2)}) collective-permute-start(f32[2,1,4,1024]{3,2,1,0:T(4,128)S(1)} %get-tuple-element.80), channel_id=1, source_target_pairs={{0,1},{1,2},{2,3},{3,4},{4,5},{5,6},{6,7},{7,8},{8,9},{9,10},{10,1... | collective-permute-start | bytes 98312 | tf_op jit(solution)/shard_map/ppermute | solution.py:20
  166.7 9.4 %collective-permute-start.17 = (f32[2,1,4,1024]{3,2,1,0:T(4,128)S(1)}, f32[2,1,4,1024]{3,2,1,0:T(4,128)S(1)}, u32[]{:S(2)}, u32[]{:S(2)}) collective-permute-start(f32[2,1,4,1024]{3,2,1,0:T(4,128)S(1)} %get-tuple-element.81), channel_id=1, source_target_pairs={{1,0},{2,1},{3,2},{4,3},{5,4},{6,5},{7,6},{8,7},{9,8},{10,9},{11,1... | collective-permute-start | bytes 98312 | tf_op jit(solution)/shard_map/ppermute | solution.py:23
where the time goes:
time: 181 us; the launch traced here: 180 us
  starting transfers between devices  64.3 us (36%)
  waiting for transfers between devices  54.9 us (30%)
  other arithmetic  51.2 us (28%)
  between operations  4.38 us (2%)
  local copies, waits for them, and re-layouts  3.21 us (2%)
  matrix products  2.35 us (1%)
    ppermute x6, waiting for transfers between devices, passed_along(): lax.ppermute(value, axis, [(source, source + steps) for source in range(i...  38.1 us
    ppermute x6, starting transfers between devices, padded_2(): lax.ppermute(lax.slice_in_dim(block, block.shape[dim] - width, None, axis...  28.8 us
    ppermute x6, starting transfers between devices, padded_2(): lax.ppermute(lax.slice_in_dim(block, 0, width, axis=dim), axis, backward)  18.6 us
    ppermute x6, starting transfers between devices, passed_along(): lax.ppermute(value, axis, [(source, source + steps) for source in range(i...  17 us
    add x3, other arithmetic, box_cols(): running = running + padded[..., step_col:step_col + col_count]  16.9 us
    ppermute x6, waiting for transfers between devices, padded_2(): lax.ppermute(lax.slice_in_dim(block, 0, width, axis=dim), axis, backward)  16.7 us
    unnamed x8, other arithmetic  13.7 us
    add x11, other arithmetic, box_rows(): running = running + field[..., step_row:step_row + out_rows, :]  10.8 us
  transfers between devices with their start and end apart: 18, of which 7 were waited for; matrix products, arithmetic and copies ran while one was open for 11% of the time, Pallas kernels for 0%

commit v1 on v0

v1 whole, which is shorter than its diff:
```python
import functools

import jax
import jax.numpy as jnp
from jax import lax
from jax.experimental import pallas as pl
from jax.experimental.pallas import tpu as pltpu
from jax.sharding import PartitionSpec as P

TAPS = 4
HALO = 12
STEPS = 19
SUBS = 8
EXT = STEPS * SUBS
TILES = 8
CELLS = 81.0
F32 = jnp.float32
BF16 = jnp.bfloat16
VMEM = pl.BlockSpec(memory_space=pltpu.VMEM)
SMEM = pl.BlockSpec(memory_space=pltpu.SMEM)
EDGE = 24
BLOCK = 32


def window_sums(seq, width):
    count = len(seq) - width + 1
    out = [None] * count
    for base in range(0, count, width):
        suffix = [None] * width
        suffix[width - 1] = seq[base + width - 1]
        for i in range(width - 2, -1, -1):
            suffix[i] = seq[base + i] + suffix[i + 1]
        prefix = None
        for i in range(width):
            if base + i >= count:
                break
            if i == 0:
                out[base] = suffix[0]
            else:
                nxt = seq[base + width + i - 1]
                prefix = nxt if prefix is None else prefix + nxt
                out[base + i] = suffix[i] + prefix
    return out


def row_window(steps):
    low = [pltpu.roll(v, 1, 0) for v in steps[-4:]]
    high = [pltpu.roll(v, SUBS - 1, 0) for v in steps[:4]]
    return window_sums(low + steps + high, 9)


def col_window(tiles, first_lane, last_lane):
    zero = jnp.zeros_like(tiles[0])
    low = [jnp.where(first_lane, zero, pltpu.roll(v, 1, 1)) for v in tiles[4:]]
    high = [jnp.where(last_lane, zero, pltpu.roll(v, 127, 1)) for v in tiles[:4]]
    seq = low + tiles + high
    suffix = [None] * 8
    suffix[7] = seq[7]
    for i in range(6, -1, -1):
        suffix[i] = seq[i] + suffix[i + 1]
    out = []
    prefix = None
    for i in range(8):
        prefix = seq[8 + i] if prefix is None else prefix + seq[8 + i]
        out.append(suffix[i] + prefix)
    return out


def steps_of(value):
    return [value[8 * k : 8 * k + 8] for k in range(STEPS)]


def lanes():
    lane = lax.broadcasted_iota(jnp.int32, (8, 128), 1)
    return lane == 0, lane == 127


def put_rows(ref, tile, values):
    for k, v in enumerate(values):
        ref[tile, 8 * k : 8 * k + 8, :] = v


def get_tiles(ref, at):
    return [ref[m, pl.ds(at, 8), :] for m in range(TILES)]


def split3(value):
    hi = value.astype(BF16).astype(F32)
    rest = value - hi
    mid = rest.astype(BF16).astype(F32)
    return hi, mid, rest - mid


def prep_kernel(shift_ref, img_ref, weights_ref, up_ref, down_ref, own_ref):
    up_ref[0:EDGE, :] = img_ref[128 - EDGE : 128, :]
    down_ref[0:EDGE, :] = img_ref[0:EDGE, :]
    shift = jnp.full((1, 128), shift_ref[0, 0], jnp.int32).astype(F32)
    lane = lax.broadcasted_iota(jnp.int32, (8, 128), 1)
    row = lax.broadcasted_iota(jnp.int32, (8, 128), 0)
    zero = jnp.zeros((8, 128), F32)
    for tap in range(TAPS):
        line = jnp.broadcast_to(weights_ref[tap : tap + 1, :], (8, 128))
        hi, mid, lo = split3(pltpu.roll(line, HALO, 1))
        full = jnp.where(row == 0, hi, jnp.where(row == 1, mid, jnp.where(row == 2, lo, zero)))
        if tap == 0:
            full = jnp.where(row == 3, jnp.broadcast_to(shift, (8, 128)), full)
        at = 256 * tap
        wrapped = jnp.where(lane < HALO, full, zero).astype(BF16)
        own_ref[:, at : at + 128] = jnp.where(lane >= HALO, full, zero).astype(BF16)
        own_ref[:, at + 128 : at + 256] = wrapped
        up_ref[EDGE:BLOCK, at : at + 128] = wrapped
        up_ref[EDGE:BLOCK, at + 128 : at + 256] = zero.astype(BF16)
        down_ref[EDGE:BLOCK, at : at + 128] = zero.astype(BF16)
        down_ref[EDGE:BLOCK, at + 128 : at + 256] = jnp.where(
            (lane >= HALO) & (lane < 2 * HALO), full, zero
        ).astype(BF16)


def matrix_kernel(shift_ref, weights_ref, out_ref):
    shift = shift_ref[0]
    base = lax.broadcasted_iota(jnp.int32, (16, 128), 0) - 8 * lax.broadcasted_iota(
        jnp.int32, (16, 128), 1
    )
    for m in range(TILES):
        taps = [
            jnp.broadcast_to(weights_ref[t : t + 1, 128 * m : 128 * m + 128].astype(F32), (16, 128))
            for t in range(TAPS)
        ]

        def body(step, carry):
            offset = base - (m + shift - 1 - 16 * step)
            value = jnp.zeros((16, 128), F32)
            for t in range(TAPS):
                value = jnp.where(offset == t, taps[t], value)
            out_ref[pl.ds(pl.multiple_of(16 * step, 16), 16), 128 * m : 128 * m + 128] = value.astype(BF16)
            return carry

        lax.fori_loop(0, 64, body, 0, unroll=8)


def warp_kernel(img_ref, low_ref, high_ref, own_ref, matrix_ref, out_ref):
    meta = (
        low_ref[EDGE:BLOCK, :].astype(F32)
        + own_ref[...].astype(F32)
        + high_ref[EDGE:BLOCK, :].astype(F32)
    ).astype(BF16)
    place = lax.broadcasted_iota(jnp.int32, (EXT, 256), 0)
    rho = (place % 8) * STEPS + place // 8
    spread = jnp.where(
        rho == lax.broadcasted_iota(jnp.int32, (EXT, 256), 1), jnp.float32(1), jnp.float32(0)
    ).astype(BF16)
    columns = [
        lax.dot_general(
            spread,
            meta[:, 256 * tap : 256 * tap + 256],
            (((1,), (1,)), ((), ())),
            preferred_element_type=F32,
        )
        for tap in range(TAPS)
    ]
    width = 2 * BLOCK + 128
    lane = lax.broadcasted_iota(jnp.int32, (EXT, width), 1)
    image_row = jnp.where(lane < EDGE, lane - EDGE, jnp.where(lane < BLOCK, -1000, lane - BLOCK))
    image_row = jnp.where(lane < BLOCK + 128 + EDGE, image_row, 2000)
    own_row = lax.broadcasted_iota(jnp.int32, (EXT, width), 0)
    own_row = (own_row % 8) * STEPS + own_row // 8 - HALO
    offset = (image_row - own_row + 1).astype(F32) - columns[0][:, 3:4]
    value = jnp.zeros((EXT, width), F32)
    for tap in range(TAPS):
        weight = columns[tap][:, 0:1] + columns[tap][:, 1:2] + columns[tap][:, 2:3]
        value = jnp.where(offset == float(tap), weight, value)
    hi, mid, lo = split3(value)
    source = jnp.concatenate([low_ref[...], img_ref[...], high_ref[...]], axis=0)
    total = jnp.zeros((EXT, 1024), F32)
    for piece in (lo, mid, hi):
        total = total + jnp.dot(piece.astype(BF16), source, preferred_element_type=F32)
    row_warped = total.astype(BF16)
    for pair in range(TILES // 2):
        cols = jnp.dot(
            row_warped, matrix_ref[:, 256 * pair : 256 * pair + 256], preferred_element_type=F32
        ).astype(BF16)
        out_ref[2 * pair] = cols[:, :128]
        out_ref[2 * pair + 1] = cols[:, 128:]


def row_bounds(strip):
    first = jnp.where(strip == 0, HALO, 0)
    last = jnp.where(strip == 15, HALO + 128, EXT)
    return first, last


def own_stats(x_ref, x_wide, sum_x, root_x, box_a, box_b):
    def rows(m, carry):
        value = x_ref[m].astype(F32)
        x_wide[m] = value
        put_rows(box_a, m, row_window(steps_of(value)))
        put_rows(box_b, m, row_window(steps_of(value * value)))
        return carry

    lax.fori_loop(0, TILES, rows, 0)
    edges = lanes()

    def cols(k, carry):
        at = pl.multiple_of(8 * k, 8)
        s1 = col_window(get_tiles(box_a, at), *edges)
        s2 = col_window(get_tiles(box_b, at), *edges)
        for m in range(TILES):
            sum_x[m, pl.ds(at, 8), :] = s1[m]
            root_x[m, pl.ds(at, 8), :] = lax.rsqrt(
                s2[m] - s1[m] * s1[m] * (1.0 / CELLS) + 0.25 * CELLS
            )
        return carry

    lax.fori_loop(0, STEPS, cols, 0)


def add_pair(y_ref, weight, bounds, first, x_wide, sum_x, root_x, sum_g, sum_h, sum_t, y_wide, coef, box_a, box_b, box_c):
    def rows(m, carry):
        value = y_ref[m].astype(F32)
        y_wide[m] = value
        put_rows(box_a, m, row_window(steps_of(value)))
        put_rows(box_b, m, row_window(steps_of(value * value)))
        put_rows(box_c, m, row_window(steps_of(value * x_wide[m])))
        return carry

    lax.fori_loop(0, TILES, rows, 0)
    edges = lanes()

    def cols(k, carry):
        at = pl.multiple_of(8 * k, 8)
        rho = lax.broadcasted_iota(jnp.int32, (8, 128), 0) * STEPS + k
        scale = jnp.where((rho >= bounds[0]) & (rho < bounds[1]), weight, jnp.float32(0))
        s1 = col_window(get_tiles(box_a, at), *edges)
        s2 = col_window(get_tiles(box_b, at), *edges)
        s3 = col_window(get_tiles(box_c, at), *edges)
        for m in range(TILES):
            here = (m, pl.ds(at, 8), slice(None))
            mean = s1[m] * (1.0 / CELLS)
            root = lax.rsqrt(s2[m] - s1[m] * mean + 0.25 * CELLS)
            cov = s3[m] - sum_x[here] * mean
            u = scale * root_x[here] * root
            coef[here] = u
            g, h = u * cov, u * s1[m]
            sum_g[here] = g if first else sum_g[here] + g
            sum_h[here] = h if first else sum_h[here] + h
        return carry

    lax.fori_loop(0, STEPS, cols, 0)

    def rows_2(m, carry):
        put_rows(box_a, m, row_window(steps_of(coef[m])))
        return carry

    lax.fori_loop(0, TILES, rows_2, 0)

    def cols_2(k, carry):
        at = pl.multiple_of(8 * k, 8)
        s1 = col_window(get_tiles(box_a, at), *edges)
        for m in range(TILES):
            here = (m, pl.ds(at, 8), slice(None))
            t = y_wide[here] * s1[m]
            sum_t[here] = t if first else sum_t[here] + t
        return carry

    lax.fori_loop(0, STEPS, cols_2, 0)


def finish(bounds, x_wide, sum_x, root_x, sum_g, sum_h, sum_t, natural, grad_ref, disp_ref, box_a, box_b, field_a, field_b):
    edges = lanes()

    def rows(m, carry):
        root = root_x[m]
        g = root * root * sum_g[m]
        put_rows(box_a, m, row_window(steps_of(sum_h[m] - g * sum_x[m])))
        put_rows(box_b, m, row_window(steps_of(g)))
        return carry

    lax.fori_loop(0, TILES, rows, 0)

    def cols(k, carry):
        at = pl.multiple_of(8 * k, 8)
        s1 = col_window(get_tiles(box_a, at), *edges)
        s2 = col_window(get_tiles(box_b, at), *edges)
        for m in range(TILES):
            here = (m, pl.ds(at, 8), slice(None))
            grad = s1[m] * (1.0 / CELLS) + x_wide[here] * s2[m] - sum_t[here]
            sum_t[here] = grad
            natural[0, pl.ds(m * EXT + k, 8, stride=STEPS), :] = grad
        return carry

    lax.fori_loop(0, STEPS, cols, 0)
    sub = lax.broadcasted_iota(jnp.int32, (8, 128), 0) * STEPS
    for m in range(TILES):
        x = steps_of(x_wide[m])
        seq = [pltpu.roll(x[-1], 1, 0)] + x + [pltpu.roll(x[0], SUBS - 1, 0)]
        out = []
        before = x_wide[m - 1] if m else None
        after = x_wide[m + 1] if m < TILES - 1 else None
        prods = []
        for k in range(STEPS):
            rho = sub + k
            inside = (rho >= bounds[0]) & (rho < bounds[1])
            grad = jnp.where(inside, sum_t[m, 8 * k : 8 * k + 8, :] * (-0.5 / 9.0), 0.0)
            out.append(grad * (seq[k + 2] - seq[k]))
            if m:
                left = before[8 * k : 8 * k + 8]
            else:
                left = jnp.where(edges[0], 0.0, pltpu.roll(x_wide[TILES - 1, 8 * k : 8 * k + 8, :], 1, 1))
            if m < TILES - 1:
                right = after[8 * k : 8 * k + 8]
            else:
                right = jnp.where(edges[1], 0.0, pltpu.roll(x_wide[0, 8 * k : 8 * k + 8, :], 127, 1))
            prods.append(grad * (right - left))
        put_rows(box_a, m, row_window(out))
        put_rows(box_b, m, row_window(prods))

    def cols_2(k, carry):
        at = pl.multiple_of(8 * k, 8)
        s1 = col_window(get_tiles(box_a, at), *edges)
        s2 = col_window(get_tiles(box_b, at), *edges)
        for m in range(TILES):
            natural[1, pl.ds(m * EXT + k, 8, stride=STEPS), :] = s1[m]
            natural[2, pl.ds(m * EXT + k, 8, stride=STEPS), :] = s2[m]
        return carry

    lax.fori_loop(0, STEPS, cols_2, 0)
    lane = lax.broadcasted_iota(jnp.int32, (8, 128), 1)
    pick = (lane % 8) * 16 + lane // 8

    def restore(block, carry):
        for field in range(3):
            v = [natural[field, pl.ds(m * EXT + HALO + 8 * block, 8), :] for m in range(TILES)]
            for bit in range(3):
                span = 16 << bit
                upper = (lane & span) != 0
                new = list(v)
                for m in range(TILES):
                    if m & (1 << bit):
                        continue
                    a, b = v[m], v[m | (1 << bit)]
                    new[m] = jnp.where(upper, pltpu.roll(b, span, 1), a)
                    new[m | (1 << bit)] = jnp.where(upper, b, pltpu.roll(a, 128 - span, 1))
                v = new
            for j in range(TILES):
                tile = jnp.take_along_axis(v[j], pick, axis=1)
                at = pl.ds(pl.multiple_of(8 * block, 8), 8)
                if field == 0:
                    grad_ref[at, 128 * j : 128 * j + 128] = tile
                else:
                    disp_ref[field - 1, at, 128 * j : 128 * j + 128] = tile
        return carry

    lax.fori_loop(0, 16, restore, 0)


def pair_weight(pair_on, own, other):
    low = jnp.minimum(own, other)
    gap = jnp.abs(own - other)
    inside = (other >= 0) & (other < 16)
    on = pair_on[jnp.clip(low, 0, 15), jnp.clip(gap - 1, 0, 2)]
    return jnp.where(inside, on, 0).astype(F32)


def others(own):
    partner = own + 1 - 2 * (own % 2)
    return {
        "a": partner,
        "b": own - 2,
        "c": own + 2,
        "d": jnp.where(own % 2 == 0, own - 3, own + 3),
        "e": partner - 2,
        "f": partner + 2,
    }


def field():
    return pltpu.VMEM((TILES, EXT, 128), F32)


def main_kernel(
    place, pair_on, x, ya, yb, yc, yd, ye, yf, grad, disp, x_wide, y_wide, sum_x, root_x, g, h, t, coef, box_a, box_b, box_c, natural
):
    own, strip = place[0], place[1]
    bounds = row_bounds(strip)
    own_stats(x, x_wide, sum_x, root_x, box_a, box_b)
    names = others(own)
    for i, (name, y) in enumerate(zip("abcdef", (ya, yb, yc, yd, ye, yf))):
        weight = pair_weight(pair_on, own, names[name])
        add_pair(y, weight, bounds, i == 0, x_wide, sum_x, root_x, g, h, t, y_wide, coef, box_a, box_b, box_c)
    finish(bounds, x_wide, sum_x, root_x, g, h, t, natural, grad, disp, box_a, box_b, box_c, coef)


def shape(dims, kind):
    return jax.ShapeDtypeStruct(dims, kind)


def exchange(value, axis, pairs):
    return lax.ppermute(value, axis, pairs)


def per_device(images, row_weights, row_shift, col_weights, col_shift, pair_on):
    place = jnp.stack([lax.axis_index("sec"), lax.axis_index("strip")]).astype(jnp.int32)
    image = images[0]
    big = pltpu.CompilerParams(vmem_limit_bytes=50 * 1024 * 1024)
    up, down, own = pl.pallas_call(
        prep_kernel,
        out_shape=(shape((BLOCK, 1024), BF16), shape((BLOCK, 1024), BF16), shape((8, 1024), BF16)),
        in_specs=[SMEM, VMEM, VMEM],
        out_specs=(VMEM, VMEM, VMEM),
        name="prep",
    )(row_shift, image, row_weights[0])
    low = exchange(up, "strip", [(i, i + 1) for i in range(15)])
    high = exchange(down, "strip", [(i + 1, i) for i in range(15)])
    taps = col_weights[0].reshape(TAPS, 128, 8).transpose(0, 2, 1).reshape(TAPS, 1024)
    matrix = pl.pallas_call(
        matrix_kernel,
        out_shape=shape((1024, 1024), BF16),
        in_specs=[SMEM, VMEM],
        out_specs=VMEM,
        name="matrix",
        cost_estimate=pl.CostEstimate(flops=2_000_000, bytes_accessed=2_000_000, transcendentals=0),
    )(col_shift, taps)
    warped = pl.pallas_call(
        warp_kernel,
        out_shape=shape((TILES, EXT, 128), BF16),
        in_specs=[VMEM] * 5,
        out_specs=VMEM,
        compiler_params=big,
        name="warp",
    )(image, low, high, own, matrix)
    sections = range(16)
    from_b = exchange(warped, "sec", [(s, s + 2) for s in sections if s + 2 < 16])
    from_c = exchange(warped, "sec", [(s, s - 2) for s in sections if s >= 2])
    odd = [(s, s + 3) if s % 2 else (s, s - 3) for s in sections]
    from_d = exchange(warped, "sec", [p for p in odd if 0 <= p[1] < 16])
    partner = [(s, s ^ 1) for s in sections]
    from_a = exchange(warped, "sec", partner)
    from_e = exchange(from_b, "sec", partner)
    from_f = exchange(from_c, "sec", partner)
    grad, disp = pl.pallas_call(
        main_kernel,
        out_shape=(shape((128, 1024), F32), shape((2, 128, 1024), F32)),
        in_specs=[SMEM, SMEM] + [VMEM] * 7,
        out_specs=(VMEM, VMEM),
        scratch_shapes=[field() for _ in range(11)] + [pltpu.VMEM((3, TILES * EXT, 128), F32)],
        compiler_params=big,
        name="pairs",
    )(place, pair_on, warped, from_a, from_b, from_c, from_d, from_e, from_f)
    return grad[None], disp[:, None]


def solution(mesh):
    return jax.shard_map(
        per_device,
        mesh=mesh,
        in_specs=(
            P("sec", "strip", None),
            P("sec", None, "strip"),
            P("sec", "strip"),
            P("sec", None, None),
            P("sec"),
            P(),
        ),
        out_specs=(P("sec", "strip", None), P(None, "sec", "strip", None)),
        check_vma=False,
    )
```

time: 181 us -> 81.8 us (0.45)
  the two profiles are of different devices: /device:TPU:110 before, /device:TPU:131 now
where the time goes in v1:
time: 81.8 us; the launch traced here: 81.4 us
  Pallas kernels  42.8 us (52%)
  starting transfers between devices  26.3 us (32%)
  waiting for transfers between devices  6.89 us (8%)
  local copies, waits for them, and re-layouts  3.26 us (4%)
  between operations  2.08 us (3%)
    pallas_call x1, Pallas kernels, per_device(): pl.pallas_call(main_kernel, out_shape=(shape((128, 1024), F32), shape((2,...  36.1 us
    ppermute x8, starting transfers between devices, exchange(): return lax.ppermute(value, axis, pairs)  26.3 us
    ppermute x8, waiting for transfers between devices, exchange(): return lax.ppermute(value, axis, pairs)  6.89 us
    pallas_call x1, Pallas kernels, per_device(): pl.pallas_call(matrix_kernel, out_shape=shape((1024, 1024), BF16), in_spe...  3.75 us
    unnamed x10, local copies, waits for them, and re-layouts  2.29 us
    pallas_call x1, Pallas kernels, per_device(): pl.pallas_call(prep_kernel, out_shape=(shape((BLOCK, 1024), BF16), shape(...  1.69 us
  transfers between devices with their start and end apart: 8, of which 2 were waited for; matrix products, arithmetic and copies ran while one was open for 2% of the time, Pallas kernels for 5%

profile of v1, /device:TPU:131, one launch (start us, length us, event | category | flops | bytes accessed | tf_op | source)
XLA Modules:
  0.0 81.4 jit_solution(7729841498195813193)
XLA Ops:
  0.6 0.0 copy-start.1
  1.3 1.7 %prep.1 = (bf16[32,1024]{1,0:T(8,128)(2,1)}, bf16[32,1024]{1,0:T(8,128)(2,1)}, bf16[8,1024]{1,0:T(8,128)(2,1)}) custom-call(s32[1,1]{1,0:T(1,128)S(6)} %copy.17.shift_ref, bf16[128,1024]{1,0:T(8,128)(2,1)} %bitcast.13, f32[4,128]{1,0:T(4,128)} %bitcast.18), custom_call_target="tpu_custom_call" | custom-call | tf_op jit(solution)/shard_map/prep/pallas_call | solution.py:405
  3.0 0.0 copy-start.2
  3.0 3.9 %collective-permute-start = (bf16[32,1024]{1,0:T(8,128)(2,1)}, bf16[32,1024]{1,0:T(8,128)(2,1)S(1)}, u32[]{:S(2)}, u32[]{:S(2)}) collective-permute-start(bf16[32,1024]{1,0:T(8,128)(2,1)} %get-tuple-element.7), channel_id=1, source_target_pairs={{0,1},{1,2},{2,3},{3,4},{4,5},{5,6},{6,7},{7,8},{8,9},{9,10},{10,1... | collective-permute-start | bytes 196616 | tf_op jit(solution)/shard_map/ppermute | solution.py:398
  6.9 5.1 %collective-permute-start.1 = (bf16[32,1024]{1,0:T(8,128)(2,1)}, bf16[32,1024]{1,0:T(8,128)(2,1)S(1)}, u32[]{:S(2)}, u32[]{:S(2)}) collective-permute-start(bf16[32,1024]{1,0:T(8,128)(2,1)} %get-tuple-element.8), channel_id=1, source_target_pairs={{1,0},{2,1},{3,2},{4,3},{5,4},{6,5},{7,6},{8,7},{9,8},{10,9},{11,1... | collective-permute-start | bytes 196616 | tf_op jit(solution)/shard_map/ppermute | solution.py:398
  12.7 0.9 %reshape_squeeze.3 = bf16[4,128,8]{2,1,0:T(8,128)(2,1)S(1)} reshape(bf16[1,4,1024]{2,1,0:T(4,128)(2,1)} %param.9) | data formatting | bytes 16384 | tf_op jit(solution)/shard_map/reshape;squeeze | solution.py:414
  13.6 0.1 copy.11
  13.7 0.6 copy.16
  14.3 0.0 copy-start.3
  14.3 3.8 %matrix.1.matrix_ref = bf16[1024,1024]{1,0:T(8,128)(2,1)} custom-call(s32[1]{0:T(128)S(6)} %copy.18.shift_ref, bf16[4,1024]{1,0:T(4,128)(2,1)} %bitcast.16), custom_call_target="tpu_custom_call" | custom-call | flops 2000000 | bytes 2000000 | tf_op jit(solution)/shard_map/matrix/pallas_call | solution.py:415
  18.0 0.0 collective-permute-done.low_ref
  18.0 0.0 collective-permute-done.1.high_ref
  18.0 0.0 copy-done.1
  18.1 0.0 copy-done.2
  18.1 0.0 copy-start
  18.1 1.6 %copy-done = bf16[1024,1024]{1,0:T(8,128)(2,1)S(1)} copy-done((bf16[1024,1024]{1,0:T(8,128)(2,1)S(1)}, bf16[1024,1024]{1,0:T(8,128)(2,1)}, u32[]{:S(2)}) %copy-start) | copy-done | bytes 2097176
  19.7 1.3 %warp.1.x = bf16[8,152,128]{2,1,0:T(8,128)(2,1)S(1)} custom-call(bf16[128,1024]{1,0:T(8,128)(2,1)S(1)} %bitcast.14, bf16[32,1024]{1,0:T(8,128)(2,1)S(1)} %collective-permute-done.low_ref, bf16[32,1024]{1,0:T(8,128)(2,1)S(1)} %collective-permute-done.1.high_ref, bf16[8,1024]{1,0:T(8,128)(2,1)S(1)} %copy-done.2, bf16[1024,1024]{1,0:T(8,128)(2,1)S(1)} %copy-done), custom_call_target="tpu_custom_call" | custom-call | tf_op jit(solution)/shard_map/warp/pallas_call | solution.py:423
  20.9 4.6 %collective-permute-start.4 = (bf16[8,152,128]{2,1,0:T(8,128)(2,1)S(1)}, bf16[8,152,128]{2,1,0:T(8,128)(2,1)S(1)}, u32[]{:S(2)}, u32[]{:S(2)}) collective-permute-start(bf16[8,152,128]{2,1,0:T(8,128)(2,1)S(1)} %warp.1.x), channel_id=1, source_target_pairs={{32,0},{48,16},{64,32},{80,48},{96,64},{112,80},{128,96},{144,112}... | collective-permute-start | bytes 933896 | tf_op jit(solution)/shard_map/ppermute | solution.py:398
  25.6 1.9 %collective-permute-start.3 = (bf16[8,152,128]{2,1,0:T(8,128)(2,1)S(1)}, bf16[8,152,128]{2,1,0:T(8,128)(2,1)S(1)}, u32[]{:S(2)}, u32[]{:S(2)}) collective-permute-start(bf16[8,152,128]{2,1,0:T(8,128)(2,1)S(1)} %warp.1.x), channel_id=1, source_target_pairs={{0,32},{16,48},{32,64},{48,80},{64,96},{80,112},{96,128},{112,144}... | collective-permute-start | bytes 933896 | tf_op jit(solution)/shard_map/ppermute | solution.py:398
  27.5 5.3 %collective-permute-start.5 = (bf16[8,152,128]{2,1,0:T(8,128)(2,1)S(1)}, bf16[8,152,128]{2,1,0:T(8,128)(2,1)S(1)}, u32[]{:S(2)}, u32[]{:S(2)}) collective-permute-start(bf16[8,152,128]{2,1,0:T(8,128)(2,1)S(1)} %warp.1.x), channel_id=1, source_target_pairs={{16,64},{48,96},{64,16},{80,128},{96,48},{112,160},{128,80},{144,1... | collective-permute-start | bytes 933896 | tf_op jit(solution)/shard_map/ppermute | solution.py:398
  32.8 0.1 collective-permute-start.2
  32.9 0.0 collective-permute-done.4.yc
  32.9 0.5 collective-permute-start.7
  33.4 4.4 %collective-permute-done.3.yb = bf16[8,152,128]{2,1,0:T(8,128)(2,1)S(1)} collective-permute-done((bf16[8,152,128]{2,1,0:T(8,128)(2,1)S(1)}, bf16[8,152,128]{2,1,0:T(8,128)(2,1)S(1)}, u32[]{:S(2)}, u32[]{:S(2)}) %collective-permute-start.3) | collective-permute-done | bytes 311328 | tf_op jit(solution)/shard_map/ppermute | solution.py:398
  37.7 4.9 %collective-permute-start.6 = (bf16[8,152,128]{2,1,0:T(8,128)(2,1)S(1)}, bf16[8,152,128]{2,1,0:T(8,128)(2,1)S(1)}, u32[]{:S(2)}, u32[]{:S(2)}) collective-permute-start(bf16[8,152,128]{2,1,0:T(8,128)(2,1)S(1)} %collective-permute-done.3.yb), channel_id=1, source_target_pairs={{0,16},{16,0},{32,48},{48,32},{64,80},{80,64},{96,112},{112,96},{1... | collective-permute-start | bytes 933896 | tf_op jit(solution)/shard_map/ppermute | solution.py:398
  42.7 0.0 copy-done.3
  42.7 0.1 copy.12.pair_on
  42.8 0.1 pad_add_fusion.place
  42.8 2.5 %collective-permute-done.5.yd = bf16[8,152,128]{2,1,0:T(8,128)(2,1)S(1)} collective-permute-done((bf16[8,152,128]{2,1,0:T(8,128)(2,1)S(1)}, bf16[8,152,128]{2,1,0:T(8,128)(2,1)S(1)}, u32[]{:S(2)}, u32[]{:S(2)}) %collective-permute-start.5) | collective-permute-done | bytes 311328 | tf_op jit(solution)/shard_map/ppermute | solution.py:398
  45.3 0.0 collective-permute-done.2.ya
  45.3 0.0 collective-permute-done.7.yf
  45.3 0.0 collective-permute-done.6.ye
  45.3 36.1 %pairs.1 = (f32[128,1024]{1,0:T(8,128)}, f32[2,128,1024]{2,1,0:T(8,128)}) custom-call(s32[2]{0:T(128)S(1)} %pad_add_fusion.place, s32[16,3]{1,0:T(8,128)S(1)} %copy.12.pair_on, bf16[8,152,128]{2,1,0:T(8,128)(2,1)S(1)} %warp.1.x, bf16[8,152,128]{2,1,0:T(8,128)(2,1)S(1)} %collective-permute-done.2.ya, bf16[8,152,128]{2,1,0:T(8,128)(2,1)S(1)} %collective-permute-done.3.yb, ...), custom_call_target="tpu_custom_call" | custom-call | tf_op jit(solution)/shard_map/pairs/pallas_call | solution.py:440
Async XLA Ops:
  0.6 17.4 %copy-start.1 = (bf16[1,128,1024]{2,1,0:T(8,128)(2,1)S(1)}, bf16[1,128,1024]{2,1,0:T(8,128)(2,1)}, u32[]{:S(2)}) copy-start(bf16[1,128,1024]{2,1,0:T(8,128)(2,1)} %param.6) | copy-start | bytes 786436
  3.0 15.0 %copy-start.2 = (bf16[8,1024]{1,0:T(8,128)(2,1)S(1)}, bf16[8,1024]{1,0:T(8,128)(2,1)}, u32[]{:S(2)}) copy-start(bf16[8,1024]{1,0:T(8,128)(2,1)} %get-tuple-element.9.own_ref) | copy-start | bytes 49156
  3.0 15.0 %collective-permute-start = (bf16[32,1024]{1,0:T(8,128)(2,1)}, bf16[32,1024]{1,0:T(8,128)(2,1)S(1)}, u32[]{:S(2)}, u32[]{:S(2)}) collective-permute-start(bf16[32,1024]{1,0:T(8,128)(2,1)} %get-tuple-element.7), channel_id=1, source_target_pairs={{0,1},{1,2},{2,3},{3,4},{4,5},{5,6},{6,7},{7,8},{8,9},{9,10},{10,1... | collective-permute-start | bytes 196616 | tf_op jit(solution)/shard_map/ppermute | solution.py:398
  6.9 11.1 %collective-permute-start.1 = (bf16[32,1024]{1,0:T(8,128)(2,1)}, bf16[32,1024]{1,0:T(8,128)(2,1)S(1)}, u32[]{:S(2)}, u32[]{:S(2)}) collective-permute-start(bf16[32,1024]{1,0:T(8,128)(2,1)} %get-tuple-element.8), channel_id=1, source_target_pairs={{1,0},{2,1},{3,2},{4,3},{5,4},{6,5},{7,6},{8,7},{9,8},{10,9},{11,1... | collective-permute-start | bytes 196616 | tf_op jit(solution)/shard_map/ppermute | solution.py:398
  14.3 28.4 %copy-start.3 = (s32[16,3]{0,1:T(4,128)S(1)}, s32[16,3]{0,1:T(4,128)}, u32[]{:S(2)}) copy-start(s32[16,3]{0,1:T(4,128)} %param.11) | copy-start | bytes 580
  18.1 1.6 %copy-start = (bf16[1024,1024]{1,0:T(8,128)(2,1)S(1)}, bf16[1024,1024]{1,0:T(8,128)(2,1)}, u32[]{:S(2)}) copy-start(bf16[1024,1024]{1,0:T(8,128)(2,1)} %matrix.1.matrix_ref) | copy-start | bytes 6291460
  20.9 11.9 %collective-permute-start.4 = (bf16[8,152,128]{2,1,0:T(8,128)(2,1)S(1)}, bf16[8,152,128]{2,1,0:T(8,128)(2,1)S(1)}, u32[]{:S(2)}, u32[]{:S(2)}) collective-permute-start(bf16[8,152,128]{2,1,0:T(8,128)(2,1)S(1)} %warp.1.x), channel_id=1, source_target_pairs={{32,0},{48,16},{64,32},{80,48},{96,64},{112,80},{128,96},{144,112}... | collective-permute-start | bytes 933896 | tf_op jit(solution)/shard_map/ppermute | solution.py:398
  25.6 12.2 %collective-permute-start.3 = (bf16[8,152,128]{2,1,0:T(8,128)(2,1)S(1)}, bf16[8,152,128]{2,1,0:T(8,128)(2,1)S(1)}, u32[]{:S(2)}, u32[]{:S(2)}) collective-permute-start(bf16[8,152,128]{2,1,0:T(8,128)(2,1)S(1)} %warp.1.x), channel_id=1, source_target_pairs={{0,32},{16,48},{32,64},{48,80},{64,96},{80,112},{96,128},{112,144}... | collective-permute-start | bytes 933896 | tf_op jit(solution)/shard_map/ppermute | solution.py:398
  27.5 17.8 %collective-permute-start.5 = (bf16[8,152,128]{2,1,0:T(8,128)(2,1)S(1)}, bf16[8,152,128]{2,1,0:T(8,128)(2,1)S(1)}, u32[]{:S(2)}, u32[]{:S(2)}) collective-permute-start(bf16[8,152,128]{2,1,0:T(8,128)(2,1)S(1)} %warp.1.x), channel_id=1, source_target_pairs={{16,64},{48,96},{64,16},{80,128},{96,48},{112,160},{128,80},{144,1... | collective-permute-start | bytes 933896 | tf_op jit(solution)/shard_map/ppermute | solution.py:398
  32.8 12.6 %collective-permute-start.2 = (bf16[8,152,128]{2,1,0:T(8,128)(2,1)S(1)}, bf16[8,152,128]{2,1,0:T(8,128)(2,1)S(1)}, u32[]{:S(2)}, u32[]{:S(2)}) collective-permute-start(bf16[8,152,128]{2,1,0:T(8,128)(2,1)S(1)} %warp.1.x), channel_id=1, source_target_pairs={{0,16},{16,0},{32,48},{48,32},{64,80},{80,64},{96,112},{112,96},{1... | collective-permute-start | bytes 933896 | tf_op jit(solution)/shard_map/ppermute | solution.py:398
  32.9 12.5 %collective-permute-start.7 = (bf16[8,152,128]{2,1,0:T(8,128)(2,1)S(1)}, bf16[8,152,128]{2,1,0:T(8,128)(2,1)S(1)}, u32[]{:S(2)}, u32[]{:S(2)}) collective-permute-start(bf16[8,152,128]{2,1,0:T(8,128)(2,1)S(1)} %collective-permute-done.4.yc), channel_id=1, source_target_pairs={{0,16},{16,0},{32,48},{48,32},{64,80},{80,64},{96,112},{112,96},{1... | collective-permute-start | bytes 933896 | tf_op jit(solution)/shard_map/ppermute | solution.py:398
  37.7 7.6 %collective-permute-start.6 = (bf16[8,152,128]{2,1,0:T(8,128)(2,1)S(1)}, bf16[8,152,128]{2,1,0:T(8,128)(2,1)S(1)}, u32[]{:S(2)}, u32[]{:S(2)}) collective-permute-start(bf16[8,152,128]{2,1,0:T(8,128)(2,1)S(1)} %collective-permute-done.3.yb), channel_id=1, source_target_pairs={{0,16},{16,0},{32,48},{48,32},{64,80},{80,64},{96,112},{112,96},{1... | collective-permute-start | bytes 933896 | tf_op jit(solution)/shard_map/ppermute | solution.py:398

commit v2 on v1

v2 whole, which is shorter than its diff:
```python
import functools

import jax
import jax.numpy as jnp
from jax import lax
from jax.experimental import pallas as pl
from jax.experimental.pallas import tpu as pltpu
from jax.sharding import PartitionSpec as P

TAPS = 4
HALO = 12
STEPS = 19
SUBS = 8
EXT = STEPS * SUBS
TILES = 8
CELLS = 81.0
F32 = jnp.float32
BF16 = jnp.bfloat16
VMEM = pl.BlockSpec(memory_space=pltpu.VMEM)
SMEM = pl.BlockSpec(memory_space=pltpu.SMEM)
EDGE = 24
BLOCK = 32


def window_sums(seq, width):
    count = len(seq) - width + 1
    out = [None] * count
    for base in range(0, count, width):
        suffix = [None] * width
        suffix[width - 1] = seq[base + width - 1]
        for i in range(width - 2, -1, -1):
            suffix[i] = seq[base + i] + suffix[i + 1]
        prefix = None
        for i in range(width):
            if base + i >= count:
                break
            if i == 0:
                out[base] = suffix[0]
            else:
                nxt = seq[base + width + i - 1]
                prefix = nxt if prefix is None else prefix + nxt
                out[base + i] = suffix[i] + prefix
    return out


def row_window(steps):
    low = [pltpu.roll(v, 1, 0) for v in steps[-4:]]
    high = [pltpu.roll(v, SUBS - 1, 0) for v in steps[:4]]
    return window_sums(low + steps + high, 9)


def col_window(seq):
    suffix = [None] * 8
    suffix[7] = seq[7]
    for i in range(6, -1, -1):
        suffix[i] = seq[i] + suffix[i + 1]
    out = []
    prefix = None
    for i in range(8):
        prefix = seq[8 + i] if prefix is None else prefix + seq[8 + i]
        out.append(suffix[i] + prefix)
    return out


def steps_of(value):
    return [value[8 * k : 8 * k + 8] for k in range(STEPS)]


def put_rows(ref, tile, values):
    for k, v in enumerate(values):
        ref[tile, 8 * k : 8 * k + 8, :] = v


def over_tiles(body, each=4):
    lane = lax.broadcasted_iota(jnp.int32, (8, 128), 1)

    def half(h, carry):
        shift = jnp.where(h == 0, 127, 1)
        keep = lane != jnp.where(h == 0, 127, 0)

        def turn(v):
            return jnp.where(keep, pltpu.roll(v, shift, 1), 0.0)

        for i in range(4):
            body(4 * h + i, turn)
        return carry

    lax.fori_loop(0, 2, half, 0)


def put_box(pair, m, turn, values):
    main, side = pair
    sums = row_window(values)
    put_rows(side, m, [turn(v) for v in sums])
    put_rows(main, m, sums)


def get_box(pair, at):
    main, side = pair
    rows = pl.ds(at, 8)
    seq = [side[m, rows, :] for m in range(4, 8)]
    seq += [main[m, rows, :] for m in range(8)]
    seq += [side[m, rows, :] for m in range(4)]
    return col_window(seq)


def over_steps(body):
    def step(k, carry):
        body(k, pl.multiple_of(8 * k, 8))
        return carry

    lax.fori_loop(0, STEPS, step, 0)


def split3(value):
    hi = value.astype(BF16).astype(F32)
    rest = value - hi
    mid = rest.astype(BF16).astype(F32)
    return hi, mid, rest - mid


def exchange_stage(ref, lead, bit, blocks, first, each):
    lane = lax.broadcasted_iota(jnp.int32, (8, 128), 1)
    span = 16 << bit
    upper = (lane & span) != 0

    def step(s, carry):
        for e in range(each):
            at = pl.ds(pl.multiple_of(8 * (s * each + e), 8) + first, 8)
            for which in lead:
                for m in range(TILES):
                    if m & (1 << bit):
                        continue
                    lo, hi = which + (m, at), which + (m | (1 << bit), at)
                    a, b = ref[lo], ref[hi]
                    ref[lo] = jnp.where(upper, pltpu.roll(b, span, 1), a)
                    ref[hi] = jnp.where(upper, b, pltpu.roll(a, 128 - span, 1))
        return carry

    lax.fori_loop(0, blocks // each, step, 0)


def prep_kernel(shift_ref, img_ref, weights_ref, taps_ref, up_ref, down_ref, own_ref, img_out, taps_out, work):
    shift = jnp.full((1, 128), shift_ref[0, 0], jnp.int32).astype(F32)
    lane = lax.broadcasted_iota(jnp.int32, (8, 128), 1)
    row = lax.broadcasted_iota(jnp.int32, (8, 128), 0)
    zero = jnp.zeros((8, 128), F32)
    pick = 8 * (lane % 16) + lane // 16
    for j in range(TILES):
        cols = slice(128 * j, 128 * j + 128)
        tile = img_ref[:, cols].astype(F32)
        for b in range(16):
            work[j, 8 * b : 8 * b + 8, :] = jnp.take_along_axis(tile[8 * b : 8 * b + 8], pick, axis=1)
        taps = jnp.concatenate([taps_ref[:, cols].astype(F32), zero[:4]], axis=0)
        work[j, 128:136, :] = jnp.take_along_axis(taps, pick, axis=1)
    for bit in range(3):
        exchange_stage(work, [()], bit, 17, 0, 17)
    for m in range(TILES):
        cols = slice(128 * m, 128 * m + 128)
        tile = work[m, 0:128, :].astype(BF16)
        img_out[:, cols] = tile
        up_ref[0:EDGE, cols] = tile[128 - EDGE :]
        down_ref[0:EDGE, cols] = tile[:EDGE]
        taps_out[m] = work[m, 128:136, :]
    for tap in range(TAPS):
        line = jnp.broadcast_to(weights_ref[tap : tap + 1, :], (8, 128))
        hi, mid, lo = split3(pltpu.roll(line, HALO, 1))
        full = jnp.where(row == 0, hi, jnp.where(row == 1, mid, jnp.where(row == 2, lo, zero)))
        if tap == 0:
            full = jnp.where(row == 3, jnp.broadcast_to(shift, (8, 128)), full)
        at = 256 * tap
        wrapped = jnp.where(lane < HALO, full, zero).astype(BF16)
        own_ref[:, at : at + 128] = jnp.where(lane >= HALO, full, zero).astype(BF16)
        own_ref[:, at + 128 : at + 256] = wrapped
        up_ref[EDGE:BLOCK, at : at + 128] = wrapped
        up_ref[EDGE:BLOCK, at + 128 : at + 256] = zero.astype(BF16)
        down_ref[EDGE:BLOCK, at : at + 128] = zero.astype(BF16)
        down_ref[EDGE:BLOCK, at + 128 : at + 256] = jnp.where(
            (lane >= HALO) & (lane < 2 * HALO), full, zero
        ).astype(BF16)


def warp_kernel(shift_ref, img_ref, low_ref, high_ref, own_ref, taps_ref, out_ref, row_warped, virtual):
    meta = (
        low_ref[EDGE:BLOCK, :].astype(F32)
        + own_ref[...].astype(F32)
        + high_ref[EDGE:BLOCK, :].astype(F32)
    ).astype(BF16)
    place = lax.broadcasted_iota(jnp.int32, (EXT, 256), 0)
    rho = (place % 8) * STEPS + place // 8
    spread = jnp.where(
        rho == lax.broadcasted_iota(jnp.int32, (EXT, 256), 1), jnp.float32(1), jnp.float32(0)
    ).astype(BF16)
    columns = [
        lax.dot_general(
            spread,
            meta[:, 256 * tap : 256 * tap + 256],
            (((1,), (1,)), ((), ())),
            preferred_element_type=F32,
        )
        for tap in range(TAPS)
    ]
    width = 2 * BLOCK + 128
    lane = lax.broadcasted_iota(jnp.int32, (EXT, width), 1)
    image_row = jnp.where(lane < EDGE, lane - EDGE, jnp.where(lane < BLOCK, -1000, lane - BLOCK))
    image_row = jnp.where(lane < BLOCK + 128 + EDGE, image_row, 2000)
    own_row = lax.broadcasted_iota(jnp.int32, (EXT, width), 0)
    own_row = (own_row % 8) * STEPS + own_row // 8 - HALO
    offset = (image_row - own_row + 1).astype(F32) - columns[0][:, 3:4]
    value = jnp.zeros((EXT, width), F32)
    for tap in range(TAPS):
        weight = columns[tap][:, 0:1] + columns[tap][:, 1:2] + columns[tap][:, 2:3]
        value = jnp.where(offset == float(tap), weight, value)
    hi, mid, lo = split3(value)
    source = jnp.concatenate([low_ref[...], img_ref[...], high_ref[...]], axis=0)
    total = jnp.zeros((EXT, 1024), F32)
    for piece in (lo, mid, hi):
        total = total + jnp.dot(piece.astype(BF16), source, preferred_element_type=F32)
    rounded = total.astype(BF16).astype(F32)
    for m in range(TILES):
        row_warped[m] = rounded[:, 128 * m : 128 * m + 128]
    first = shift_ref[0] - 1
    lane = lax.broadcasted_iota(jnp.int32, (EXT, 128), 1)
    for v in range(TILES + TAPS - 1):
        column = first + v
        tile = lax.bitwise_and(column, 7)
        far = lax.shift_right_arithmetic(column, 3)
        moved = pltpu.roll(row_warped[tile], lax.bitwise_and(-far, 127), 1)
        virtual[v] = jnp.where((lane + far >= 0) & (lane + far < 128), moved, 0.0)
    for m in range(TILES):
        terms = [taps_ref[m, t : t + 1, :] * virtual[m + t] for t in range(TAPS)]
        out_ref[m] = ((terms[0] + terms[1]) + (terms[2] + terms[3])).astype(BF16)


def row_bounds(strip):
    first = jnp.where(strip == 0, HALO, 0)
    last = jnp.where(strip == 15, HALO + 128, EXT)
    return first, last


def inside_rows(k, bounds):
    rho = lax.broadcasted_iota(jnp.int32, (8, 128), 0) * STEPS + k
    return (rho >= bounds[0]) & (rho < bounds[1])


def own_stats(x_ref, bounds, x_wide, sum_x, root_x, slope_r, slope_c, boxes):
    def rows(m, turn):
        value = x_ref[m].astype(F32)
        x_wide[m] = value
        steps = steps_of(value)
        put_box(boxes[0], m, turn, steps)
        put_box(boxes[1], m, turn, steps_of(value * value))
        put_rows(boxes[2][1], m, [turn(v) for v in steps])
        seq = [pltpu.roll(steps[-1], 1, 0)] + steps + [pltpu.roll(steps[0], SUBS - 1, 0)]
        put_rows(slope_r, m, [(seq[k + 2] - seq[k]) for k in range(STEPS)])

    over_tiles(rows)

    def cols(k, at):
        s1 = get_box(boxes[0], at)
        s2 = get_box(boxes[1], at)
        scale = jnp.where(inside_rows(k, bounds), -0.5 / 9.0, 0.0)
        rows = pl.ds(at, 8)
        x = [boxes[2][1][7, rows, :]] + [x_wide[m, rows, :] for m in range(8)] + [boxes[2][1][0, rows, :]]
        for m in range(TILES):
            sum_x[m, rows, :] = s1[m]
            root_x[m, rows, :] = lax.rsqrt(s2[m] - s1[m] * s1[m] * (1.0 / CELLS) + 0.25 * CELLS)
            slope_r[m, rows, :] = slope_r[m, rows, :] * scale
            slope_c[m, rows, :] = (x[m + 2] - x[m]) * scale

    over_steps(cols)


def add_pair(y_ref, weight, bounds, first, x_wide, sum_x, root_x, sum_g, sum_h, sum_t, y_wide, coef, boxes):
    def rows(m, turn):
        value = y_ref[m].astype(F32)
        y_wide[m] = value
        put_box(boxes[0], m, turn, steps_of(value))
        put_box(boxes[1], m, turn, steps_of(value * value))
        put_box(boxes[2], m, turn, steps_of(value * x_wide[m]))

    over_tiles(rows)

    def cols(k, at):
        scale = jnp.where(inside_rows(k, bounds), weight, jnp.float32(0))
        s1 = get_box(boxes[0], at)
        s2 = get_box(boxes[1], at)
        s3 = get_box(boxes[2], at)
        for m in range(TILES):
            here = (m, pl.ds(at, 8), slice(None))
            mean = s1[m] * (1.0 / CELLS)
            root = lax.rsqrt(s2[m] - s1[m] * mean + 0.25 * CELLS)
            cov = s3[m] - sum_x[here] * mean
            u = scale * root_x[here] * root
            coef[here] = u
            g, h = u * cov, u * s1[m]
            sum_g[here] = g if first else sum_g[here] + g
            sum_h[here] = h if first else sum_h[here] + h

    over_steps(cols)

    def rows_2(m, turn):
        put_box(boxes[0], m, turn, steps_of(coef[m]))

    over_tiles(rows_2)

    def cols_2(k, at):
        s1 = get_box(boxes[0], at)
        for m in range(TILES):
            here = (m, pl.ds(at, 8), slice(None))
            t = y_wide[here] * s1[m]
            sum_t[here] = t if first else sum_t[here] + t

    over_steps(cols_2)


def finish(x_wide, sum_x, root_x, slope_r, slope_c, sum_g, sum_h, sum_t, natural, grad_ref, disp_ref, boxes):
    def rows(m, turn):
        root = root_x[m]
        g = root * root * sum_g[m]
        put_box(boxes[0], m, turn, steps_of(sum_h[m] - g * sum_x[m]))
        put_box(boxes[1], m, turn, steps_of(g))

    over_tiles(rows)

    def cols(k, at):
        s1 = get_box(boxes[0], at)
        s2 = get_box(boxes[1], at)
        for m in range(TILES):
            here = (m, pl.ds(at, 8), slice(None))
            grad = s1[m] * (1.0 / CELLS) + x_wide[here] * s2[m] - sum_t[here]
            natural[0, m, pl.ds(k, 8, stride=STEPS), :] = grad
            sum_g[here] = grad * slope_r[here]
            sum_h[here] = grad * slope_c[here]

    over_steps(cols)

    def rows_2(m, turn):
        put_box(boxes[0], m, turn, steps_of(sum_g[m]))
        put_box(boxes[1], m, turn, steps_of(sum_h[m]))

    over_tiles(rows_2)

    def cols_2(k, at):
        s1 = get_box(boxes[0], at)
        s2 = get_box(boxes[1], at)
        for m in range(TILES):
            natural[1, m, pl.ds(k, 8, stride=STEPS), :] = s1[m]
            natural[2, m, pl.ds(k, 8, stride=STEPS), :] = s2[m]

    over_steps(cols_2)
    for bit in range(3):
        exchange_stage(natural, [(0,), (1,), (2,)], bit, 16, HALO, 8)
    lane = lax.broadcasted_iota(jnp.int32, (8, 128), 1)
    pick = (lane % 8) * 16 + lane // 8

    def restore(step, carry):
        for e in range(8):
            at = pl.multiple_of(8 * (8 * step + e), 8)
            for which in range(3):
                for j in range(TILES):
                    tile = jnp.take_along_axis(natural[which, j, pl.ds(at + HALO, 8), :], pick, axis=1)
                    if which == 0:
                        grad_ref[pl.ds(at, 8), 128 * j : 128 * j + 128] = tile
                    else:
                        disp_ref[which - 1, pl.ds(at, 8), 128 * j : 128 * j + 128] = tile
        return carry

    lax.fori_loop(0, 2, restore, 0)


def pair_weight(pair_on, own, other):
    low = jnp.minimum(own, other)
    gap = jnp.abs(own - other)
    inside = (other >= 0) & (other < 16)
    on = pair_on[jnp.clip(low, 0, 15), jnp.clip(gap - 1, 0, 2)]
    return jnp.where(inside, on, 0).astype(F32)


def others(own):
    way = 1 - 2 * (own % 2)
    return [own + way, own + 2 * way, own - way, own - 2 * way, own - 3 * way, own + 3 * way]


def field():
    return pltpu.VMEM((TILES, EXT, 128), F32)


def shape(dims, kind):
    return jax.ShapeDtypeStruct(dims, kind)


FIELD = shape((TILES, EXT, 128), F32)


def own_kernel(place, x, x_wide, sum_x, root_x, slope_r, slope_c, *boxes):
    own_stats(x, row_bounds(place[1]), x_wide, sum_x, root_x, slope_r, slope_c, paired(boxes))


def paired(refs):
    return [(refs[2 * i], refs[2 * i + 1]) for i in range(3)]


def pair_kernel(turns, place, pair_on, *refs):
    ys, refs = refs[: len(turns)], refs[len(turns) :]
    first = 0 in turns
    kept = 0 if first else 3
    x_wide, sum_x, root_x = refs[:3]
    g, h, t = refs[3 + kept : 6 + kept]
    y_wide, coef = refs[6 + kept : 8 + kept]
    boxes = paired(refs[8 + kept :])
    names = others(place[0])
    for i, y in zip(turns, ys):
        weight = pair_weight(pair_on, place[0], names[i])
        add_pair(y, weight, row_bounds(place[1]), i == 0, x_wide, sum_x, root_x, g, h, t, y_wide, coef, boxes)


def last_kernel(turns, place, pair_on, *refs):
    ys, refs = refs[: len(turns)], refs[len(turns) :]
    x_wide, sum_x, root_x, slope_r, slope_c, g_in, h_in, t_in, grad, disp, g, h, t, y_wide, coef, natural = refs[:16]
    boxes = paired(refs[16:])
    names = others(place[0])
    for i, y in zip(turns, ys):
        weight = pair_weight(pair_on, place[0], names[i])
        add_pair(y, weight, row_bounds(place[1]), False, x_wide, sum_x, root_x, g, h, t, y_wide, coef, boxes)
    finish(x_wide, sum_x, root_x, slope_r, slope_c, g, h, t, natural, grad, disp, boxes)


def params(mib=24):
    return pltpu.CompilerParams(vmem_limit_bytes=mib * 1024 * 1024)


def cost(us):
    return pl.CostEstimate(flops=int(us * 4_000_000), bytes_accessed=1_000_000, transcendentals=0)


def add_pairs(turns, place, pair_on, ys, stats, sums):
    ins = [place, pair_on, *ys, *stats, *sums]
    start = len(ins) - len(sums)
    return pl.pallas_call(
        functools.partial(pair_kernel, turns),
        out_shape=(FIELD,) * 3,
        in_specs=[SMEM, SMEM] + [VMEM] * (len(ins) - 2),
        out_specs=(VMEM,) * 3,
        scratch_shapes=[field() for _ in range(8)],
        input_output_aliases={start + i: i for i in range(len(sums))},
        compiler_params=params(),
        cost_estimate=cost(1.5 * len(turns)),
        name="pair",
    )(*ins)


def per_device(images, row_weights, row_shift, col_weights, col_shift, pair_on):
    place = jnp.stack([lax.axis_index("sec"), lax.axis_index("strip")]).astype(jnp.int32)
    block = shape((BLOCK, 1024), BF16)
    up, down, own, image, taps = pl.pallas_call(
        prep_kernel,
        out_shape=(block, block, shape((8, 1024), BF16), shape((128, 1024), BF16), shape((TILES, 8, 128), F32)),
        in_specs=[SMEM, VMEM, VMEM, VMEM],
        out_specs=(VMEM,) * 5,
        scratch_shapes=[pltpu.VMEM((TILES, 136, 128), F32)],
        compiler_params=params(),
        name="prep",
    )(row_shift, images[0], row_weights[0], col_weights[0])
    low = lax.ppermute(up, "strip", [(i, i + 1) for i in range(15)])
    high = lax.ppermute(down, "strip", [(i + 1, i) for i in range(15)])
    warped = pl.pallas_call(
        warp_kernel,
        out_shape=shape((TILES, EXT, 128), BF16),
        in_specs=[SMEM] + [VMEM] * 5,
        out_specs=VMEM,
        scratch_shapes=[field(), pltpu.VMEM((TILES + TAPS - 1, EXT, 128), F32)],
        compiler_params=params(),
        name="warp",
    )(col_shift, image, low, high, own, taps)
    sections = range(16)

    def send(value, target):
        pairs = [(s, target(s, 1 - 2 * (s % 2))) for s in sections]
        return lax.ppermute(value, "sec", [p for p in pairs if 0 <= p[1] < 16])

    from_0 = send(warped, lambda s, way: s + way)
    from_1 = send(warped, lambda s, way: s - 2 * way)
    from_2 = send(from_1, lambda s, way: s + way)
    from_3 = send(warped, lambda s, way: s + 2 * way)
    from_4 = send(from_1, lambda s, way: s - way)
    from_5 = send(from_3, lambda s, way: s + way)
    x_wide, sum_x, root_x, slope_r, slope_c = pl.pallas_call(
        own_kernel,
        out_shape=(FIELD,) * 5,
        in_specs=[SMEM, VMEM],
        out_specs=(VMEM,) * 5,
        scratch_shapes=[field() for _ in range(6)],
        compiler_params=params(),
        cost_estimate=cost(1.3),
        name="own",
    )(place, warped)
    stats = (x_wide, sum_x, root_x)
    sums = add_pairs((0,), place, pair_on, (from_0,), stats, ())
    sums = add_pairs((1, 2), place, pair_on, (from_1, from_2), stats, sums)
    sums = add_pairs((3,), place, pair_on, (from_3,), stats, sums)
    grad, disp = pl.pallas_call(
        functools.partial(last_kernel, (4, 5)),
        out_shape=(shape((128, 1024), F32), shape((2, 128, 1024), F32)) + (FIELD,) * 3,
        in_specs=[SMEM, SMEM] + [VMEM] * 10,
        out_specs=(VMEM,) * 5,
        scratch_shapes=[field(), field(), pltpu.VMEM((3, TILES, EXT, 128), F32)] + [field() for _ in range(6)],
        input_output_aliases={9: 2, 10: 3, 11: 4},
        compiler_params=params(),
        cost_estimate=cost(5),
        name="last",
    )(place, pair_on, from_4, from_5, *stats, slope_r, slope_c, *sums)[:2]
    return grad[None], disp[:, None]


def solution(mesh):
    return jax.shard_map(
        per_device,
        mesh=mesh,
        in_specs=(
            P("sec", "strip", None),
            P("sec", None, "strip"),
            P("sec", "strip"),
            P("sec", None, None),
            P("sec"),
            P(),
        ),
        out_specs=(P("sec", "strip", None), P(None, "sec", "strip", None)),
        check_vma=False,
    )
```

time: 81.8 us -> 61.6 us (0.75)
  the two profiles are of different devices: /device:TPU:131 before, /device:TPU:110 now
where the time goes in v2:
time: 61.6 us; the launch traced here: 60.6 us
  Pallas kernels  22.8 us (37%)
  starting transfers between devices  19.9 us (32%)
  waiting for transfers between devices  12.8 us (21%)
  local copies, waits for them, and re-layouts  3.08 us (5%)
  between operations  2.08 us (3%)
    ppermute x6, starting transfers between devices, send(): return lax.ppermute(value, 'sec', [p for p in pairs if 0 <= p[1] < 16])  12.1 us
    pallas_call x3, Pallas kernels, add_pairs(): pl.pallas_call(functools.partial(pair_kernel, turns), out_shape=(FIELD,)...  9.8 us
    pallas_call x1, Pallas kernels, per_device(): pl.pallas_call(functools.partial(last_kernel, (4, 5)), out_shape=(shape((...  9.65 us
    ppermute x1, waiting for transfers between devices, per_device(): high = lax.ppermute(down, 'strip', [(i + 1, i) for i in range(15)])  7.19 us
    ppermute x1, starting transfers between devices, per_device(): low = lax.ppermute(up, 'strip', [(i, i + 1) for i in range(15)])  5.88 us
    ppermute x6, waiting for transfers between devices, send(): return lax.ppermute(value, 'sec', [p for p in pairs if 0 <= p[1] < 16])  5.57 us
    unnamed x9, local copies, waits for them, and re-layouts  3.08 us
    ppermute x1, starting transfers between devices, per_device(): high = lax.ppermute(down, 'strip', [(i + 1, i) for i in range(15)])  1.92 us
  transfers between devices with their start and end apart: 8, of which 2 were waited for; matrix products, arithmetic and copies ran while one was open for 0% of the time, Pallas kernels for 19%

profile of v2, /device:TPU:110, one launch (start us, length us, event | category | flops | bytes accessed | tf_op | source)
XLA Modules:
  0.0 60.6 jit_solution(6770603726984733970)
XLA Ops:
  1.3 0.0 copy-start.2
  1.3 0.7 %copy-done.2 = f32[1,4,128]{2,1,0:T(4,128)S(1)} copy-done((f32[1,4,128]{2,1,0:T(4,128)S(1)}, f32[1,4,128]{2,1,0:T(4,128)}, u32[]{:S(2)}) %copy-start.2) | copy-done | bytes 2072
  2.0 0.0 copy-start
  2.0 0.9 %copy-done = bf16[1,128,1024]{2,1,0:T(8,128)(2,1)S(1)} copy-done((bf16[1,128,1024]{2,1,0:T(8,128)(2,1)S(1)}, bf16[1,128,1024]{2,1,0:T(8,128)(2,1)}, u32[]{:S(2)}) %copy-start) | copy-done | bytes 262168
  2.9 0.0 copy-start.1
  2.9 0.7 %copy-done.1 = bf16[1,4,1024]{2,1,0:T(4,128)(2,1)S(1)} copy-done((bf16[1,4,1024]{2,1,0:T(4,128)(2,1)S(1)}, bf16[1,4,1024]{2,1,0:T(4,128)(2,1)}, u32[]{:S(2)}) %copy-start.1) | copy-done | bytes 8216
  3.6 0.4 prep.1
  4.0 5.9 %collective-permute-start = (bf16[32,1024]{1,0:T(8,128)(2,1)S(1)}, bf16[32,1024]{1,0:T(8,128)(2,1)S(1)}, u32[]{:S(2)}, u32[]{:S(2)}) collective-permute-start(bf16[32,1024]{1,0:T(8,128)(2,1)S(1)} %get-tuple-element.24), channel_id=1, source_target_pairs={{0,1},{1,2},{2,3},{3,4},{4,5},{5,6},{6,7},{7,8},{8,9},{9,10},{10,1... | collective-permute-start | bytes 196616 | tf_op jit(solution)/shard_map/ppermute | solution.py:465
  9.9 1.9 %collective-permute-start.1 = (bf16[32,1024]{1,0:T(8,128)(2,1)S(1)}, bf16[32,1024]{1,0:T(8,128)(2,1)S(1)}, u32[]{:S(2)}, u32[]{:S(2)}) collective-permute-start(bf16[32,1024]{1,0:T(8,128)(2,1)S(1)} %get-tuple-element.25), channel_id=1, source_target_pairs={{1,0},{2,1},{3,2},{4,3},{5,4},{6,5},{7,6},{8,7},{9,8},{10,9},{11,1... | collective-permute-start | bytes 196616 | tf_op jit(solution)/shard_map/ppermute | solution.py:466
  12.5 0.0 collective-permute-done.low_ref
  12.5 7.2 %collective-permute-done.1.high_ref = bf16[32,1024]{1,0:T(8,128)(2,1)S(1)} collective-permute-done((bf16[32,1024]{1,0:T(8,128)(2,1)S(1)}, bf16[32,1024]{1,0:T(8,128)(2,1)S(1)}, u32[]{:S(2)}, u32[]{:S(2)}) %collective-permute-start.1) | collective-permute-done | bytes 65568 | tf_op jit(solution)/shard_map/ppermute | solution.py:466
  19.7 1.2 %warp.1.x = bf16[8,152,128]{2,1,0:T(8,128)(2,1)S(1)} custom-call(s32[1]{0:T(128)S(6)} %copy.32.shift_ref, bf16[128,1024]{1,0:T(8,128)(2,1)S(1)} %get-tuple-element.23.img_ref, bf16[32,1024]{1,0:T(8,128)(2,1)S(1)} %collective-permute-done.low_ref, bf16[32,1024]{1,0:T(8,128)(2,1)S(1)} %collective-permute-done.1.high_ref, ...), custom_call_target="tpu_custom_call" | custom-call | tf_op jit(solution)/shard_map/warp/pallas_call | solution.py:467
  20.9 2.4 %collective-permute-start.2 = (bf16[8,152,128]{2,1,0:T(8,128)(2,1)S(1)}, bf16[8,152,128]{2,1,0:T(8,128)(2,1)S(1)}, u32[]{:S(2)}, u32[]{:S(2)}) collective-permute-start(bf16[8,152,128]{2,1,0:T(8,128)(2,1)S(1)} %warp.1.x), channel_id=1, source_target_pairs={{16,48},{32,0},{48,80},{64,32},{80,112},{96,64},{112,144},{128,96}... | collective-permute-start | bytes 933896 | tf_op jit(solution)/shard_map/ppermute | solution.py:480
  23.2 3.5 %collective-permute-start.4 = (bf16[8,152,128]{2,1,0:T(8,128)(2,1)S(1)}, bf16[8,152,128]{2,1,0:T(8,128)(2,1)S(1)}, u32[]{:S(2)}, u32[]{:S(2)}) collective-permute-start(bf16[8,152,128]{2,1,0:T(8,128)(2,1)S(1)} %warp.1.x), channel_id=1, source_target_pairs={{0,32},{32,64},{48,16},{64,96},{80,48},{96,128},{112,80},{128,160}... | collective-permute-start | bytes 933896 | tf_op jit(solution)/shard_map/ppermute | solution.py:480
  26.7 0.1 collective-permute-start.7
  26.8 5.5 %collective-permute-done.2.refs_0_ = bf16[8,152,128]{2,1,0:T(8,128)(2,1)S(1)} collective-permute-done((bf16[8,152,128]{2,1,0:T(8,128)(2,1)S(1)}, bf16[8,152,128]{2,1,0:T(8,128)(2,1)S(1)}, u32[]{:S(2)}, u32[]{:S(2)}) %collective-permute-start.2) | collective-permute-done | bytes 311328 | tf_op jit(solution)/shard_map/ppermute | solution.py:480
  32.3 0.0 collective-permute-start.6
  32.4 0.0 collective-permute-done.4.refs_0_
  32.4 0.5 collective-permute-start.5
  32.9 5.7 %collective-permute-start.3 = (bf16[8,152,128]{2,1,0:T(8,128)(2,1)S(1)}, bf16[8,152,128]{2,1,0:T(8,128)(2,1)S(1)}, u32[]{:S(2)}, u32[]{:S(2)}) collective-permute-start(bf16[8,152,128]{2,1,0:T(8,128)(2,1)S(1)} %collective-permute-done.2.refs_0_), channel_id=1, source_target_pairs={{16,32},{32,16},{48,64},{64,48},{80,96},{96,80},{112,128},{128,112... | collective-permute-start | bytes 933896 | tf_op jit(solution)/shard_map/ppermute | solution.py:480
  38.5 0.0 copy-start.3
  38.6 0.7 %copy-done.3 = s32[16,3]{0,1:T(4,128)S(1)} copy-done((s32[16,3]{0,1:T(4,128)S(1)}, s32[16,3]{0,1:T(4,128)}, u32[]{:S(2)}) %copy-start.3) | copy-done | bytes 216
  39.2 0.1 copy.20.pair_on
  39.3 0.1 pad_add_fusion.place
  39.4 1.7 %own.1 = (f32[8,152,128]{2,1,0:T(8,128)S(1)}, f32[8,152,128]{2,1,0:T(8,128)S(1)}, f32[8,152,128]{2,1,0:T(8,128)S(1)}, f32[8,152,128]{2,1,0:T(8,128)S(1)}, f32[8,152,128]{2,1,0:T(8,128)S(1)}) custom-call(s32[2]{0:T(128)S(1)} %pad_add_fusion.place, bf16[8,152,128]{2,1,0:T(8,128)(2,1)S(1)} %warp.1.x), custom_call_target="tpu_custom_call" | custom-call | flops 5200000 | bytes 1000000 | tf_op jit(solution)/shard_map/own/pallas_call | solution.py:488
  41.1 0.0 collective-permute-done.7.refs_0_
  41.1 2.5 %pair.3 = (f32[8,152,128]{2,1,0:T(8,128)S(1)}, f32[8,152,128]{2,1,0:T(8,128)S(1)}, f32[8,152,128]{2,1,0:T(8,128)S(1)}) custom-call(s32[2]{0:T(128)S(1)} %pad_add_fusion.place, s32[16,3]{1,0:T(8,128)S(1)} %copy.20.pair_on, bf16[8,152,128]{2,1,0:T(8,128)(2,1)S(1)} %collective-permute-done.7.refs_0_, f32[8,152,128]{2,1,0:T(8,128)S(1)} %get-tuple-element.28.refs_1_.refs_2_, ...), custom_call_target="tpu_custom_call" | custom-call | flops 6000000 | bytes 1000000 | tf_op jit(solution)/shard_map/pair/pallas_call | solution.py:440
  43.7 0.0 collective-permute-done.6.refs_1_
  43.7 4.6 %pair.4 = (f32[8,152,128]{2,1,0:T(8,128)S(1)}, f32[8,152,128]{2,1,0:T(8,128)S(1)}, f32[8,152,128]{2,1,0:T(8,128)S(1)}) custom-call(s32[2]{0:T(128)S(1)} %pad_add_fusion.place, s32[16,3]{1,0:T(8,128)S(1)} %copy.20.pair_on, bf16[8,152,128]{2,1,0:T(8,128)(2,1)S(1)} %collective-permute-done.2.refs_0_, ...), custom_call_target="tpu_custom_call", output_to_operand_aliasing={{0}: (7, {}), {1}: (8, {}), {2}: (9, {})} | custom-call | flops 12000000 | bytes 1000000 | tf_op jit(solution)/shard_map/pair/pallas_call | solution.py:440
  48.3 2.7 %pair.5 = (f32[8,152,128]{2,1,0:T(8,128)S(1)}, f32[8,152,128]{2,1,0:T(8,128)S(1)}, f32[8,152,128]{2,1,0:T(8,128)S(1)}) custom-call(s32[2]{0:T(128)S(1)} %pad_add_fusion.place, s32[16,3]{1,0:T(8,128)S(1)} %copy.20.pair_on, bf16[8,152,128]{2,1,0:T(8,128)(2,1)S(1)} %collective-permute-done.4.refs_0_, ...), custom_call_target="tpu_custom_call", output_to_operand_aliasing={{0}: (6, {}), {1}: (7, {}), {2}: (8, {})} | custom-call | flops 6000000 | bytes 1000000 | tf_op jit(solution)/shard_map/pair/pallas_call | solution.py:440
  51.0 0.0 collective-permute-done.5.refs_1_
  51.0 0.0 collective-permute-done.3.refs_0_
  51.0 9.6 %last.1 = (f32[128,1024]{1,0:T(8,128)}, f32[2,128,1024]{2,1,0:T(8,128)}, f32[8,152,128]{2,1,0:T(8,128)S(1)}, f32[8,152,128]{2,1,0:T(8,128)S(1)}, f32[8,152,128]{2,1,0:T(8,128)S(1)}) custom-call(s32[2]{0:T(128)S(1)} %pad_add_fusion.place, s32[16,3]{1,0:T(8,128)S(1)} %copy.20.pair_on, ...), custom_call_target="tpu_custom_call", output_to_operand_aliasing={{2}: (9, {}), {3}: (10, {}), {4}: (11, {})} | custom-call | flops 20000000 | bytes 1000000 | tf_op jit(solution)/shard_map/last/pallas_call | solution.py:502
Async XLA Ops:
  1.3 0.7 %copy-start.2 = (f32[1,4,128]{2,1,0:T(4,128)S(1)}, f32[1,4,128]{2,1,0:T(4,128)}, u32[]{:S(2)}) copy-start(f32[1,4,128]{2,1,0:T(4,128)} %param.7) | copy-start | bytes 6148
  2.0 0.9 %copy-start = (bf16[1,128,1024]{2,1,0:T(8,128)(2,1)S(1)}, bf16[1,128,1024]{2,1,0:T(8,128)(2,1)}, u32[]{:S(2)}) copy-start(bf16[1,128,1024]{2,1,0:T(8,128)(2,1)} %param.6) | copy-start | bytes 786436
  2.9 0.7 %copy-start.1 = (bf16[1,4,1024]{2,1,0:T(4,128)(2,1)S(1)}, bf16[1,4,1024]{2,1,0:T(4,128)(2,1)}, u32[]{:S(2)}) copy-start(bf16[1,4,1024]{2,1,0:T(4,128)(2,1)} %param.9) | copy-start | bytes 24580
  4.0 8.5 %collective-permute-start = (bf16[32,1024]{1,0:T(8,128)(2,1)S(1)}, bf16[32,1024]{1,0:T(8,128)(2,1)S(1)}, u32[]{:S(2)}, u32[]{:S(2)}) collective-permute-start(bf16[32,1024]{1,0:T(8,128)(2,1)S(1)} %get-tuple-element.24), channel_id=1, source_target_pairs={{0,1},{1,2},{2,3},{3,4},{4,5},{5,6},{6,7},{7,8},{8,9},{9,10},{10,1... | collective-permute-start | bytes 196616 | tf_op jit(solution)/shard_map/ppermute | solution.py:465
  9.9 9.8 %collective-permute-start.1 = (bf16[32,1024]{1,0:T(8,128)(2,1)S(1)}, bf16[32,1024]{1,0:T(8,128)(2,1)S(1)}, u32[]{:S(2)}, u32[]{:S(2)}) collective-permute-start(bf16[32,1024]{1,0:T(8,128)(2,1)S(1)} %get-tuple-element.25), channel_id=1, source_target_pairs={{1,0},{2,1},{3,2},{4,3},{5,4},{6,5},{7,6},{8,7},{9,8},{10,9},{11,1... | collective-permute-start | bytes 196616 | tf_op jit(solution)/shard_map/ppermute | solution.py:466
  20.9 11.5 %collective-permute-start.2 = (bf16[8,152,128]{2,1,0:T(8,128)(2,1)S(1)}, bf16[8,152,128]{2,1,0:T(8,128)(2,1)S(1)}, u32[]{:S(2)}, u32[]{:S(2)}) collective-permute-start(bf16[8,152,128]{2,1,0:T(8,128)(2,1)S(1)} %warp.1.x), channel_id=1, source_target_pairs={{16,48},{32,0},{48,80},{64,32},{80,112},{96,64},{112,144},{128,96}... | collective-permute-start | bytes 933896 | tf_op jit(solution)/shard_map/ppermute | solution.py:480
  23.2 9.2 %collective-permute-start.4 = (bf16[8,152,128]{2,1,0:T(8,128)(2,1)S(1)}, bf16[8,152,128]{2,1,0:T(8,128)(2,1)S(1)}, u32[]{:S(2)}, u32[]{:S(2)}) collective-permute-start(bf16[8,152,128]{2,1,0:T(8,128)(2,1)S(1)} %warp.1.x), channel_id=1, source_target_pairs={{0,32},{32,64},{48,16},{64,96},{80,48},{96,128},{112,80},{128,160}... | collective-permute-start | bytes 933896 | tf_op jit(solution)/shard_map/ppermute | solution.py:480
  26.7 14.4 %collective-permute-start.7 = (bf16[8,152,128]{2,1,0:T(8,128)(2,1)S(1)}, bf16[8,152,128]{2,1,0:T(8,128)(2,1)S(1)}, u32[]{:S(2)}, u32[]{:S(2)}) collective-permute-start(bf16[8,152,128]{2,1,0:T(8,128)(2,1)S(1)} %warp.1.x), channel_id=1, source_target_pairs={{0,16},{16,0},{32,48},{48,32},{64,80},{80,64},{96,112},{112,96},{1... | collective-permute-start | bytes 933896 | tf_op jit(solution)/shard_map/ppermute | solution.py:480
  32.3 11.3 %collective-permute-start.6 = (bf16[8,152,128]{2,1,0:T(8,128)(2,1)S(1)}, bf16[8,152,128]{2,1,0:T(8,128)(2,1)S(1)}, u32[]{:S(2)}, u32[]{:S(2)}) collective-permute-start(bf16[8,152,128]{2,1,0:T(8,128)(2,1)S(1)} %collective-permute-done.2.refs_0_), channel_id=1, source_target_pairs={{0,16},{16,0},{32,48},{48,32},{64,80},{80,64},{96,112},{112,96},{1... | collective-permute-start | bytes 933896 | tf_op jit(solution)/shard_map/ppermute | solution.py:480
  32.4 18.6 %collective-permute-start.5 = (bf16[8,152,128]{2,1,0:T(8,128)(2,1)S(1)}, bf16[8,152,128]{2,1,0:T(8,128)(2,1)S(1)}, u32[]{:S(2)}, u32[]{:S(2)}) collective-permute-start(bf16[8,152,128]{2,1,0:T(8,128)(2,1)S(1)} %collective-permute-done.4.refs_0_), channel_id=1, source_target_pairs={{0,16},{16,0},{32,48},{48,32},{64,80},{80,64},{96,112},{112,96},{1... | collective-permute-start | bytes 933896 | tf_op jit(solution)/shard_map/ppermute | solution.py:480
  32.9 18.1 %collective-permute-start.3 = (bf16[8,152,128]{2,1,0:T(8,128)(2,1)S(1)}, bf16[8,152,128]{2,1,0:T(8,128)(2,1)S(1)}, u32[]{:S(2)}, u32[]{:S(2)}) collective-permute-start(bf16[8,152,128]{2,1,0:T(8,128)(2,1)S(1)} %collective-permute-done.2.refs_0_), channel_id=1, source_target_pairs={{16,32},{32,16},{48,64},{64,48},{80,96},{96,80},{112,128},{128,112... | collective-permute-start | bytes 933896 | tf_op jit(solution)/shard_map/ppermute | solution.py:480
  38.5 0.7 %copy-start.3 = (s32[16,3]{0,1:T(4,128)S(1)}, s32[16,3]{0,1:T(4,128)}, u32[]{:S(2)}) copy-start(s32[16,3]{0,1:T(4,128)} %param.11) | copy-start | bytes 580

commit v3 on v2

--- a/solution.py
+++ b/solution.py
@@ -6,6 +6,7 @@
 from jax.experimental import pallas as pl
 from jax.experimental.pallas import tpu as pltpu
 from jax.sharding import PartitionSpec as P
+
 
 TAPS = 4
 HALO = 12
@@ -18,7 +19,11 @@
 BF16 = jnp.bfloat16
 VMEM = pl.BlockSpec(memory_space=pltpu.VMEM)
 SMEM = pl.BlockSpec(memory_space=pltpu.SMEM)
+HBM = pl.BlockSpec(memory_space=pl.ANY)
 EDGE = 24
+UNROLL = 3
+GROUP = 8
+EACH = 16
 BLOCK = 32
 
 
@@ -71,21 +76,26 @@
         ref[tile, 8 * k : 8 * k + 8, :] = v
 
 
-def over_tiles(body, each=4):
+def over_tiles(body, each=GROUP):
     lane = lax.broadcasted_iota(jnp.int32, (8, 128), 1)
 
-    def half(h, carry):
-        shift = jnp.where(h == 0, 127, 1)
-        keep = lane != jnp.where(h == 0, 127, 0)
-
-        def turn(v):
-            return jnp.where(keep, pltpu.roll(v, shift, 1), 0.0)
-
-        for i in range(4):
-            body(4 * h + i, turn)
+    def turn_to(shift, edge):
+        keep = lane != edge
+        return lambda v: jnp.where(keep, pltpu.roll(v, shift, 1), 0.0)
+
+    if each == TILES:
+        for m in range(TILES):
+            body(m, turn_to(127, 127) if m < 4 else turn_to(1, 0))
+        return
+
+    def part(q, carry):
+        low = each * q < 4
+        turn = turn_to(jnp.where(low, 127, 1), jnp.where(low, 127, 0))
+        for i in range(each):
+            body(each * q + i, turn)
         return carry
 
-    lax.fori_loop(0, 2, half, 0)
+    lax.fori_loop(0, TILES // each, part, 0)
 
 
 def put_box(pair, m, turn, values):
@@ -104,12 +114,16 @@
     return col_window(seq)
 
 
-def over_steps(body):
-    def step(k, carry):
-        body(k, pl.multiple_of(8 * k, 8))
+def over_steps(body, each=UNROLL):
+    def step(i, carry):
+        for e in range(each):
+            k = each * i + e
+            body(k, pl.multiple_of(8 * k, 8))
         return carry
 
-    lax.fori_loop(0, STEPS, step, 0)
+    lax.fori_loop(0, STEPS // each, step, 0)
+    for k in range(STEPS // each * each, STEPS):
+        body(k, 8 * k)
 
 
 def split3(value):
@@ -119,7 +133,7 @@
     return hi, mid, rest - mid
 
 
-def exchange_stage(ref, lead, bit, blocks, first, each):
+def exchange_stage(source, target, lead, bit, blocks, first, each):
     lane = lax.broadcasted_iota(jnp.int32, (8, 128), 1)
     span = 16 << bit
     upper = (lane & span) != 0
@@ -132,16 +146,16 @@
                     if m & (1 << bit):
                         continue
                     lo, hi = which + (m, at), which + (m | (1 << bit), at)
-                    a, b = ref[lo], ref[hi]
-                    ref[lo] = jnp.where(upper, pltpu.roll(b, span, 1), a)
-                    ref[hi] = jnp.where(upper, b, pltpu.roll(a, 128 - span, 1))
+                    a, b = source[lo], source[hi]
+                    target[lo] = jnp.where(upper, pltpu.roll(b, span, 1), a)
+                    target[hi] = jnp.where(upper, b, pltpu.roll(a, 128 - span, 1))
         return carry
 
     lax.fori_loop(0, blocks // each, step, 0)
 
 
-def prep_kernel(shift_ref, img_ref, weights_ref, taps_ref, up_ref, down_ref, own_ref, img_out, taps_out, work):
-    shift = jnp.full((1, 128), shift_ref[0, 0], jnp.int32).astype(F32)
+def prep_kernel(img_ref, small_ref, up_ref, down_ref, own_ref, img_out, taps_out, work, other):
+    shift = small_ref[8:9, 0:128]
     lane = lax.broadcasted_iota(jnp.int32, (8, 128), 1)
     row = lax.broadcasted_iota(jnp.int32, (8, 128), 0)
     zero = jnp.zeros((8, 128), F32)
@@ -151,19 +165,19 @@
         tile = img_ref[:, cols].astype(F32)
         for b in range(16):
             work[j, 8 * b : 8 * b + 8, :] = jnp.take_along_axis(tile[8 * b : 8 * b + 8], pick, axis=1)
-        taps = jnp.concatenate([taps_ref[:, cols].astype(F32), zero[:4]], axis=0)
-        work[j, 128:136, :] = jnp.take_along_axis(taps, pick, axis=1)
-    for bit in range(3):
-        exchange_stage(work, [()], bit, 17, 0, 17)
+        work[j, 128:136, :] = jnp.take_along_axis(small_ref[0:8, cols], pick, axis=1)
+    exchange_stage(work, other, [()], 0, 17, 0, 17)
+    exchange_stage(other, work, [()], 1, 17, 0, 17)
+    exchange_stage(work, other, [()], 2, 17, 0, 17)
     for m in range(TILES):
         cols = slice(128 * m, 128 * m + 128)
-        tile = work[m, 0:128, :].astype(BF16)
+        tile = other[m, 0:128, :].astype(BF16)
         img_out[:, cols] = tile
         up_ref[0:EDGE, cols] = tile[128 - EDGE :]
         down_ref[0:EDGE, cols] = tile[:EDGE]
-        taps_out[m] = work[m, 128:136, :]
+        taps_out[m] = other[m, 128:136, :]
     for tap in range(TAPS):
-        line = jnp.broadcast_to(weights_ref[tap : tap + 1, :], (8, 128))
+        line = jnp.broadcast_to(small_ref[4 + tap : 5 + tap, 0:128], (8, 128))
         hi, mid, lo = split3(pltpu.roll(line, HALO, 1))
         full = jnp.where(row == 0, hi, jnp.where(row == 1, mid, jnp.where(row == 2, lo, zero)))
         if tap == 0:
@@ -232,18 +246,12 @@
         out_ref[m] = ((terms[0] + terms[1]) + (terms[2] + terms[3])).astype(BF16)
 
 
-def row_bounds(strip):
-    first = jnp.where(strip == 0, HALO, 0)
-    last = jnp.where(strip == 15, HALO + 128, EXT)
-    return first, last
-
-
-def inside_rows(k, bounds):
-    rho = lax.broadcasted_iota(jnp.int32, (8, 128), 0) * STEPS + k
-    return (rho >= bounds[0]) & (rho < bounds[1])
-
-
-def own_stats(x_ref, bounds, x_wide, sum_x, root_x, slope_r, slope_c, boxes):
+def inside_rows(k, plan):
+    rho = (lax.broadcasted_iota(jnp.int32, (8, 128), 0) * STEPS + k).astype(F32)
+    return (rho >= plan[6:7, :]) & (rho < plan[7:8, :])
+
+
+def own_stats(x_ref, plan, x_wide, sum_x, root_x, slope_r, slope_c, boxes):
     def rows(m, turn):
         value = x_ref[m].astype(F32)
         x_wide[m] = value
@@ -259,7 +267,7 @@
     def cols(k, at):
         s1 = get_box(boxes[0], at)
         s2 = get_box(boxes[1], at)
-        scale = jnp.where(inside_rows(k, bounds), -0.5 / 9.0, 0.0)
+        scale = jnp.where(inside_rows(k, plan), -0.5 / 9.0, 0.0)
         rows = pl.ds(at, 8)
         x = [boxes[2][1][7, rows, :]] + [x_wide[m, rows, :] for m in range(8)] + [boxes[2][1][0, rows, :]]
         for m in range(TILES):
@@ -271,7 +279,7 @@
     over_steps(cols)
 
 
-def add_pair(y_ref, weight, bounds, first, x_wide, sum_x, root_x, sum_g, sum_h, sum_t, y_wide, coef, boxes):
+def add_pair(y_ref, which, plan, first, x_wide, sum_x, root_x, sum_g, sum_h, sum_t, y_wide, coef, boxes):
     def rows(m, turn):
         value = y_ref[m].astype(F32)
         y_wide[m] = value
@@ -282,7 +290,7 @@
     over_tiles(rows)
 
     def cols(k, at):
-        scale = jnp.where(inside_rows(k, bounds), weight, jnp.float32(0))
+        scale = jnp.where(inside_rows(k, plan), plan[which : which + 1, :], 0.0)
         s1 = get_box(boxes[0], at)
         s2 = get_box(boxes[1], at)
         s3 = get_box(boxes[2], at)
@@ -314,7 +322,28 @@
     over_steps(cols_2)
 
 
-def finish(x_wide, sum_x, root_x, slope_r, slope_c, sum_g, sum_h, sum_t, natural, grad_ref, disp_ref, boxes):
+def restore(natural, other, which, target):
+    lead = [(w,) for w in which]
+    exchange_stage(natural, other, lead, 0, 16, HALO, EACH // len(which))
+    exchange_stage(other, natural, lead, 1, 16, HALO, EACH // len(which))
+    exchange_stage(natural, other, lead, 2, 16, HALO, EACH // len(which))
+    lane = lax.broadcasted_iota(jnp.int32, (8, 128), 1)
+    pick = (lane % 8) * 16 + lane // 8
+    each = EACH // len(which)
+
+    def step(s, carry):
+        for e in range(each):
+            at = pl.multiple_of(8 * (each * s + e), 8)
+            for w in which:
+                for j in range(TILES):
+                    tile = jnp.take_along_axis(other[w, j, pl.ds(at + HALO, 8), :], pick, axis=1)
+                    target[w, pl.ds(at, 8), 128 * j : 128 * j + 128] = tile
+        return carry
+
+    lax.fori_loop(0, 16 // each, step, 0)
+
+
+def finish(x_wide, sum_x, root_x, slope_r, slope_c, sum_g, sum_h, sum_t, natural, other, wide, sems, grad_hbm, disp_hbm, boxes):
     def rows(m, turn):
         root = root_x[m]
         g = root * root * sum_g[m]
@@ -334,6 +363,9 @@
             sum_h[here] = grad * slope_c[here]
 
     over_steps(cols)
+    restore(natural, other, [0], wide)
+    out = pltpu.make_async_copy(wide.at[0], grad_hbm, sems.at[0])
+    out.start()
 
     def rows_2(m, turn):
         put_box(boxes[0], m, turn, steps_of(sum_g[m]))
@@ -349,32 +381,11 @@
             natural[2, m, pl.ds(k, 8, stride=STEPS), :] = s2[m]
 
     over_steps(cols_2)
-    for bit in range(3):
-        exchange_stage(natural, [(0,), (1,), (2,)], bit, 16, HALO, 8)
-    lane = lax.broadcasted_iota(jnp.int32, (8, 128), 1)
-    pick = (lane % 8) * 16 + lane // 8
-
-    def restore(step, carry):
-        for e in range(8):
-            at = pl.multiple_of(8 * (8 * step + e), 8)
-            for which in range(3):
-                for j in range(TILES):
-                    tile = jnp.take_along_axis(natural[which, j, pl.ds(at + HALO, 8), :], pick, axis=1)
-                    if which == 0:
-                        grad_ref[pl.ds(at, 8), 128 * j : 128 * j + 128] = tile
-                    else:
-                        disp_ref[which - 1, pl.ds(at, 8), 128 * j : 128 * j + 128] = tile
-        return carry
-
-    lax.fori_loop(0, 2, restore, 0)
-
-
-def pair_weight(pair_on, own, other):
-    low = jnp.minimum(own, other)
-    gap = jnp.abs(own - other)
-    inside = (other >= 0) & (other < 16)
-    on = pair_on[jnp.clip(low, 0, 15), jnp.clip(gap - 1, 0, 2)]
-    return jnp.where(inside, on, 0).astype(F32)
+    restore(natural, other, [1, 2], wide)
+    out_2 = pltpu.make_async_copy(wide.at[pl.ds(1, 2)], disp_hbm, sems.at[1])
+    out_2.start()
+    out.wait()
+    out_2.wait()
 
 
 def others(own):
@@ -393,15 +404,26 @@
 FIELD = shape((TILES, EXT, 128), F32)
 
 
-def own_kernel(place, x, x_wide, sum_x, root_x, slope_r, slope_c, *boxes):
-    own_stats(x, row_bounds(place[1]), x_wide, sum_x, root_x, slope_r, slope_c, paired(boxes))
+def own_kernel(small, x, x_wide, sum_x, root_x, slope_r, slope_c, plan, *boxes):
+    own, strip = lax.axis_index("sec"), lax.axis_index("strip")
+    row = lax.broadcasted_iota(jnp.int32, (8, 128), 0)
+    lane = lax.broadcasted_iota(jnp.int32, (8, 128), 1)
+    table = small[8:16, 0:128]
+    lines = jnp.where(row == 6, jnp.where(strip == 0, HALO, 0), jnp.where(strip == 15, HALO + 128, EXT)).astype(F32)
+    for i, section in enumerate(others(own)):
+        low, gap = jnp.minimum(own, section), jnp.abs(own - section)
+        here = (row == gap) & (lane == low) & (section >= 0) & (section < 16)
+        weight = jnp.sum(jnp.sum(jnp.where(here, table, 0.0), axis=1, keepdims=True), axis=0, keepdims=True)
+        lines = jnp.where(row == i, weight, lines)
+    plan[...] = lines
+    own_stats(x, lines, x_wide, sum_x, root_x, slope_r, slope_c, paired(boxes))
 
 
 def paired(refs):
     return [(refs[2 * i], refs[2 * i + 1]) for i in range(3)]
 
 
-def pair_kernel(turns, place, pair_on, *refs):
+def pair_kernel(turns, plan, *refs):
     ys, refs = refs[: len(turns)], refs[len(turns) :]
     first = 0 in turns
     kept = 0 if first else 3
@@ -409,21 +431,23 @@
     g, h, t = refs[3 + kept : 6 + kept]
     y_wide, coef = refs[6 + kept : 8 + kept]
     boxes = paired(refs[8 + kept :])
-    names = others(place[0])
     for i, y in zip(turns, ys):
-        weight = pair_weight(pair_on, place[0], names[i])
-        add_pair(y, weight, row_bounds(place[1]), i == 0, x_wide, sum_x, root_x, g, h, t, y_wide, coef, boxes)
-
-
-def last_kernel(turns, place, pair_on, *refs):
+        add_pair(y, i, plan[...], i == 0, x_wide, sum_x, root_x, g, h, t, y_wide, coef, boxes)
+
+
+def last_kernel(turns, plan, *refs):
     ys, refs = refs[: len(turns)], refs[len(turns) :]
-    x_wide, sum_x, root_x, slope_r, slope_c, g_in, h_in, t_in, grad, disp, g, h, t, y_wide, coef, natural = refs[:16]
-    boxes = paired(refs[16:])
-    names = others(place[0])
+    x_wide, sum_x, root_x, slope_r, slope_c, _, _, _, grad, disp, g, h, t, y_wide, coef, natural, other, wide, sems = refs[:19]
+    boxes = paired(refs[19:])
     for i, y in zip(turns, ys):
-        weight = pair_weight(pair_on, place[0], names[i])
-        add_pair(y, weight, row_bounds(place[1]), False, x_wide, sum_x, root_x, g, h, t, y_wide, coef, boxes)
-    finish(x_wide, sum_x, root_x, slope_r, slope_c, g, h, t, natural, grad, disp, boxes)
+        add_pair(y, i, plan[...], False, x_wide, sum_x, root_x, g, h, t, y_wide, coef, boxes)
+    finish(x_wide, sum_x, root_x, slope_r, slope_c, g, h, t, natural, other, wide, sems, grad, disp, boxes)
+
+
+def last_scratch():
+    three = pltpu.VMEM((3, TILES, EXT, 128), F32)
+    wide = pltpu.VMEM((3, 128, 1024), F32)
+    return [field(), field(), three, three, wide, pltpu.SemaphoreType.DMA((2,))] + [field() for _ in range(6)]
 
 
 def params(mib=24):
@@ -434,13 +458,13 @@
     return pl.CostEstimate(flops=int(us * 4_000_000), bytes_accessed=1_000_000, transcendentals=0)
 
 
-def add_pairs(turns, place, pair_on, ys, stats, sums):
-    ins = [place, pair_on, *ys, *stats, *sums]
+def add_pairs(turns, plan, ys, stats, sums):
+    ins = [plan, *ys, *stats, *sums]
     start = len(ins) - len(sums)
     return pl.pallas_call(
         functools.partial(pair_kernel, turns),
         out_shape=(FIELD,) * 3,
-        in_specs=[SMEM, SMEM] + [VMEM] * (len(ins) - 2),
+        in_specs=[VMEM] * len(ins),
         out_specs=(VMEM,) * 3,
         scratch_shapes=[field() for _ in range(8)],
         input_output_aliases={start + i: i for i in range(len(sums))},
@@ -451,17 +475,35 @@
 
 
 def per_device(images, row_weights, row_shift, col_weights, col_shift, pair_on):
-    place = jnp.stack([lax.axis_index("sec"), lax.axis_index("strip")]).astype(jnp.int32)
     block = shape((BLOCK, 1024), BF16)
+
+    def wide(value):
+        return jnp.pad(value.astype(F32), ((0, 0), (0, 1024 - value.shape[1])))
+
+    small = jnp.concatenate(
+        [
+            col_weights[0].astype(F32),
+            wide(row_weights[0]),
+            jnp.broadcast_to(row_shift.astype(F32), (1, 1024)),
+            wide(pair_on.T),
+            jnp.zeros((4, 1024), F32),
+        ]
+    )
     up, down, own, image, taps = pl.pallas_call(
         prep_kernel,
-        out_shape=(block, block, shape((8, 1024), BF16), shape((128, 1024), BF16), shape((TILES, 8, 128), F32)),
-        in_specs=[SMEM, VMEM, VMEM, VMEM],
+        out_shape=(
+            block,
+            block,
+            shape((8, 1024), BF16),
+            shape((128, 1024), BF16),
+            shape((TILES, 8, 128), F32),
+        ),
+        in_specs=[VMEM] * 2,
         out_specs=(VMEM,) * 5,
-        scratch_shapes=[pltpu.VMEM((TILES, 136, 128), F32)],
+        scratch_shapes=[pltpu.VMEM((TILES, 136, 128), F32)] * 2,
         compiler_params=params(),
         name="prep",
-    )(row_shift, images[0], row_weights[0], col_weights[0])
+    )(images[0], small)
     low = lax.ppermute(up, "strip", [(i, i + 1) for i in range(15)])
     high = lax.ppermute(down, "strip", [(i + 1, i) for i in range(15)])
     warped = pl.pallas_call(
@@ -485,31 +527,31 @@
     from_3 = send(warped, lambda s, way: s + 2 * way)
     from_4 = send(from_1, lambda s, way: s - way)
     from_5 = send(from_3, lambda s, way: s + way)
-    x_wide, sum_x, root_x, slope_r, slope_c = pl.pallas_call(
+    x_wide, sum_x, root_x, slope_r, slope_c, plan = pl.pallas_call(
         own_kernel,
-        out_shape=(FIELD,) * 5,
-        in_specs=[SMEM, VMEM],
-        out_specs=(VMEM,) * 5,
+        out_shape=(FIELD,) * 5 + (shape((8, 128), F32),),
+        in_specs=[VMEM, VMEM],
+        out_specs=(VMEM,) * 6,
         scratch_shapes=[field() for _ in range(6)],
         compiler_params=params(),
         cost_estimate=cost(1.3),
         name="own",
-    )(place, warped)
+    )(small, warped)
     stats = (x_wide, sum_x, root_x)
-    sums = add_pairs((0,), place, pair_on, (from_0,), stats, ())
-    sums = add_pairs((1, 2), place, pair_on, (from_1, from_2), stats, sums)
-    sums = add_pairs((3,), place, pair_on, (from_3,), stats, sums)
+    sums = ()
+    for i, y in enumerate((from_0, from_1, from_2, from_3, from_4)):
+        sums = add_pairs((i,), plan, (y,), stats, sums)
     grad, disp = pl.pallas_call(
-        functools.partial(last_kernel, (4, 5)),
+        functools.partial(last_kernel, (5,)),
         out_shape=(shape((128, 1024), F32), shape((2, 128, 1024), F32)) + (FIELD,) * 3,
-        in_specs=[SMEM, SMEM] + [VMEM] * 10,
-        out_specs=(VMEM,) * 5,
-        scratch_shapes=[field(), field(), pltpu.VMEM((3, TILES, EXT, 128), F32)] + [field() for _ in range(6)],
-        input_output_aliases={9: 2, 10: 3, 11: 4},
+        in_specs=[VMEM] * 10,
+        out_specs=(HBM, HBM) + (VMEM,) * 3,
+        scratch_shapes=last_scratch(),
+        input_output_aliases={7: 2, 8: 3, 9: 4},
         compiler_params=params(),
         cost_estimate=cost(5),
         name="last",
-    )(place, pair_on, from_4, from_5, *stats, slope_r, slope_c, *sums)[:2]
+    )(plan, from_5, *stats, slope_r, slope_c, *sums)[:2]
     return grad[None], disp[:, None]
 
 

time: 61.6 us -> 54.7 us (0.89)
  the two profiles are of different devices: /device:TPU:110 before, /device:TPU:103 now
where the time goes in v3:
time: 54.7 us; the launch traced here: 54.3 us
  starting transfers between devices  26.2 us (48%)
  Pallas kernels  16.2 us (30%)
  waiting for transfers between devices  7.38 us (13%)
  local copies, waits for them, and re-layouts  2.39 us (4%)
  between operations  2.12 us (4%)
    ppermute x6, starting transfers between devices, send(): return lax.ppermute(value, 'sec', [p for p in pairs if 0 <= p[1] < 16])  18.7 us
    pallas_call x5, Pallas kernels, add_pairs(): pl.pallas_call(functools.partial(pair_kernel, turns), out_shape=(FIELD,)...  7.6 us
    pallas_call x1, Pallas kernels, per_device(): pl.pallas_call(functools.partial(last_kernel, (5,)), out_shape=(shape((12...  6.08 us
    ppermute x1, waiting for transfers between devices, per_device(): high = lax.ppermute(down, 'strip', [(i + 1, i) for i in range(15)])  6.04 us
    ppermute x1, starting transfers between devices, per_device(): low = lax.ppermute(up, 'strip', [(i, i + 1) for i in range(15)])  5.6 us
    unnamed x8, local copies, waits for them, and re-layouts  2.32 us
    ppermute x1, starting transfers between devices, per_device(): high = lax.ppermute(down, 'strip', [(i + 1, i) for i in range(15)])  1.92 us
    ppermute x6, waiting for transfers between devices, send(): return lax.ppermute(value, 'sec', [p for p in pairs if 0 <= p[1] < 16])  1.34 us
  transfers between devices with their start and end apart: 8, of which 2 were waited for; matrix products, arithmetic and copies ran while one was open for 0% of the time, Pallas kernels for 16%

profile of v3, /device:TPU:103, one launch (start us, length us, event | category | flops | bytes accessed | tf_op | source)
XLA Modules:
  0.0 54.3 jit_solution(12809049346190736905)
XLA Ops:
  0.6 0.0 copy-start.3
  1.3 0.0 copy-done.3
  1.3 0.0 copy-start.2
  1.3 0.7 %copy-done.2 = f32[1,4,128]{2,1,0:T(4,128)S(1)} copy-done((f32[1,4,128]{2,1,0:T(4,128)S(1)}, f32[1,4,128]{2,1,0:T(4,128)}, u32[]{:S(2)}) %copy-start.2) | copy-done | bytes 2072
  2.0 0.0 copy-start.1
  2.0 0.7 %copy-done.1 = bf16[1,4,1024]{2,1,0:T(4,128)(2,1)S(1)} copy-done((bf16[1,4,1024]{2,1,0:T(4,128)(2,1)S(1)}, bf16[1,4,1024]{2,1,0:T(4,128)(2,1)}, u32[]{:S(2)}) %copy-start.1) | copy-done | bytes 8216
  2.7 0.1 concatenate.3.small_ref.small
  2.8 0.0 copy-start
  2.8 0.9 %copy-done = bf16[1,128,1024]{2,1,0:T(8,128)(2,1)S(1)} copy-done((bf16[1,128,1024]{2,1,0:T(8,128)(2,1)S(1)}, bf16[1,128,1024]{2,1,0:T(8,128)(2,1)}, u32[]{:S(2)}) %copy-start) | copy-done | bytes 262168
  3.7 0.4 prep.1
  4.2 5.6 %collective-permute-start = (bf16[32,1024]{1,0:T(8,128)(2,1)S(1)}, bf16[32,1024]{1,0:T(8,128)(2,1)S(1)}, u32[]{:S(2)}, u32[]{:S(2)}) collective-permute-start(bf16[32,1024]{1,0:T(8,128)(2,1)S(1)} %get-tuple-element.31), channel_id=1, source_target_pairs={{0,1},{1,2},{2,3},{3,4},{4,5},{5,6},{6,7},{7,8},{8,9},{9,10},{10,1... | collective-permute-start | bytes 196616 | tf_op jit(solution)/shard_map/ppermute | solution.py:507
  9.8 1.9 %collective-permute-start.1 = (bf16[32,1024]{1,0:T(8,128)(2,1)S(1)}, bf16[32,1024]{1,0:T(8,128)(2,1)S(1)}, u32[]{:S(2)}, u32[]{:S(2)}) collective-permute-start(bf16[32,1024]{1,0:T(8,128)(2,1)S(1)} %get-tuple-element.32), channel_id=1, source_target_pairs={{1,0},{2,1},{3,2},{4,3},{5,4},{6,5},{7,6},{8,7},{9,8},{10,9},{11,1... | collective-permute-start | bytes 196616 | tf_op jit(solution)/shard_map/ppermute | solution.py:508
  12.4 0.0 collective-permute-done.low_ref
  12.4 6.0 %collective-permute-done.1.high_ref = bf16[32,1024]{1,0:T(8,128)(2,1)S(1)} collective-permute-done((bf16[32,1024]{1,0:T(8,128)(2,1)S(1)}, bf16[32,1024]{1,0:T(8,128)(2,1)S(1)}, u32[]{:S(2)}, u32[]{:S(2)}) %collective-permute-start.1) | collective-permute-done | bytes 65568 | tf_op jit(solution)/shard_map/ppermute | solution.py:508
  18.4 1.2 %warp.1.x = bf16[8,152,128]{2,1,0:T(8,128)(2,1)S(1)} custom-call(s32[1]{0:T(128)S(6)} %copy.40.shift_ref, bf16[128,1024]{1,0:T(8,128)(2,1)S(1)} %get-tuple-element.30.img_ref, bf16[32,1024]{1,0:T(8,128)(2,1)S(1)} %collective-permute-done.low_ref, bf16[32,1024]{1,0:T(8,128)(2,1)S(1)} %collective-permute-done.1.high_ref, ...), custom_call_target="tpu_custom_call" | custom-call | tf_op jit(solution)/shard_map/warp/pallas_call | solution.py:509
  19.6 3.2 %collective-permute-start.4 = (bf16[8,152,128]{2,1,0:T(8,128)(2,1)S(1)}, bf16[8,152,128]{2,1,0:T(8,128)(2,1)S(1)}, u32[]{:S(2)}, u32[]{:S(2)}) collective-permute-start(bf16[8,152,128]{2,1,0:T(8,128)(2,1)S(1)} %warp.1.x), channel_id=1, source_target_pairs={{16,48},{32,0},{48,80},{64,32},{80,112},{96,64},{112,144},{128,96}... | collective-permute-start | bytes 933896 | tf_op jit(solution)/shard_map/ppermute | solution.py:522
  22.8 4.2 %collective-permute-start.2 = (bf16[8,152,128]{2,1,0:T(8,128)(2,1)S(1)}, bf16[8,152,128]{2,1,0:T(8,128)(2,1)S(1)}, u32[]{:S(2)}, u32[]{:S(2)}) collective-permute-start(bf16[8,152,128]{2,1,0:T(8,128)(2,1)S(1)} %warp.1.x), channel_id=1, source_target_pairs={{0,32},{32,64},{48,16},{64,96},{80,48},{96,128},{112,80},{128,160}... | collective-permute-start | bytes 933896 | tf_op jit(solution)/shard_map/ppermute | solution.py:522
  27.0 1.0 %collective-permute-start.7 = (bf16[8,152,128]{2,1,0:T(8,128)(2,1)S(1)}, bf16[8,152,128]{2,1,0:T(8,128)(2,1)S(1)}, u32[]{:S(2)}, u32[]{:S(2)}) collective-permute-start(bf16[8,152,128]{2,1,0:T(8,128)(2,1)S(1)} %warp.1.x), channel_id=1, source_target_pairs={{0,16},{16,0},{32,48},{48,32},{64,80},{80,64},{96,112},{112,96},{1... | collective-permute-start | bytes 933896 | tf_op jit(solution)/shard_map/ppermute | solution.py:522
  28.0 1.3 %collective-permute-done.4.refs_0_ = bf16[8,152,128]{2,1,0:T(8,128)(2,1)S(1)} collective-permute-done((bf16[8,152,128]{2,1,0:T(8,128)(2,1)S(1)}, bf16[8,152,128]{2,1,0:T(8,128)(2,1)S(1)}, u32[]{:S(2)}, u32[]{:S(2)}) %collective-permute-start.4) | collective-permute-done | bytes 311328 | tf_op jit(solution)/shard_map/ppermute | solution.py:522
  29.3 3.8 %collective-permute-start.6 = (bf16[8,152,128]{2,1,0:T(8,128)(2,1)S(1)}, bf16[8,152,128]{2,1,0:T(8,128)(2,1)S(1)}, u32[]{:S(2)}, u32[]{:S(2)}) collective-permute-start(bf16[8,152,128]{2,1,0:T(8,128)(2,1)S(1)} %collective-permute-done.4.refs_0_), channel_id=1, source_target_pairs={{0,16},{16,0},{32,48},{48,32},{64,80},{80,64},{96,112},{112,96},{1... | collective-permute-start | bytes 933896 | tf_op jit(solution)/shard_map/ppermute | solution.py:522
  33.2 3.1 %collective-permute-start.5 = (bf16[8,152,128]{2,1,0:T(8,128)(2,1)S(1)}, bf16[8,152,128]{2,1,0:T(8,128)(2,1)S(1)}, u32[]{:S(2)}, u32[]{:S(2)}) collective-permute-start(bf16[8,152,128]{2,1,0:T(8,128)(2,1)S(1)} %collective-permute-done.4.refs_0_), channel_id=1, source_target_pairs={{16,32},{32,16},{48,64},{64,48},{80,96},{96,80},{112,128},{128,112... | collective-permute-start | bytes 933896 | tf_op jit(solution)/shard_map/ppermute | solution.py:522
  36.3 0.0 collective-permute-done.2.refs_0_
  36.3 3.3 %collective-permute-start.3 = (bf16[8,152,128]{2,1,0:T(8,128)(2,1)S(1)}, bf16[8,152,128]{2,1,0:T(8,128)(2,1)S(1)}, u32[]{:S(2)}, u32[]{:S(2)}) collective-permute-start(bf16[8,152,128]{2,1,0:T(8,128)(2,1)S(1)} %collective-permute-done.2.refs_0_), channel_id=1, source_target_pairs={{0,16},{16,0},{32,48},{48,32},{64,80},{80,64},{96,112},{112,96},{1... | collective-permute-start | bytes 933896 | tf_op jit(solution)/shard_map/ppermute | solution.py:522
  39.6 0.9 %own.1 = (f32[8,152,128]{2,1,0:T(8,128)S(1)}, f32[8,152,128]{2,1,0:T(8,128)S(1)}, f32[8,152,128]{2,1,0:T(8,128)S(1)}, f32[8,152,128]{2,1,0:T(8,128)S(1)}, f32[8,...) custom-call(f32[16,1024]{1,0:T(8,128)S(1)} %concatenate.3.small_ref.small, bf16[8,152,128]{2,1,0:T(8,128)(2,1)S(1)} %warp.1.x), custom_call_target="tpu_custom_call" | custom-call | flops 5200000 | bytes 1000000 | tf_op jit(solution)/shard_map/own/pallas_call | solution.py:530
  40.5 0.0 collective-permute-done.7.refs_0_
  40.6 1.4 %pair.5 = (f32[8,152,128]{2,1,0:T(8,128)S(1)}, f32[8,152,128]{2,1,0:T(8,128)S(1)}, f32[8,152,128]{2,1,0:T(8,128)S(1)}) custom-call(f32[8,128]{1,0:T(8,128)S(1)} %get-tuple-element.35.plan, bf16[8,152,128]{2,1,0:T(8,128)(2,1)S(1)} %collective-permute-done.7.refs_0_, f32[8,152,128]{2,1,0:T(8,128)S(1)} %get-tuple-element.36.refs_1_, ...), custom_call_target="tpu_custom_call" | custom-call | flops 6000000 | bytes 1000000 | tf_op jit(solution)/shard_map/pair/pallas_call | solution.py:464
  42.0 1.5 %pair.6 = (f32[8,152,128]{2,1,0:T(8,128)S(1)}, f32[8,152,128]{2,1,0:T(8,128)S(1)}, f32[8,152,128]{2,1,0:T(8,128)S(1)}) custom-call(f32[8,128]{1,0:T(8,128)S(1)} %get-tuple-element.35.plan, bf16[8,152,128]{2,1,0:T(8,128)(2,1)S(1)} %collective-permute-done.4.refs_0_, ...), custom_call_target="tpu_custom_call", output_to_operand_aliasing={{0}: (5, {}), {1}: (6, {}), {2}: (7, {})} | custom-call | flops 6000000 | bytes 1000000 | tf_op jit(solution)/shard_map/pair/pallas_call | solution.py:464
  43.5 0.0 collective-permute-done.6.refs_0_
  43.5 1.5 %pair.7 = (f32[8,152,128]{2,1,0:T(8,128)S(1)}, f32[8,152,128]{2,1,0:T(8,128)S(1)}, f32[8,152,128]{2,1,0:T(8,128)S(1)}) custom-call(f32[8,128]{1,0:T(8,128)S(1)} %get-tuple-element.35.plan, bf16[8,152,128]{2,1,0:T(8,128)(2,1)S(1)} %collective-permute-done.6.refs_0_, ...), custom_call_target="tpu_custom_call", output_to_operand_aliasing={{0}: (5, {}), {1}: (6, {}), {2}: (7, {})} | custom-call | flops 6000000 | bytes 1000000 | tf_op jit(solution)/shard_map/pair/pallas_call | solution.py:464
  45.1 1.5 %pair.8 = (f32[8,152,128]{2,1,0:T(8,128)S(1)}, f32[8,152,128]{2,1,0:T(8,128)S(1)}, f32[8,152,128]{2,1,0:T(8,128)S(1)}) custom-call(f32[8,128]{1,0:T(8,128)S(1)} %get-tuple-element.35.plan, bf16[8,152,128]{2,1,0:T(8,128)(2,1)S(1)} %collective-permute-done.2.refs_0_, ...), custom_call_target="tpu_custom_call", output_to_operand_aliasing={{0}: (5, {}), {1}: (6, {}), {2}: (7, {})} | custom-call | flops 6000000 | bytes 1000000 | tf_op jit(solution)/shard_map/pair/pallas_call | solution.py:464
  46.6 0.0 collective-permute-done.5.refs_0_
  46.6 1.5 %pair.9 = (f32[8,152,128]{2,1,0:T(8,128)S(1)}, f32[8,152,128]{2,1,0:T(8,128)S(1)}, f32[8,152,128]{2,1,0:T(8,128)S(1)}) custom-call(f32[8,128]{1,0:T(8,128)S(1)} %get-tuple-element.35.plan, bf16[8,152,128]{2,1,0:T(8,128)(2,1)S(1)} %collective-permute-done.5.refs_0_, ...), custom_call_target="tpu_custom_call", output_to_operand_aliasing={{0}: (5, {}), {1}: (6, {}), {2}: (7, {})} | custom-call | flops 6000000 | bytes 1000000 | tf_op jit(solution)/shard_map/pair/pallas_call | solution.py:464
  48.2 0.0 collective-permute-done.3.refs_0_
  48.2 6.1 %last.1 = (f32[128,1024]{1,0:T(8,128)}, f32[2,128,1024]{2,1,0:T(8,128)}, f32[8,152,128]{2,1,0:T(8,128)S(1)}, f32[8,152,128]{2,1,0:T(8,128)S(1)}, f32[8,152,128]{2,1,0:T(8,128)S(1)}) custom-call(f32[8,128]{1,0:T(8,128)S(1)} %get-tuple-element.35.plan, ...), custom_call_target="tpu_custom_call", output_to_operand_aliasing={{2}: (7, {}), {3}: (8, {}), {4}: (9, {})} | custom-call | flops 20000000 | bytes 1000000 | tf_op jit(solution)/shard_map/last/pallas_call | solution.py:544
  (6 shorter events, 0.0 us)
Async XLA Ops:
  0.6 0.7 %copy-start.3 = (s32[16,3]{0,1:T(4,128)S(1)}, s32[16,3]{0,1:T(4,128)}, u32[]{:S(2)}) copy-start(s32[16,3]{0,1:T(4,128)} %param.11) | copy-start | bytes 580
  1.3 0.7 %copy-start.2 = (f32[1,4,128]{2,1,0:T(4,128)S(1)}, f32[1,4,128]{2,1,0:T(4,128)}, u32[]{:S(2)}) copy-start(f32[1,4,128]{2,1,0:T(4,128)} %param.7) | copy-start | bytes 6148
  2.0 0.7 %copy-start.1 = (bf16[1,4,1024]{2,1,0:T(4,128)(2,1)S(1)}, bf16[1,4,1024]{2,1,0:T(4,128)(2,1)}, u32[]{:S(2)}) copy-start(bf16[1,4,1024]{2,1,0:T(4,128)(2,1)} %param.9) | copy-start | bytes 24580
  2.8 1.0 %copy-start = (bf16[1,128,1024]{2,1,0:T(8,128)(2,1)S(1)}, bf16[1,128,1024]{2,1,0:T(8,128)(2,1)}, u32[]{:S(2)}) copy-start(bf16[1,128,1024]{2,1,0:T(8,128)(2,1)} %param.6) | copy-start | bytes 786436
  4.2 8.2 %collective-permute-start = (bf16[32,1024]{1,0:T(8,128)(2,1)S(1)}, bf16[32,1024]{1,0:T(8,128)(2,1)S(1)}, u32[]{:S(2)}, u32[]{:S(2)}) collective-permute-start(bf16[32,1024]{1,0:T(8,128)(2,1)S(1)} %get-tuple-element.31), channel_id=1, source_target_pairs={{0,1},{1,2},{2,3},{3,4},{4,5},{5,6},{6,7},{7,8},{8,9},{9,10},{10,1... | collective-permute-start | bytes 196616 | tf_op jit(solution)/shard_map/ppermute | solution.py:507
  9.8 8.6 %collective-permute-start.1 = (bf16[32,1024]{1,0:T(8,128)(2,1)S(1)}, bf16[32,1024]{1,0:T(8,128)(2,1)S(1)}, u32[]{:S(2)}, u32[]{:S(2)}) collective-permute-start(bf16[32,1024]{1,0:T(8,128)(2,1)S(1)} %get-tuple-element.32), channel_id=1, source_target_pairs={{1,0},{2,1},{3,2},{4,3},{5,4},{6,5},{7,6},{8,7},{9,8},{10,9},{11,1... | collective-permute-start | bytes 196616 | tf_op jit(solution)/shard_map/ppermute | solution.py:508
  19.6 9.8 %collective-permute-start.4 = (bf16[8,152,128]{2,1,0:T(8,128)(2,1)S(1)}, bf16[8,152,128]{2,1,0:T(8,128)(2,1)S(1)}, u32[]{:S(2)}, u32[]{:S(2)}) collective-permute-start(bf16[8,152,128]{2,1,0:T(8,128)(2,1)S(1)} %warp.1.x), channel_id=1, source_target_pairs={{16,48},{32,0},{48,80},{64,32},{80,112},{96,64},{112,144},{128,96}... | collective-permute-start | bytes 933896 | tf_op jit(solution)/shard_map/ppermute | solution.py:522
  22.8 13.5 %collective-permute-start.2 = (bf16[8,152,128]{2,1,0:T(8,128)(2,1)S(1)}, bf16[8,152,128]{2,1,0:T(8,128)(2,1)S(1)}, u32[]{:S(2)}, u32[]{:S(2)}) collective-permute-start(bf16[8,152,128]{2,1,0:T(8,128)(2,1)S(1)} %warp.1.x), channel_id=1, source_target_pairs={{0,32},{32,64},{48,16},{64,96},{80,48},{96,128},{112,80},{128,160}... | collective-permute-start | bytes 933896 | tf_op jit(solution)/shard_map/ppermute | solution.py:522
  27.0 13.6 %collective-permute-start.7 = (bf16[8,152,128]{2,1,0:T(8,128)(2,1)S(1)}, bf16[8,152,128]{2,1,0:T(8,128)(2,1)S(1)}, u32[]{:S(2)}, u32[]{:S(2)}) collective-permute-start(bf16[8,152,128]{2,1,0:T(8,128)(2,1)S(1)} %warp.1.x), channel_id=1, source_target_pairs={{0,16},{16,0},{32,48},{48,32},{64,80},{80,64},{96,112},{112,96},{1... | collective-permute-start | bytes 933896 | tf_op jit(solution)/shard_map/ppermute | solution.py:522
  29.3 14.2 %collective-permute-start.6 = (bf16[8,152,128]{2,1,0:T(8,128)(2,1)S(1)}, bf16[8,152,128]{2,1,0:T(8,128)(2,1)S(1)}, u32[]{:S(2)}, u32[]{:S(2)}) collective-permute-start(bf16[8,152,128]{2,1,0:T(8,128)(2,1)S(1)} %collective-permute-done.4.refs_0_), channel_id=1, source_target_pairs={{0,16},{16,0},{32,48},{48,32},{64,80},{80,64},{96,112},{112,96},{1... | collective-permute-start | bytes 933896 | tf_op jit(solution)/shard_map/ppermute | solution.py:522
  33.2 13.5 %collective-permute-start.5 = (bf16[8,152,128]{2,1,0:T(8,128)(2,1)S(1)}, bf16[8,152,128]{2,1,0:T(8,128)(2,1)S(1)}, u32[]{:S(2)}, u32[]{:S(2)}) collective-permute-start(bf16[8,152,128]{2,1,0:T(8,128)(2,1)S(1)} %collective-permute-done.4.refs_0_), channel_id=1, source_target_pairs={{16,32},{32,16},{48,64},{64,48},{80,96},{96,80},{112,128},{128,112... | collective-permute-start | bytes 933896 | tf_op jit(solution)/shard_map/ppermute | solution.py:522
  36.3 11.9 %collective-permute-start.3 = (bf16[8,152,128]{2,1,0:T(8,128)(2,1)S(1)}, bf16[8,152,128]{2,1,0:T(8,128)(2,1)S(1)}, u32[]{:S(2)}, u32[]{:S(2)}) collective-permute-start(bf16[8,152,128]{2,1,0:T(8,128)(2,1)S(1)} %collective-permute-done.2.refs_0_), channel_id=1, source_target_pairs={{0,16},{16,0},{32,48},{48,32},{64,80},{80,64},{96,112},{112,96},{1... | collective-permute-start | bytes 933896 | tf_op jit(solution)/shard_map/ppermute | solution.py:522

commit v4 on v3

--- a/solution.py
+++ b/solution.py
@@ -154,52 +154,105 @@
     lax.fori_loop(0, blocks // each, step, 0)
 
 
-def prep_kernel(img_ref, small_ref, up_ref, down_ref, own_ref, img_out, taps_out, work, other):
-    shift = small_ref[8:9, 0:128]
+def to_blocked(work, other, blocks):
+    exchange_stage(work, other, [()], 0, blocks, 0, blocks)
+    exchange_stage(other, work, [()], 1, blocks, 0, blocks)
+    exchange_stage(work, other, [()], 2, blocks, 0, blocks)
+
+
+def grouped_lanes():
     lane = lax.broadcasted_iota(jnp.int32, (8, 128), 1)
+    return 8 * (lane % 16) + lane // 16
+
+
+def table_rows(line, shift, tap):
     row = lax.broadcasted_iota(jnp.int32, (8, 128), 0)
+    hi, mid, lo = split3(pltpu.roll(line, HALO, 1))
     zero = jnp.zeros((8, 128), F32)
-    pick = 8 * (lane % 16) + lane // 16
+    full = jnp.where(row == 0, hi, jnp.where(row == 1, mid, jnp.where(row == 2, lo, zero)))
+    if tap == 0:
+        full = jnp.where(row == 3, shift, full)
+    return full
+
+
+def halo_kernel(shift_ref, img_hbm, weights_hbm, first_ref, second_ref, edge, weights, work, other, sems):
+    moves = [
+        pltpu.make_async_copy(img_hbm.at[0, pl.ds(0, EDGE)], edge.at[0], sems.at[0]),
+        pltpu.make_async_copy(img_hbm.at[0, pl.ds(128 - EDGE, EDGE)], edge.at[1], sems.at[1]),
+        pltpu.make_async_copy(weights_hbm.at[0], weights, sems.at[2]),
+    ]
+    for move in moves:
+        move.start()
+    for move in moves:
+        move.wait()
+    pick = grouped_lanes()
+    for j in range(TILES):
+        for side in range(2):
+            tile = edge[side, :, 128 * j : 128 * j + 128].astype(F32)
+            for b in range(3):
+                work[j, 24 * side + 8 * b : 24 * side + 8 * b + 8, :] = jnp.take_along_axis(
+                    tile[8 * b : 8 * b + 8], pick, axis=1
+                )
+    to_blocked(work, other, 6)
+    lane = lax.broadcasted_iota(jnp.int32, (8, 128), 1)
+    zero = jnp.zeros((8, 128), F32)
+    shift = jnp.broadcast_to(shift_ref[0:1, :], (8, 128))
+    even = lax.axis_index("strip") % 2 == 0
+
+    def fill(up_ref, down_ref):
+        for m in range(TILES):
+            cols = slice(128 * m, 128 * m + 128)
+            down_ref[0:EDGE, cols] = other[m, 0:EDGE, :].astype(BF16)
+            up_ref[0:EDGE, cols] = other[m, EDGE : 2 * EDGE, :].astype(BF16)
+        for tap in range(TAPS):
+            line = jnp.broadcast_to(weights[tap : tap + 1, :], (8, 128))
+            full = table_rows(line, shift, tap)
+            at = 256 * tap
+            up_ref[EDGE:BLOCK, at : at + 128] = jnp.where(lane < HALO, full, zero).astype(BF16)
+            up_ref[EDGE:BLOCK, at + 128 : at + 256] = zero.astype(BF16)
+            down_ref[EDGE:BLOCK, at : at + 128] = zero.astype(BF16)
+            down_ref[EDGE:BLOCK, at + 128 : at + 256] = jnp.where(
+                (lane >= HALO) & (lane < 2 * HALO), full, zero
+            ).astype(BF16)
+
+    @pl.when(even)
+    def _():
+        fill(first_ref, second_ref)
+
+    @pl.when(jnp.logical_not(even))
+    def _():
+        fill(second_ref, first_ref)
+
+
+def prep_kernel(img_ref, small_ref, own_ref, img_out, taps_out, work, other):
+    shift = jnp.broadcast_to(small_ref[8:9, 0:128], (8, 128))
+    lane = lax.broadcasted_iota(jnp.int32, (8, 128), 1)
+    zero = jnp.zeros((8, 128), F32)
+    pick = grouped_lanes()
     for j in range(TILES):
         cols = slice(128 * j, 128 * j + 128)
         tile = img_ref[:, cols].astype(F32)
         for b in range(16):
             work[j, 8 * b : 8 * b + 8, :] = jnp.take_along_axis(tile[8 * b : 8 * b + 8], pick, axis=1)
         work[j, 128:136, :] = jnp.take_along_axis(small_ref[0:8, cols], pick, axis=1)
-    exchange_stage(work, other, [()], 0, 17, 0, 17)
-    exchange_stage(other, work, [()], 1, 17, 0, 17)
-    exchange_stage(work, other, [()], 2, 17, 0, 17)
+    to_blocked(work, other, 17)
     for m in range(TILES):
-        cols = slice(128 * m, 128 * m + 128)
-        tile = other[m, 0:128, :].astype(BF16)
-        img_out[:, cols] = tile
-        up_ref[0:EDGE, cols] = tile[128 - EDGE :]
-        down_ref[0:EDGE, cols] = tile[:EDGE]
+        img_out[:, 128 * m : 128 * m + 128] = other[m, 0:128, :].astype(BF16)
         taps_out[m] = other[m, 128:136, :]
     for tap in range(TAPS):
         line = jnp.broadcast_to(small_ref[4 + tap : 5 + tap, 0:128], (8, 128))
-        hi, mid, lo = split3(pltpu.roll(line, HALO, 1))
-        full = jnp.where(row == 0, hi, jnp.where(row == 1, mid, jnp.where(row == 2, lo, zero)))
-        if tap == 0:
-            full = jnp.where(row == 3, jnp.broadcast_to(shift, (8, 128)), full)
+        full = table_rows(line, shift, tap)
         at = 256 * tap
-        wrapped = jnp.where(lane < HALO, full, zero).astype(BF16)
         own_ref[:, at : at + 128] = jnp.where(lane >= HALO, full, zero).astype(BF16)
-        own_ref[:, at + 128 : at + 256] = wrapped
-        up_ref[EDGE:BLOCK, at : at + 128] = wrapped
-        up_ref[EDGE:BLOCK, at + 128 : at + 256] = zero.astype(BF16)
-        down_ref[EDGE:BLOCK, at : at + 128] = zero.astype(BF16)
-        down_ref[EDGE:BLOCK, at + 128 : at + 256] = jnp.where(
-            (lane >= HALO) & (lane < 2 * HALO), full, zero
-        ).astype(BF16)
-
-
-def warp_kernel(shift_ref, img_ref, low_ref, high_ref, own_ref, taps_ref, out_ref, row_warped, virtual):
-    meta = (
-        low_ref[EDGE:BLOCK, :].astype(F32)
-        + own_ref[...].astype(F32)
-        + high_ref[EDGE:BLOCK, :].astype(F32)
-    ).astype(BF16)
+        own_ref[:, at + 128 : at + 256] = jnp.where(lane < HALO, full, zero).astype(BF16)
+
+
+def warp_kernel(shift_ref, img_ref, first_ref, second_ref, own_ref, taps_ref, out_ref, row_warped, virtual):
+    even = lax.axis_index("strip") % 2 == 0
+    first, second = first_ref[...], second_ref[...]
+    low = jnp.where(even, second, first)
+    high = jnp.where(even, first, second)
+    meta = (first[EDGE:].astype(F32) + own_ref[...].astype(F32) + second[EDGE:].astype(F32)).astype(BF16)
     place = lax.broadcasted_iota(jnp.int32, (EXT, 256), 0)
     rho = (place % 8) * STEPS + place // 8
     spread = jnp.where(
@@ -226,7 +279,7 @@
         weight = columns[tap][:, 0:1] + columns[tap][:, 1:2] + columns[tap][:, 2:3]
         value = jnp.where(offset == float(tap), weight, value)
     hi, mid, lo = split3(value)
-    source = jnp.concatenate([low_ref[...], img_ref[...], high_ref[...]], axis=0)
+    source = jnp.concatenate([low, img_ref[...], high], axis=0)
     total = jnp.zeros((EXT, 1024), F32)
     for piece in (lo, mid, hi):
         total = total + jnp.dot(piece.astype(BF16), source, preferred_element_type=F32)
@@ -489,23 +542,39 @@
             jnp.zeros((4, 1024), F32),
         ]
     )
-    up, down, own, image, taps = pl.pallas_call(
+    halo = pl.pallas_call(
+        halo_kernel,
+        out_shape=(block, block),
+        in_specs=[VMEM, HBM, HBM],
+        out_specs=(VMEM,) * 2,
+        scratch_shapes=[
+            pltpu.VMEM((2, EDGE, 1024), BF16),
+            pltpu.VMEM((TAPS, 128), F32),
+            pltpu.VMEM((TILES, 48, 128), F32),
+            pltpu.VMEM((TILES, 48, 128), F32),
+            pltpu.SemaphoreType.DMA((3,)),
+        ],
+        compiler_params=pltpu.CompilerParams(vmem_limit_bytes=66_500_000),
+        name="halo",
+    )(jnp.broadcast_to(row_shift.astype(F32), (8, 128)), images, row_weights)
+    strips = range(16)
+
+    def swap(value, step):
+        pairs = [(s, s + step * (1 - 2 * (s % 2))) for s in strips]
+        return lax.ppermute(value, "strip", [p for p in pairs if 0 <= p[1] < 16])
+
+    first = swap(halo[0], 1)
+    second = swap(halo[1], -1)
+    own, image, taps = pl.pallas_call(
         prep_kernel,
-        out_shape=(
-            block,
-            block,
-            shape((8, 1024), BF16),
-            shape((128, 1024), BF16),
-            shape((TILES, 8, 128), F32),
-        ),
+        out_shape=(shape((8, 1024), BF16), shape((128, 1024), BF16), shape((TILES, 8, 128), F32)),
         in_specs=[VMEM] * 2,
-        out_specs=(VMEM,) * 5,
+        out_specs=(VMEM,) * 3,
         scratch_shapes=[pltpu.VMEM((TILES, 136, 128), F32)] * 2,
         compiler_params=params(),
+        cost_estimate=cost(1),
         name="prep",
     )(images[0], small)
-    low = lax.ppermute(up, "strip", [(i, i + 1) for i in range(15)])
-    high = lax.ppermute(down, "strip", [(i + 1, i) for i in range(15)])
     warped = pl.pallas_call(
         warp_kernel,
         out_shape=shape((TILES, EXT, 128), BF16),
@@ -514,7 +583,7 @@
         scratch_shapes=[field(), pltpu.VMEM((TILES + TAPS - 1, EXT, 128), F32)],
         compiler_params=params(),
         name="warp",
-    )(col_shift, image, low, high, own, taps)
+    )(col_shift, image, first, second, own, taps)
     sections = range(16)
 
     def send(value, target):

time: 54.7 us -> 53.7 us (0.982)
  the two profiles are of different devices: /device:TPU:103 before, /device:TPU:131 now
where the time goes in v4:
time: 53.7 us; the launch traced here: 53.3 us
  starting transfers between devices  26.5 us (49%)
  Pallas kernels  18.8 us (35%)
  waiting for transfers between devices  4.34 us (8%)
  between operations  2.33 us (4%)
  local copies, waits for them, and re-layouts  1.34 us (2%)
    ppermute x6, starting transfers between devices, send(): return lax.ppermute(value, 'sec', [p for p in pairs if 0 <= p[1] < 16])  21.8 us
    pallas_call x5, Pallas kernels, add_pairs(): pl.pallas_call(functools.partial(pair_kernel, turns), out_shape=(FIELD,)...  7.6 us
    pallas_call x1, Pallas kernels, per_device(): pl.pallas_call(functools.partial(last_kernel, (5,)), out_shape=(shape((12...  6.08 us
    ppermute x2, starting transfers between devices, swap(): return lax.ppermute(value, 'strip', [p for p in pairs if 0 <= p[1] < 16])  4.63 us
    ppermute x2, waiting for transfers between devices, swap(): return lax.ppermute(value, 'strip', [p for p in pairs if 0 <= p[1] < 16])  4.32 us
    pallas_call x1, Pallas kernels, per_device(): pl.pallas_call(halo_kernel, out_shape=(block, block), in_specs=[VMEM, HBM...  2.63 us
    pallas_call x1, Pallas kernels, per_device(): pl.pallas_call(warp_kernel, out_shape=shape((TILES, EXT, 128), BF16), in_...  1.16 us
  transfers between devices with their start and end apart: 8, of which 1 were waited for; matrix products, arithmetic and copies ran while one was open for 0% of the time, Pallas kernels for 17%

profile of v4, /device:TPU:131, one launch (start us, length us, event | category | flops | bytes accessed | tf_op | source)
XLA Modules:
  0.0 53.3 jit_solution(2938544757277563586)
XLA Ops:
  0.6 0.0 copy-start
  1.3 0.6 %broadcast_in_dim.24.shift_ref = f32[8,128]{1,0:T(8,128)} broadcast(f32[]{:T(128)} %bitcast.2), dimensions={} | broadcast | bytes 4100 | tf_op jit(solution)/shard_map/broadcast_in_dim | solution.py:559
  1.9 0.0 copy-start.2
  1.9 2.6 %halo.1 = (bf16[32,1024]{1,0:T(8,128)(2,1)}, bf16[32,1024]{1,0:T(8,128)(2,1)}) custom-call(f32[8,128]{1,0:T(8,128)} %broadcast_in_dim.24.shift_ref, bf16[1,128,1024]{2,1,0:T(8,128)(2,1)} %img_hbm.1, f32[1,4,128]{2,1,0:T(4,128)} %weights_hbm.1), custom_call_target="tpu_custom_call" | custom-call | tf_op jit(solution)/shard_map/halo/pallas_call | solution.py:545
  4.6 1.9 %collective-permute-start = (bf16[32,1024]{1,0:T(8,128)(2,1)}, bf16[32,1024]{1,0:T(8,128)(2,1)S(1)}, u32[]{:S(2)}, u32[]{:S(2)}) collective-permute-start(bf16[32,1024]{1,0:T(8,128)(2,1)} %get-tuple-element.31), channel_id=1, source_target_pairs={{0,1},{1,0},{2,3},{3,2},{4,5},{5,4},{6,7},{7,6},{8,9},{9,8},{10,11... | collective-permute-start | bytes 196616 | tf_op jit(solution)/shard_map/ppermute | solution.py:564
  6.5 0.0 copy-start.3
  6.5 2.7 %collective-permute-start.1 = (bf16[32,1024]{1,0:T(8,128)(2,1)}, bf16[32,1024]{1,0:T(8,128)(2,1)S(1)}, u32[]{:S(2)}, u32[]{:S(2)}) collective-permute-start(bf16[32,1024]{1,0:T(8,128)(2,1)} %get-tuple-element.32), channel_id=1, source_target_pairs={{1,2},{2,1},{3,4},{4,3},{5,6},{6,5},{7,8},{8,7},{9,10},{10,9},{11,... | collective-permute-start | bytes 196616 | tf_op jit(solution)/shard_map/ppermute | solution.py:564
  9.2 0.0 copy-done.2
  9.2 0.0 copy-done.3
  9.9 0.0 copy-start.1
  9.9 0.7 %copy-done.1 = f32[1,4,128]{2,1,0:T(4,128)S(1)} copy-done((f32[1,4,128]{2,1,0:T(4,128)S(1)}, f32[1,4,128]{2,1,0:T(4,128)}, u32[]{:S(2)}) %copy-start.1) | copy-done | bytes 2072
  10.6 0.1 concatenate.3.small_ref.small
  10.7 0.0 copy-done
  10.7 0.4 prep.1
  11.1 0.0 collective-permute-done.first_ref
  11.1 4.3 %collective-permute-done.1.second_ref = bf16[32,1024]{1,0:T(8,128)(2,1)S(1)} collective-permute-done((bf16[32,1024]{1,0:T(8,128)(2,1)}, bf16[32,1024]{1,0:T(8,128)(2,1)S(1)}, u32[]{:S(2)}, u32[]{:S(2)}) %collective-permute-start.1) | collective-permute-done | bytes 65568 | tf_op jit(solution)/shard_map/ppermute | solution.py:564
  15.4 1.2 %warp.1.x = bf16[8,152,128]{2,1,0:T(8,128)(2,1)S(1)} custom-call(s32[1]{0:T(128)S(6)} %copy.40.shift_ref, bf16[128,1024]{1,0:T(8,128)(2,1)S(1)} %get-tuple-element.30.img_ref, bf16[32,1024]{1,0:T(8,128)(2,1)S(1)} %collective-permute-done.first_ref, bf16[32,1024]{1,0:T(8,128)(2,1)S(1)} %collective-permute-done.1.second_ref, ...), custom_call_target="tpu_custom_call" | custom-call | tf_op jit(solution)/shard_map/warp/pallas_call | solution.py:578
  16.6 3.2 %collective-permute-start.4 = (bf16[8,152,128]{2,1,0:T(8,128)(2,1)S(1)}, bf16[8,152,128]{2,1,0:T(8,128)(2,1)S(1)}, u32[]{:S(2)}, u32[]{:S(2)}) collective-permute-start(bf16[8,152,128]{2,1,0:T(8,128)(2,1)S(1)} %warp.1.x), channel_id=1, source_target_pairs={{16,48},{32,0},{48,80},{64,32},{80,112},{96,64},{112,144},{128,96}... | collective-permute-start | bytes 933896 | tf_op jit(solution)/shard_map/ppermute | solution.py:591
  19.8 4.2 %collective-permute-start.2 = (bf16[8,152,128]{2,1,0:T(8,128)(2,1)S(1)}, bf16[8,152,128]{2,1,0:T(8,128)(2,1)S(1)}, u32[]{:S(2)}, u32[]{:S(2)}) collective-permute-start(bf16[8,152,128]{2,1,0:T(8,128)(2,1)S(1)} %warp.1.x), channel_id=1, source_target_pairs={{0,32},{32,64},{48,16},{64,96},{80,48},{96,128},{112,80},{128,160}... | collective-permute-start | bytes 933896 | tf_op jit(solution)/shard_map/ppermute | solution.py:591
  24.1 2.5 %collective-permute-start.7 = (bf16[8,152,128]{2,1,0:T(8,128)(2,1)S(1)}, bf16[8,152,128]{2,1,0:T(8,128)(2,1)S(1)}, u32[]{:S(2)}, u32[]{:S(2)}) collective-permute-start(bf16[8,152,128]{2,1,0:T(8,128)(2,1)S(1)} %warp.1.x), channel_id=1, source_target_pairs={{0,16},{16,0},{32,48},{48,32},{64,80},{80,64},{96,112},{112,96},{1... | collective-permute-start | bytes 933896 | tf_op jit(solution)/shard_map/ppermute | solution.py:591
  26.5 0.0 collective-permute-done.4.refs_0_
  26.5 5.1 %collective-permute-start.6 = (bf16[8,152,128]{2,1,0:T(8,128)(2,1)S(1)}, bf16[8,152,128]{2,1,0:T(8,128)(2,1)S(1)}, u32[]{:S(2)}, u32[]{:S(2)}) collective-permute-start(bf16[8,152,128]{2,1,0:T(8,128)(2,1)S(1)} %collective-permute-done.4.refs_0_), channel_id=1, source_target_pairs={{0,16},{16,0},{32,48},{48,32},{64,80},{80,64},{96,112},{112,96},{1... | collective-permute-start | bytes 933896 | tf_op jit(solution)/shard_map/ppermute | solution.py:591
  31.6 1.9 %collective-permute-start.5 = (bf16[8,152,128]{2,1,0:T(8,128)(2,1)S(1)}, bf16[8,152,128]{2,1,0:T(8,128)(2,1)S(1)}, u32[]{:S(2)}, u32[]{:S(2)}) collective-permute-start(bf16[8,152,128]{2,1,0:T(8,128)(2,1)S(1)} %collective-permute-done.4.refs_0_), channel_id=1, source_target_pairs={{16,32},{32,16},{48,64},{64,48},{80,96},{96,80},{112,128},{128,112... | collective-permute-start | bytes 933896 | tf_op jit(solution)/shard_map/ppermute | solution.py:591
  33.5 0.0 collective-permute-done.2.refs_0_
  33.5 5.0 %collective-permute-start.3 = (bf16[8,152,128]{2,1,0:T(8,128)(2,1)S(1)}, bf16[8,152,128]{2,1,0:T(8,128)(2,1)S(1)}, u32[]{:S(2)}, u32[]{:S(2)}) collective-permute-start(bf16[8,152,128]{2,1,0:T(8,128)(2,1)S(1)} %collective-permute-done.2.refs_0_), channel_id=1, source_target_pairs={{0,16},{16,0},{32,48},{48,32},{64,80},{80,64},{96,112},{112,96},{1... | collective-permute-start | bytes 933896 | tf_op jit(solution)/shard_map/ppermute | solution.py:591
  38.5 0.9 %own.1 = (f32[8,152,128]{2,1,0:T(8,128)S(1)}, f32[8,152,128]{2,1,0:T(8,128)S(1)}, f32[8,152,128]{2,1,0:T(8,128)S(1)}, f32[8,152,128]{2,1,0:T(8,128)S(1)}, f32[8,...) custom-call(f32[16,1024]{1,0:T(8,128)S(1)} %concatenate.3.small_ref.small, bf16[8,152,128]{2,1,0:T(8,128)(2,1)S(1)} %warp.1.x), custom_call_target="tpu_custom_call" | custom-call | flops 5200000 | bytes 1000000 | tf_op jit(solution)/shard_map/own/pallas_call | solution.py:599
  39.4 0.0 collective-permute-done.7.refs_0_
  39.5 1.4 %pair.5 = (f32[8,152,128]{2,1,0:T(8,128)S(1)}, f32[8,152,128]{2,1,0:T(8,128)S(1)}, f32[8,152,128]{2,1,0:T(8,128)S(1)}) custom-call(f32[8,128]{1,0:T(8,128)S(1)} %get-tuple-element.35.plan, bf16[8,152,128]{2,1,0:T(8,128)(2,1)S(1)} %collective-permute-done.7.refs_0_, f32[8,152,128]{2,1,0:T(8,128)S(1)} %get-tuple-element.36.refs_1_, ...), custom_call_target="tpu_custom_call" | custom-call | flops 6000000 | bytes 1000000 | tf_op jit(solution)/shard_map/pair/pallas_call | solution.py:517
  40.9 1.5 %pair.6 = (f32[8,152,128]{2,1,0:T(8,128)S(1)}, f32[8,152,128]{2,1,0:T(8,128)S(1)}, f32[8,152,128]{2,1,0:T(8,128)S(1)}) custom-call(f32[8,128]{1,0:T(8,128)S(1)} %get-tuple-element.35.plan, bf16[8,152,128]{2,1,0:T(8,128)(2,1)S(1)} %collective-permute-done.4.refs_0_, ...), custom_call_target="tpu_custom_call", output_to_operand_aliasing={{0}: (5, {}), {1}: (6, {}), {2}: (7, {})} | custom-call | flops 6000000 | bytes 1000000 | tf_op jit(solution)/shard_map/pair/pallas_call | solution.py:517
  42.4 0.0 collective-permute-done.6.refs_0_
  42.4 1.5 %pair.7 = (f32[8,152,128]{2,1,0:T(8,128)S(1)}, f32[8,152,128]{2,1,0:T(8,128)S(1)}, f32[8,152,128]{2,1,0:T(8,128)S(1)}) custom-call(f32[8,128]{1,0:T(8,128)S(1)} %get-tuple-element.35.plan, bf16[8,152,128]{2,1,0:T(8,128)(2,1)S(1)} %collective-permute-done.6.refs_0_, ...), custom_call_target="tpu_custom_call", output_to_operand_aliasing={{0}: (5, {}), {1}: (6, {}), {2}: (7, {})} | custom-call | flops 6000000 | bytes 1000000 | tf_op jit(solution)/shard_map/pair/pallas_call | solution.py:517
  44.0 1.5 %pair.8 = (f32[8,152,128]{2,1,0:T(8,128)S(1)}, f32[8,152,128]{2,1,0:T(8,128)S(1)}, f32[8,152,128]{2,1,0:T(8,128)S(1)}) custom-call(f32[8,128]{1,0:T(8,128)S(1)} %get-tuple-element.35.plan, bf16[8,152,128]{2,1,0:T(8,128)(2,1)S(1)} %collective-permute-done.2.refs_0_, ...), custom_call_target="tpu_custom_call", output_to_operand_aliasing={{0}: (5, {}), {1}: (6, {}), {2}: (7, {})} | custom-call | flops 6000000 | bytes 1000000 | tf_op jit(solution)/shard_map/pair/pallas_call | solution.py:517
  45.5 0.0 collective-permute-done.5.refs_0_
  45.6 1.5 %pair.9 = (f32[8,152,128]{2,1,0:T(8,128)S(1)}, f32[8,152,128]{2,1,0:T(8,128)S(1)}, f32[8,152,128]{2,1,0:T(8,128)S(1)}) custom-call(f32[8,128]{1,0:T(8,128)S(1)} %get-tuple-element.35.plan, bf16[8,152,128]{2,1,0:T(8,128)(2,1)S(1)} %collective-permute-done.5.refs_0_, ...), custom_call_target="tpu_custom_call", output_to_operand_aliasing={{0}: (5, {}), {1}: (6, {}), {2}: (7, {})} | custom-call | flops 6000000 | bytes 1000000 | tf_op jit(solution)/shard_map/pair/pallas_call | solution.py:517
  47.1 0.0 collective-permute-done.3.refs_0_
  47.1 6.1 %last.1 = (f32[128,1024]{1,0:T(8,128)}, f32[2,128,1024]{2,1,0:T(8,128)}, f32[8,152,128]{2,1,0:T(8,128)S(1)}, f32[8,152,128]{2,1,0:T(8,128)S(1)}, f32[8,152,128]{2,1,0:T(8,128)S(1)}) custom-call(f32[8,128]{1,0:T(8,128)S(1)} %get-tuple-element.35.plan, ...), custom_call_target="tpu_custom_call", output_to_operand_aliasing={{2}: (7, {}), {3}: (8, {}), {4}: (9, {})} | custom-call | flops 20000000 | bytes 1000000 | tf_op jit(solution)/shard_map/last/pallas_call | solution.py:613
  (6 shorter events, 0.0 us)
Async XLA Ops:
  0.6 10.0 %copy-start = (bf16[1,128,1024]{2,1,0:T(8,128)(2,1)S(1)}, bf16[1,128,1024]{2,1,0:T(8,128)(2,1)}, u32[]{:S(2)}) copy-start(bf16[1,128,1024]{2,1,0:T(8,128)(2,1)} %img_hbm.1) | copy-start | bytes 786436
  1.9 7.3 %copy-start.2 = (bf16[1,4,1024]{2,1,0:T(4,128)(2,1)S(1)}, bf16[1,4,1024]{2,1,0:T(4,128)(2,1)}, u32[]{:S(2)}) copy-start(bf16[1,4,1024]{2,1,0:T(4,128)(2,1)} %param.9) | copy-start | bytes 24580
  4.6 6.6 %collective-permute-start = (bf16[32,1024]{1,0:T(8,128)(2,1)}, bf16[32,1024]{1,0:T(8,128)(2,1)S(1)}, u32[]{:S(2)}, u32[]{:S(2)}) collective-permute-start(bf16[32,1024]{1,0:T(8,128)(2,1)} %get-tuple-element.31), channel_id=1, source_target_pairs={{0,1},{1,0},{2,3},{3,2},{4,5},{5,4},{6,7},{7,6},{8,9},{9,8},{10,11... | collective-permute-start | bytes 196616 | tf_op jit(solution)/shard_map/ppermute | solution.py:564
  6.5 2.7 %copy-start.3 = (s32[16,3]{0,1:T(4,128)S(1)}, s32[16,3]{0,1:T(4,128)}, u32[]{:S(2)}) copy-start(s32[16,3]{0,1:T(4,128)} %param.11) | copy-start | bytes 580
  6.5 9.0 %collective-permute-start.1 = (bf16[32,1024]{1,0:T(8,128)(2,1)}, bf16[32,1024]{1,0:T(8,128)(2,1)S(1)}, u32[]{:S(2)}, u32[]{:S(2)}) collective-permute-start(bf16[32,1024]{1,0:T(8,128)(2,1)} %get-tuple-element.32), channel_id=1, source_target_pairs={{1,2},{2,1},{3,4},{4,3},{5,6},{6,5},{7,8},{8,7},{9,10},{10,9},{11,... | collective-permute-start | bytes 196616 | tf_op jit(solution)/shard_map/ppermute | solution.py:564
  9.9 0.7 %copy-start.1 = (f32[1,4,128]{2,1,0:T(4,128)S(1)}, f32[1,4,128]{2,1,0:T(4,128)}, u32[]{:S(2)}) copy-start(f32[1,4,128]{2,1,0:T(4,128)} %weights_hbm.1) | copy-start | bytes 6148
  16.6 9.9 %collective-permute-start.4 = (bf16[8,152,128]{2,1,0:T(8,128)(2,1)S(1)}, bf16[8,152,128]{2,1,0:T(8,128)(2,1)S(1)}, u32[]{:S(2)}, u32[]{:S(2)}) collective-permute-start(bf16[8,152,128]{2,1,0:T(8,128)(2,1)S(1)} %warp.1.x), channel_id=1, source_target_pairs={{16,48},{32,0},{48,80},{64,32},{80,112},{96,64},{112,144},{128,96}... | collective-permute-start | bytes 933896 | tf_op jit(solution)/shard_map/ppermute | solution.py:591
  19.8 13.7 %collective-permute-start.2 = (bf16[8,152,128]{2,1,0:T(8,128)(2,1)S(1)}, bf16[8,152,128]{2,1,0:T(8,128)(2,1)S(1)}, u32[]{:S(2)}, u32[]{:S(2)}) collective-permute-start(bf16[8,152,128]{2,1,0:T(8,128)(2,1)S(1)} %warp.1.x), channel_id=1, source_target_pairs={{0,32},{32,64},{48,16},{64,96},{80,48},{96,128},{112,80},{128,160}... | collective-permute-start | bytes 933896 | tf_op jit(solution)/shard_map/ppermute | solution.py:591
  24.1 15.4 %collective-permute-start.7 = (bf16[8,152,128]{2,1,0:T(8,128)(2,1)S(1)}, bf16[8,152,128]{2,1,0:T(8,128)(2,1)S(1)}, u32[]{:S(2)}, u32[]{:S(2)}) collective-permute-start(bf16[8,152,128]{2,1,0:T(8,128)(2,1)S(1)} %warp.1.x), channel_id=1, source_target_pairs={{0,16},{16,0},{32,48},{48,32},{64,80},{80,64},{96,112},{112,96},{1... | collective-permute-start | bytes 933896 | tf_op jit(solution)/shard_map/ppermute | solution.py:591
  26.5 15.9 %collective-permute-start.6 = (bf16[8,152,128]{2,1,0:T(8,128)(2,1)S(1)}, bf16[8,152,128]{2,1,0:T(8,128)(2,1)S(1)}, u32[]{:S(2)}, u32[]{:S(2)}) collective-permute-start(bf16[8,152,128]{2,1,0:T(8,128)(2,1)S(1)} %collective-permute-done.4.refs_0_), channel_id=1, source_target_pairs={{0,16},{16,0},{32,48},{48,32},{64,80},{80,64},{96,112},{112,96},{1... | collective-permute-start | bytes 933896 | tf_op jit(solution)/shard_map/ppermute | solution.py:591
  31.6 13.9 %collective-permute-start.5 = (bf16[8,152,128]{2,1,0:T(8,128)(2,1)S(1)}, bf16[8,152,128]{2,1,0:T(8,128)(2,1)S(1)}, u32[]{:S(2)}, u32[]{:S(2)}) collective-permute-start(bf16[8,152,128]{2,1,0:T(8,128)(2,1)S(1)} %collective-permute-done.4.refs_0_), channel_id=1, source_target_pairs={{16,32},{32,16},{48,64},{64,48},{80,96},{96,80},{112,128},{128,112... | collective-permute-start | bytes 933896 | tf_op jit(solution)/shard_map/ppermute | solution.py:591
  33.5 13.6 %collective-permute-start.3 = (bf16[8,152,128]{2,1,0:T(8,128)(2,1)S(1)}, bf16[8,152,128]{2,1,0:T(8,128)(2,1)S(1)}, u32[]{:S(2)}, u32[]{:S(2)}) collective-permute-start(bf16[8,152,128]{2,1,0:T(8,128)(2,1)S(1)} %collective-permute-done.2.refs_0_), channel_id=1, source_target_pairs={{0,16},{16,0},{32,48},{48,32},{64,80},{80,64},{96,112},{112,96},{1... | collective-permute-start | bytes 933896 | tf_op jit(solution)/shard_map/ppermute | solution.py:591

commit v5 on v4

--- a/solution.py
+++ b/solution.py
@@ -23,7 +23,6 @@
 EDGE = 24
 UNROLL = 3
 GROUP = 8
-EACH = 16
 BLOCK = 32
 
 
@@ -196,7 +195,7 @@
     to_blocked(work, other, 6)
     lane = lax.broadcasted_iota(jnp.int32, (8, 128), 1)
     zero = jnp.zeros((8, 128), F32)
-    shift = jnp.broadcast_to(shift_ref[0:1, :], (8, 128))
+    shift = jnp.full((8, 128), shift_ref[0, 0], jnp.int32).astype(F32)
     even = lax.axis_index("strip") % 2 == 0
 
     def fill(up_ref, down_ref):
@@ -224,7 +223,8 @@
         fill(second_ref, first_ref)
 
 
-def prep_kernel(img_ref, small_ref, own_ref, img_out, taps_out, work, other):
+def prep_kernel(img_ref, small_ref, own_ref, img_out, taps_out, order, work, other):
+    order[...] = column_order()
     shift = jnp.broadcast_to(small_ref[8:9, 0:128], (8, 128))
     lane = lax.broadcasted_iota(jnp.int32, (8, 128), 1)
     zero = jnp.zeros((8, 128), F32)
@@ -336,8 +336,12 @@
     def rows(m, turn):
         value = y_ref[m].astype(F32)
         y_wide[m] = value
-        put_box(boxes[0], m, turn, steps_of(value))
-        put_box(boxes[1], m, turn, steps_of(value * value))
+        steps = steps_of(value)
+        turned = [turn(v) for v in steps]
+        put_rows(boxes[0][0], m, row_window(steps))
+        put_rows(boxes[1][0], m, row_window([v * v for v in steps]))
+        put_rows(boxes[0][1], m, row_window(turned))
+        put_rows(boxes[1][1], m, row_window([v * v for v in turned]))
         put_box(boxes[2], m, turn, steps_of(value * x_wide[m]))
 
     over_tiles(rows)
@@ -375,28 +379,33 @@
     over_steps(cols_2)
 
 
-def restore(natural, other, which, target):
-    lead = [(w,) for w in which]
-    exchange_stage(natural, other, lead, 0, 16, HALO, EACH // len(which))
-    exchange_stage(other, natural, lead, 1, 16, HALO, EACH // len(which))
-    exchange_stage(natural, other, lead, 2, 16, HALO, EACH // len(which))
-    lane = lax.broadcasted_iota(jnp.int32, (8, 128), 1)
-    pick = (lane % 8) * 16 + lane // 8
-    each = EACH // len(which)
-
-    def step(s, carry):
-        for e in range(each):
-            at = pl.multiple_of(8 * (each * s + e), 8)
-            for w in which:
-                for j in range(TILES):
-                    tile = jnp.take_along_axis(other[w, j, pl.ds(at + HALO, 8), :], pick, axis=1)
-                    target[w, pl.ds(at, 8), 128 * j : 128 * j + 128] = tile
-        return carry
-
-    lax.fori_loop(0, 16 // each, step, 0)
-
-
-def finish(x_wide, sum_x, root_x, slope_r, slope_c, sum_g, sum_h, sum_t, natural, other, wide, sems, grad_hbm, disp_hbm, boxes):
+def column_order():
+    source = lax.broadcasted_iota(jnp.int32, (512, 512), 0)
+    column = lax.broadcasted_iota(jnp.int32, (512, 512), 1)
+    tile = 4 * ((source // 64) % 2) + source // 128
+    return jnp.where(8 * (source % 64) + tile == column, 1.0, 0.0).astype(BF16)
+
+
+def restore(natural, order, which, target):
+    lane = lax.broadcasted_iota(jnp.int32, (128, 128), 1)
+    upper = lane >= 64
+    rows = slice(HALO, HALO + 128)
+    for w in which:
+        halves = [], []
+        for m in range(4):
+            a, b = natural[w, m, rows, :], natural[w, m + 4, rows, :]
+            halves[0].append(jnp.where(upper, pltpu.roll(b, 64, 1), a))
+            halves[1].append(jnp.where(upper, b, pltpu.roll(a, 64, 1)))
+        for h in range(2):
+            value = jnp.concatenate(halves[h], axis=1)
+            hi = value.astype(BF16)
+            lo = (value - hi.astype(F32)).astype(BF16)
+            target[w, :, 512 * h : 512 * h + 512] = jnp.dot(
+                hi, order[...], preferred_element_type=F32
+            ) + jnp.dot(lo, order[...], preferred_element_type=F32)
+
+
+def finish(x_wide, sum_x, root_x, slope_r, slope_c, sum_g, sum_h, sum_t, natural, order, wide, sems, grad_hbm, disp_hbm, boxes):
     def rows(m, turn):
         root = root_x[m]
         g = root * root * sum_g[m]
@@ -416,7 +425,7 @@
             sum_h[here] = grad * slope_c[here]
 
     over_steps(cols)
-    restore(natural, other, [0], wide)
+    restore(natural, order, [0], wide)
     out = pltpu.make_async_copy(wide.at[0], grad_hbm, sems.at[0])
     out.start()
 
@@ -434,7 +443,7 @@
             natural[2, m, pl.ds(k, 8, stride=STEPS), :] = s2[m]
 
     over_steps(cols_2)
-    restore(natural, other, [1, 2], wide)
+    restore(natural, order, [1, 2], wide)
     out_2 = pltpu.make_async_copy(wide.at[pl.ds(1, 2)], disp_hbm, sems.at[1])
     out_2.start()
     out.wait()
@@ -490,17 +499,17 @@
 
 def last_kernel(turns, plan, *refs):
     ys, refs = refs[: len(turns)], refs[len(turns) :]
-    x_wide, sum_x, root_x, slope_r, slope_c, _, _, _, grad, disp, g, h, t, y_wide, coef, natural, other, wide, sems = refs[:19]
+    x_wide, sum_x, root_x, slope_r, slope_c, order, _, _, _, grad, disp, g, h, t, y_wide, coef, natural, wide, sems = refs[:19]
     boxes = paired(refs[19:])
     for i, y in zip(turns, ys):
         add_pair(y, i, plan[...], False, x_wide, sum_x, root_x, g, h, t, y_wide, coef, boxes)
-    finish(x_wide, sum_x, root_x, slope_r, slope_c, g, h, t, natural, other, wide, sems, grad, disp, boxes)
+    finish(x_wide, sum_x, root_x, slope_r, slope_c, g, h, t, natural, order, wide, sems, grad, disp, boxes)
 
 
 def last_scratch():
     three = pltpu.VMEM((3, TILES, EXT, 128), F32)
     wide = pltpu.VMEM((3, 128, 1024), F32)
-    return [field(), field(), three, three, wide, pltpu.SemaphoreType.DMA((2,))] + [field() for _ in range(6)]
+    return [field(), field(), three, wide, pltpu.SemaphoreType.DMA((2,))] + [field() for _ in range(6)]
 
 
 def params(mib=24):
@@ -545,7 +554,7 @@
     halo = pl.pallas_call(
         halo_kernel,
         out_shape=(block, block),
-        in_specs=[VMEM, HBM, HBM],
+        in_specs=[SMEM, HBM, HBM],
         out_specs=(VMEM,) * 2,
         scratch_shapes=[
             pltpu.VMEM((2, EDGE, 1024), BF16),
@@ -556,7 +565,7 @@
         ],
         compiler_params=pltpu.CompilerParams(vmem_limit_bytes=66_500_000),
         name="halo",
-    )(jnp.broadcast_to(row_shift.astype(F32), (8, 128)), images, row_weights)
+    )(row_shift, images, row_weights)
     strips = range(16)
 
     def swap(value, step):
@@ -565,11 +574,16 @@
 
     first = swap(halo[0], 1)
     second = swap(halo[1], -1)
-    own, image, taps = pl.pallas_call(
+    own, image, taps, order = pl.pallas_call(
         prep_kernel,
-        out_shape=(shape((8, 1024), BF16), shape((128, 1024), BF16), shape((TILES, 8, 128), F32)),
+        out_shape=(
+            shape((8, 1024), BF16),
+            shape((128, 1024), BF16),
+            shape((TILES, 8, 128), F32),
+            shape((512, 512), BF16),
+        ),
         in_specs=[VMEM] * 2,
-        out_specs=(VMEM,) * 3,
+        out_specs=(VMEM,) * 4,
         scratch_shapes=[pltpu.VMEM((TILES, 136, 128), F32)] * 2,
         compiler_params=params(),
         cost_estimate=cost(1),
@@ -613,14 +627,14 @@
     grad, disp = pl.pallas_call(
         functools.partial(last_kernel, (5,)),
         out_shape=(shape((128, 1024), F32), shape((2, 128, 1024), F32)) + (FIELD,) * 3,
-        in_specs=[VMEM] * 10,
+        in_specs=[VMEM] * 11,
         out_specs=(HBM, HBM) + (VMEM,) * 3,
         scratch_shapes=last_scratch(),
-        input_output_aliases={7: 2, 8: 3, 9: 4},
+        input_output_aliases={8: 2, 9: 3, 10: 4},
         compiler_params=params(),
         cost_estimate=cost(5),
         name="last",
-    )(plan, from_5, *stats, slope_r, slope_c, *sums)[:2]
+    )(plan, from_5, *stats, slope_r, slope_c, order, *sums)[:2]
     return grad[None], disp[:, None]
 
 

time: 53.7 us -> 51.1 us (0.952)
  Pallas kernels: 18.8 us -> 17.2 us
  local copies, waits for them, and re-layouts: 1.34 us -> 0.75 us
    pallas_call x1, Pallas kernels: 6.08 us -> 5.01 us  [per_device(): pl.pallas_call(functools.partial(last_kernel, (5,)), out_shape=(shape((12...]
    pallas_call x1, Pallas kernels: 2.63 us -> 1.94 us  [per_device(): pl.pallas_call(halo_kernel, out_shape=(block, block), in_specs=[SMEM, HBM...]
    broadcast_in_dim x1 -> x0, local copies, waits for them, and re-layouts: 0.59 us -> none  [per_device(): jnp.broadcast_to(row_shift.astype(F32), (8, 128))]
  transfers between devices with their start and end apart: 8 -> 8, of which waited for: 1 -> 1; matrix products, arithmetic and copies ran while one was open for 0% -> 0% of each run, Pallas kernels for 17% -> 18%
where the time goes in v5:
time: 51.1 us; the launch traced here: 50.9 us
  starting transfers between devices  26.5 us (52%)
  Pallas kernels  17.2 us (34%)
  waiting for transfers between devices  4.06 us (8%)
  between operations  2.34 us (5%)
  local copies, waits for them, and re-layouts  0.75 us (1%)
    ppermute x6, starting transfers between devices, send(): return lax.ppermute(value, 'sec', [p for p in pairs if 0 <= p[1] < 16])  21.8 us
    pallas_call x5, Pallas kernels, add_pairs(): pl.pallas_call(functools.partial(pair_kernel, turns), out_shape=(FIELD,)...  7.45 us
    pallas_call x1, Pallas kernels, per_device(): pl.pallas_call(functools.partial(last_kernel, (5,)), out_shape=(shape((12...  5.01 us
    ppermute x2, starting transfers between devices, swap(): return lax.ppermute(value, 'strip', [p for p in pairs if 0 <= p[1] < 16])  4.63 us
    ppermute x2, waiting for transfers between devices, swap(): return lax.ppermute(value, 'strip', [p for p in pairs if 0 <= p[1] < 16])  4.04 us
    pallas_call x1, Pallas kernels, per_device(): pl.pallas_call(halo_kernel, out_shape=(block, block), in_specs=[SMEM, HBM...  1.94 us
    pallas_call x1, Pallas kernels, per_device(): pl.pallas_call(warp_kernel, out_shape=shape((TILES, EXT, 128), BF16), in_...  1.16 us
  transfers between devices with their start and end apart: 8, of which 1 were waited for; matrix products, arithmetic and copies ran while one was open for 0% of the time, Pallas kernels for 18%

profile of v5, /device:TPU:131, one launch (start us, length us, event | category | flops | bytes accessed | tf_op | source)
XLA Modules:
  0.0 50.9 jit_solution(5176244930981184397)
XLA Ops:
  0.6 0.0 copy-start
  1.3 0.0 copy-start.2
  1.3 1.9 %halo.1 = (bf16[32,1024]{1,0:T(8,128)(2,1)}, bf16[32,1024]{1,0:T(8,128)(2,1)}) custom-call(s32[1,1]{1,0:T(1,128)S(6)} %copy.39.shift_ref, bf16[1,128,1024]{2,1,0:T(8,128)(2,1)} %img_hbm.1, f32[1,4,128]{2,1,0:T(4,128)} %weights_hbm.1), custom_call_target="tpu_custom_call" | custom-call | tf_op jit(solution)/shard_map/halo/pallas_call | solution.py:554
  3.3 1.9 %collective-permute-start = (bf16[32,1024]{1,0:T(8,128)(2,1)}, bf16[32,1024]{1,0:T(8,128)(2,1)S(1)}, u32[]{:S(2)}, u32[]{:S(2)}) collective-permute-start(bf16[32,1024]{1,0:T(8,128)(2,1)} %get-tuple-element.32), channel_id=1, source_target_pairs={{0,1},{1,0},{2,3},{3,2},{4,5},{5,4},{6,7},{7,6},{8,9},{9,8},{10,11... | collective-permute-start | bytes 196616 | tf_op jit(solution)/shard_map/ppermute | solution.py:573
  5.2 0.0 copy-start.3
  5.2 2.7 %collective-permute-start.1 = (bf16[32,1024]{1,0:T(8,128)(2,1)}, bf16[32,1024]{1,0:T(8,128)(2,1)S(1)}, u32[]{:S(2)}, u32[]{:S(2)}) collective-permute-start(bf16[32,1024]{1,0:T(8,128)(2,1)} %get-tuple-element.33), channel_id=1, source_target_pairs={{1,2},{2,1},{3,4},{4,3},{5,6},{6,5},{7,8},{8,7},{9,10},{10,9},{11,... | collective-permute-start | bytes 196616 | tf_op jit(solution)/shard_map/ppermute | solution.py:573
  7.9 0.0 copy-done.2
  8.0 0.0 copy-done.3
  8.6 0.0 copy-start.1
  8.6 0.7 %copy-done.1 = f32[1,4,128]{2,1,0:T(4,128)S(1)} copy-done((f32[1,4,128]{2,1,0:T(4,128)S(1)}, f32[1,4,128]{2,1,0:T(4,128)}, u32[]{:S(2)}) %copy-start.1) | copy-done | bytes 2072
  9.3 0.1 concatenate.3.small_ref.small
  9.4 0.0 copy-done
  9.4 0.7 %prep.1 = (bf16[8,1024]{1,0:T(8,128)(2,1)S(1)}, bf16[128,1024]{1,0:T(8,128)(2,1)S(1)}, f32[8,8,128]{2,1,0:T(8,128)S(1)}, bf16[512,512]{1,0:T(8,128)(2,1)S(1)}) custom-call(bf16[128,1024]{1,0:T(8,128)(2,1)S(1)} %bitcast.12, f32[16,1024]{1,0:T(8,128)S(1)} %concatenate.3.small_ref.small), custom_call_target="tpu_custom_call" | custom-call | flops 4000000 | bytes 1000000 | tf_op jit(solution)/shard_map/prep/pallas_call | solution.py:577
  10.1 0.0 collective-permute-done.first_ref
  10.1 4.0 %collective-permute-done.1.second_ref = bf16[32,1024]{1,0:T(8,128)(2,1)S(1)} collective-permute-done((bf16[32,1024]{1,0:T(8,128)(2,1)}, bf16[32,1024]{1,0:T(8,128)(2,1)S(1)}, u32[]{:S(2)}, u32[]{:S(2)}) %collective-permute-start.1) | collective-permute-done | bytes 65568 | tf_op jit(solution)/shard_map/ppermute | solution.py:573
  14.2 1.2 %warp.1.x = bf16[8,152,128]{2,1,0:T(8,128)(2,1)S(1)} custom-call(s32[1]{0:T(128)S(6)} %copy.40.shift_ref, bf16[128,1024]{1,0:T(8,128)(2,1)S(1)} %get-tuple-element.31.img_ref, bf16[32,1024]{1,0:T(8,128)(2,1)S(1)} %collective-permute-done.first_ref, bf16[32,1024]{1,0:T(8,128)(2,1)S(1)} %collective-permute-done.1.second_ref, ...), custom_call_target="tpu_custom_call" | custom-call | tf_op jit(solution)/shard_map/warp/pallas_call | solution.py:592
  15.3 3.2 %collective-permute-start.4 = (bf16[8,152,128]{2,1,0:T(8,128)(2,1)S(1)}, bf16[8,152,128]{2,1,0:T(8,128)(2,1)S(1)}, u32[]{:S(2)}, u32[]{:S(2)}) collective-permute-start(bf16[8,152,128]{2,1,0:T(8,128)(2,1)S(1)} %warp.1.x), channel_id=1, source_target_pairs={{16,48},{32,0},{48,80},{64,32},{80,112},{96,64},{112,144},{128,96}... | collective-permute-start | bytes 933896 | tf_op jit(solution)/shard_map/ppermute | solution.py:605
  18.6 4.2 %collective-permute-start.2 = (bf16[8,152,128]{2,1,0:T(8,128)(2,1)S(1)}, bf16[8,152,128]{2,1,0:T(8,128)(2,1)S(1)}, u32[]{:S(2)}, u32[]{:S(2)}) collective-permute-start(bf16[8,152,128]{2,1,0:T(8,128)(2,1)S(1)} %warp.1.x), channel_id=1, source_target_pairs={{0,32},{32,64},{48,16},{64,96},{80,48},{96,128},{112,80},{128,160}... | collective-permute-start | bytes 933896 | tf_op jit(solution)/shard_map/ppermute | solution.py:605
  22.8 2.5 %collective-permute-start.7 = (bf16[8,152,128]{2,1,0:T(8,128)(2,1)S(1)}, bf16[8,152,128]{2,1,0:T(8,128)(2,1)S(1)}, u32[]{:S(2)}, u32[]{:S(2)}) collective-permute-start(bf16[8,152,128]{2,1,0:T(8,128)(2,1)S(1)} %warp.1.x), channel_id=1, source_target_pairs={{0,16},{16,0},{32,48},{48,32},{64,80},{80,64},{96,112},{112,96},{1... | collective-permute-start | bytes 933896 | tf_op jit(solution)/shard_map/ppermute | solution.py:605
  25.3 0.0 collective-permute-done.4.refs_0_
  25.3 5.1 %collective-permute-start.6 = (bf16[8,152,128]{2,1,0:T(8,128)(2,1)S(1)}, bf16[8,152,128]{2,1,0:T(8,128)(2,1)S(1)}, u32[]{:S(2)}, u32[]{:S(2)}) collective-permute-start(bf16[8,152,128]{2,1,0:T(8,128)(2,1)S(1)} %collective-permute-done.4.refs_0_), channel_id=1, source_target_pairs={{0,16},{16,0},{32,48},{48,32},{64,80},{80,64},{96,112},{112,96},{1... | collective-permute-start | bytes 933896 | tf_op jit(solution)/shard_map/ppermute | solution.py:605
  30.3 1.9 %collective-permute-start.5 = (bf16[8,152,128]{2,1,0:T(8,128)(2,1)S(1)}, bf16[8,152,128]{2,1,0:T(8,128)(2,1)S(1)}, u32[]{:S(2)}, u32[]{:S(2)}) collective-permute-start(bf16[8,152,128]{2,1,0:T(8,128)(2,1)S(1)} %collective-permute-done.4.refs_0_), channel_id=1, source_target_pairs={{16,32},{32,16},{48,64},{64,48},{80,96},{96,80},{112,128},{128,112... | collective-permute-start | bytes 933896 | tf_op jit(solution)/shard_map/ppermute | solution.py:605
  32.3 0.0 collective-permute-done.2.refs_0_
  32.3 5.0 %collective-permute-start.3 = (bf16[8,152,128]{2,1,0:T(8,128)(2,1)S(1)}, bf16[8,152,128]{2,1,0:T(8,128)(2,1)S(1)}, u32[]{:S(2)}, u32[]{:S(2)}) collective-permute-start(bf16[8,152,128]{2,1,0:T(8,128)(2,1)S(1)} %collective-permute-done.2.refs_0_), channel_id=1, source_target_pairs={{0,16},{16,0},{32,48},{48,32},{64,80},{80,64},{96,112},{112,96},{1... | collective-permute-start | bytes 933896 | tf_op jit(solution)/shard_map/ppermute | solution.py:605
  37.2 0.9 %own.1 = (f32[8,152,128]{2,1,0:T(8,128)S(1)}, f32[8,152,128]{2,1,0:T(8,128)S(1)}, f32[8,152,128]{2,1,0:T(8,128)S(1)}, f32[8,152,128]{2,1,0:T(8,128)S(1)}, f32[8,...) custom-call(f32[16,1024]{1,0:T(8,128)S(1)} %concatenate.3.small_ref.small, bf16[8,152,128]{2,1,0:T(8,128)(2,1)S(1)} %warp.1.x), custom_call_target="tpu_custom_call" | custom-call | flops 5200000 | bytes 1000000 | tf_op jit(solution)/shard_map/own/pallas_call | solution.py:613
  38.2 0.0 collective-permute-done.7.refs_0_
  38.2 1.4 %pair.5 = (f32[8,152,128]{2,1,0:T(8,128)S(1)}, f32[8,152,128]{2,1,0:T(8,128)S(1)}, f32[8,152,128]{2,1,0:T(8,128)S(1)}) custom-call(f32[8,128]{1,0:T(8,128)S(1)} %get-tuple-element.36.plan, bf16[8,152,128]{2,1,0:T(8,128)(2,1)S(1)} %collective-permute-done.7.refs_0_, f32[8,152,128]{2,1,0:T(8,128)S(1)} %get-tuple-element.37.refs_1_, ...), custom_call_target="tpu_custom_call" | custom-call | flops 6000000 | bytes 1000000 | tf_op jit(solution)/shard_map/pair/pallas_call | solution.py:526
  39.6 1.5 %pair.6 = (f32[8,152,128]{2,1,0:T(8,128)S(1)}, f32[8,152,128]{2,1,0:T(8,128)S(1)}, f32[8,152,128]{2,1,0:T(8,128)S(1)}) custom-call(f32[8,128]{1,0:T(8,128)S(1)} %get-tuple-element.36.plan, bf16[8,152,128]{2,1,0:T(8,128)(2,1)S(1)} %collective-permute-done.4.refs_0_, ...), custom_call_target="tpu_custom_call", output_to_operand_aliasing={{0}: (5, {}), {1}: (6, {}), {2}: (7, {})} | custom-call | flops 6000000 | bytes 1000000 | tf_op jit(solution)/shard_map/pair/pallas_call | solution.py:526
  41.1 0.0 collective-permute-done.6.refs_0_
  41.1 1.5 %pair.7 = (f32[8,152,128]{2,1,0:T(8,128)S(1)}, f32[8,152,128]{2,1,0:T(8,128)S(1)}, f32[8,152,128]{2,1,0:T(8,128)S(1)}) custom-call(f32[8,128]{1,0:T(8,128)S(1)} %get-tuple-element.36.plan, bf16[8,152,128]{2,1,0:T(8,128)(2,1)S(1)} %collective-permute-done.6.refs_0_, ...), custom_call_target="tpu_custom_call", output_to_operand_aliasing={{0}: (5, {}), {1}: (6, {}), {2}: (7, {})} | custom-call | flops 6000000 | bytes 1000000 | tf_op jit(solution)/shard_map/pair/pallas_call | solution.py:526
  42.6 1.5 %pair.8 = (f32[8,152,128]{2,1,0:T(8,128)S(1)}, f32[8,152,128]{2,1,0:T(8,128)S(1)}, f32[8,152,128]{2,1,0:T(8,128)S(1)}) custom-call(f32[8,128]{1,0:T(8,128)S(1)} %get-tuple-element.36.plan, bf16[8,152,128]{2,1,0:T(8,128)(2,1)S(1)} %collective-permute-done.2.refs_0_, ...), custom_call_target="tpu_custom_call", output_to_operand_aliasing={{0}: (5, {}), {1}: (6, {}), {2}: (7, {})} | custom-call | flops 6000000 | bytes 1000000 | tf_op jit(solution)/shard_map/pair/pallas_call | solution.py:526
  44.1 0.0 collective-permute-done.5.refs_0_
  44.2 1.5 %pair.9 = (f32[8,152,128]{2,1,0:T(8,128)S(1)}, f32[8,152,128]{2,1,0:T(8,128)S(1)}, f32[8,152,128]{2,1,0:T(8,128)S(1)}) custom-call(f32[8,128]{1,0:T(8,128)S(1)} %get-tuple-element.36.plan, bf16[8,152,128]{2,1,0:T(8,128)(2,1)S(1)} %collective-permute-done.5.refs_0_, ...), custom_call_target="tpu_custom_call", output_to_operand_aliasing={{0}: (5, {}), {1}: (6, {}), {2}: (7, {})} | custom-call | flops 6000000 | bytes 1000000 | tf_op jit(solution)/shard_map/pair/pallas_call | solution.py:526
  45.7 0.0 collective-permute-done.3.refs_0_
  45.7 5.0 %last.1 = (f32[128,1024]{1,0:T(8,128)}, f32[2,128,1024]{2,1,0:T(8,128)}, f32[8,152,128]{2,1,0:T(8,128)S(1)}, f32[8,152,128]{2,1,0:T(8,128)S(1)}, f32[8,152,128]{2,1,0:T(8,128)S(1)}) custom-call(f32[8,128]{1,0:T(8,128)S(1)} %get-tuple-element.36.plan, ...), custom_call_target="tpu_custom_call", output_to_operand_aliasing={{2}: (8, {}), {3}: (9, {}), {4}: (10, {})} | custom-call | flops 20000000 | bytes 1000000 | tf_op jit(solution)/shard_map/last/pallas_call | solution.py:627
  (6 shorter events, 0.0 us)
Async XLA Ops:
  0.6 8.8 %copy-start = (bf16[1,128,1024]{2,1,0:T(8,128)(2,1)S(1)}, bf16[1,128,1024]{2,1,0:T(8,128)(2,1)}, u32[]{:S(2)}) copy-start(bf16[1,128,1024]{2,1,0:T(8,128)(2,1)} %img_hbm.1) | copy-start | bytes 786436
  1.3 6.6 %copy-start.2 = (bf16[1,4,1024]{2,1,0:T(4,128)(2,1)S(1)}, bf16[1,4,1024]{2,1,0:T(4,128)(2,1)}, u32[]{:S(2)}) copy-start(bf16[1,4,1024]{2,1,0:T(4,128)(2,1)} %param.9) | copy-start | bytes 24580
  3.3 6.8 %collective-permute-start = (bf16[32,1024]{1,0:T(8,128)(2,1)}, bf16[32,1024]{1,0:T(8,128)(2,1)S(1)}, u32[]{:S(2)}, u32[]{:S(2)}) collective-permute-start(bf16[32,1024]{1,0:T(8,128)(2,1)} %get-tuple-element.32), channel_id=1, source_target_pairs={{0,1},{1,0},{2,3},{3,2},{4,5},{5,4},{6,7},{7,6},{8,9},{9,8},{10,11... | collective-permute-start | bytes 196616 | tf_op jit(solution)/shard_map/ppermute | solution.py:573
  5.2 2.7 %copy-start.3 = (s32[16,3]{0,1:T(4,128)S(1)}, s32[16,3]{0,1:T(4,128)}, u32[]{:S(2)}) copy-start(s32[16,3]{0,1:T(4,128)} %param.11) | copy-start | bytes 580
  5.2 9.0 %collective-permute-start.1 = (bf16[32,1024]{1,0:T(8,128)(2,1)}, bf16[32,1024]{1,0:T(8,128)(2,1)S(1)}, u32[]{:S(2)}, u32[]{:S(2)}) collective-permute-start(bf16[32,1024]{1,0:T(8,128)(2,1)} %get-tuple-element.33), channel_id=1, source_target_pairs={{1,2},{2,1},{3,4},{4,3},{5,6},{6,5},{7,8},{8,7},{9,10},{10,9},{11,... | collective-permute-start | bytes 196616 | tf_op jit(solution)/shard_map/ppermute | solution.py:573
  8.6 0.7 %copy-start.1 = (f32[1,4,128]{2,1,0:T(4,128)S(1)}, f32[1,4,128]{2,1,0:T(4,128)}, u32[]{:S(2)}) copy-start(f32[1,4,128]{2,1,0:T(4,128)} %weights_hbm.1) | copy-start | bytes 6148
  15.3 9.9 %collective-permute-start.4 = (bf16[8,152,128]{2,1,0:T(8,128)(2,1)S(1)}, bf16[8,152,128]{2,1,0:T(8,128)(2,1)S(1)}, u32[]{:S(2)}, u32[]{:S(2)}) collective-permute-start(bf16[8,152,128]{2,1,0:T(8,128)(2,1)S(1)} %warp.1.x), channel_id=1, source_target_pairs={{16,48},{32,0},{48,80},{64,32},{80,112},{96,64},{112,144},{128,96}... | collective-permute-start | bytes 933896 | tf_op jit(solution)/shard_map/ppermute | solution.py:605
  18.6 13.7 %collective-permute-start.2 = (bf16[8,152,128]{2,1,0:T(8,128)(2,1)S(1)}, bf16[8,152,128]{2,1,0:T(8,128)(2,1)S(1)}, u32[]{:S(2)}, u32[]{:S(2)}) collective-permute-start(bf16[8,152,128]{2,1,0:T(8,128)(2,1)S(1)} %warp.1.x), channel_id=1, source_target_pairs={{0,32},{32,64},{48,16},{64,96},{80,48},{96,128},{112,80},{128,160}... | collective-permute-start | bytes 933896 | tf_op jit(solution)/shard_map/ppermute | solution.py:605
  22.8 15.4 %collective-permute-start.7 = (bf16[8,152,128]{2,1,0:T(8,128)(2,1)S(1)}, bf16[8,152,128]{2,1,0:T(8,128)(2,1)S(1)}, u32[]{:S(2)}, u32[]{:S(2)}) collective-permute-start(bf16[8,152,128]{2,1,0:T(8,128)(2,1)S(1)} %warp.1.x), channel_id=1, source_target_pairs={{0,16},{16,0},{32,48},{48,32},{64,80},{80,64},{96,112},{112,96},{1... | collective-permute-start | bytes 933896 | tf_op jit(solution)/shard_map/ppermute | solution.py:605
  25.3 15.8 %collective-permute-start.6 = (bf16[8,152,128]{2,1,0:T(8,128)(2,1)S(1)}, bf16[8,152,128]{2,1,0:T(8,128)(2,1)S(1)}, u32[]{:S(2)}, u32[]{:S(2)}) collective-permute-start(bf16[8,152,128]{2,1,0:T(8,128)(2,1)S(1)} %collective-permute-done.4.refs_0_), channel_id=1, source_target_pairs={{0,16},{16,0},{32,48},{48,32},{64,80},{80,64},{96,112},{112,96},{1... | collective-permute-start | bytes 933896 | tf_op jit(solution)/shard_map/ppermute | solution.py:605
  30.3 13.8 %collective-permute-start.5 = (bf16[8,152,128]{2,1,0:T(8,128)(2,1)S(1)}, bf16[8,152,128]{2,1,0:T(8,128)(2,1)S(1)}, u32[]{:S(2)}, u32[]{:S(2)}) collective-permute-start(bf16[8,152,128]{2,1,0:T(8,128)(2,1)S(1)} %collective-permute-done.4.refs_0_), channel_id=1, source_target_pairs={{16,32},{32,16},{48,64},{64,48},{80,96},{96,80},{112,128},{128,112... | collective-permute-start | bytes 933896 | tf_op jit(solution)/shard_map/ppermute | solution.py:605
  32.3 13.4 %collective-permute-start.3 = (bf16[8,152,128]{2,1,0:T(8,128)(2,1)S(1)}, bf16[8,152,128]{2,1,0:T(8,128)(2,1)S(1)}, u32[]{:S(2)}, u32[]{:S(2)}) collective-permute-start(bf16[8,152,128]{2,1,0:T(8,128)(2,1)S(1)} %collective-permute-done.2.refs_0_), channel_id=1, source_target_pairs={{0,16},{16,0},{32,48},{48,32},{64,80},{80,64},{96,112},{112,96},{1... | collective-permute-start | bytes 933896 | tf_op jit(solution)/shard_map/ppermute | solution.py:605

commit v6 on v5

--- a/solution.py
+++ b/solution.py
@@ -23,7 +23,7 @@
 EDGE = 24
 UNROLL = 3
 GROUP = 8
-BLOCK = 32
+BLOCK = 24
 
 
 def window_sums(seq, width):
@@ -198,21 +198,19 @@
     shift = jnp.full((8, 128), shift_ref[0, 0], jnp.int32).astype(F32)
     even = lax.axis_index("strip") % 2 == 0
 
+    row = lax.broadcasted_iota(jnp.int32, (8, 128), 0)
+    tables = [table_rows(jnp.broadcast_to(weights[tap : tap + 1, :], (8, 128)), shift, tap) for tap in range(TAPS)]
+
     def fill(up_ref, down_ref):
         for m in range(TILES):
             cols = slice(128 * m, 128 * m + 128)
-            down_ref[0:EDGE, cols] = other[m, 0:EDGE, :].astype(BF16)
-            up_ref[0:EDGE, cols] = other[m, EDGE : 2 * EDGE, :].astype(BF16)
-        for tap in range(TAPS):
-            line = jnp.broadcast_to(weights[tap : tap + 1, :], (8, 128))
-            full = table_rows(line, shift, tap)
-            at = 256 * tap
-            up_ref[EDGE:BLOCK, at : at + 128] = jnp.where(lane < HALO, full, zero).astype(BF16)
-            up_ref[EDGE:BLOCK, at + 128 : at + 256] = zero.astype(BF16)
-            down_ref[EDGE:BLOCK, at : at + 128] = zero.astype(BF16)
-            down_ref[EDGE:BLOCK, at + 128 : at + 256] = jnp.where(
-                (lane >= HALO) & (lane < 2 * HALO), full, zero
-            ).astype(BF16)
+            table = tables[m // 2]
+            before = jnp.where(lane < HALO, table, zero) if m % 2 == 0 else zero
+            after = jnp.where((lane >= HALO) & (lane < 2 * HALO), table, zero) if m % 2 else zero
+            up_0 = jnp.where(row < 4, before, other[m, EDGE : EDGE + 8, :])
+            down_2 = jnp.where(row >= 4, pltpu.roll(after, 4, 0), other[m, 16:24, :])
+            up_ref[:, cols] = jnp.concatenate([up_0, other[m, EDGE + 8 : 2 * EDGE, :]], axis=0).astype(BF16)
+            down_ref[:, cols] = jnp.concatenate([other[m, 0:16, :], down_2], axis=0).astype(BF16)
 
     @pl.when(even)
     def _():
@@ -249,10 +247,10 @@
 
 def warp_kernel(shift_ref, img_ref, first_ref, second_ref, own_ref, taps_ref, out_ref, row_warped, virtual):
     even = lax.axis_index("strip") % 2 == 0
-    first, second = first_ref[...], second_ref[...]
+    first, second = first_ref[...].astype(F32), second_ref[...].astype(F32)
     low = jnp.where(even, second, first)
     high = jnp.where(even, first, second)
-    meta = (first[EDGE:].astype(F32) + own_ref[...].astype(F32) + second[EDGE:].astype(F32)).astype(BF16)
+    meta = (low[0:8] + own_ref[...].astype(F32) + pltpu.roll(high[16:24], 4, 0)).astype(BF16)
     place = lax.broadcasted_iota(jnp.int32, (EXT, 256), 0)
     rho = (place % 8) * STEPS + place // 8
     spread = jnp.where(
@@ -269,8 +267,7 @@
     ]
     width = 2 * BLOCK + 128
     lane = lax.broadcasted_iota(jnp.int32, (EXT, width), 1)
-    image_row = jnp.where(lane < EDGE, lane - EDGE, jnp.where(lane < BLOCK, -1000, lane - BLOCK))
-    image_row = jnp.where(lane < BLOCK + 128 + EDGE, image_row, 2000)
+    image_row = jnp.where((lane >= 7) & (lane < EDGE + 128 + 18), lane - EDGE, 2000)
     own_row = lax.broadcasted_iota(jnp.int32, (EXT, width), 0)
     own_row = (own_row % 8) * STEPS + own_row // 8 - HALO
     offset = (image_row - own_row + 1).astype(F32) - columns[0][:, 3:4]
@@ -279,7 +276,7 @@
         weight = columns[tap][:, 0:1] + columns[tap][:, 1:2] + columns[tap][:, 2:3]
         value = jnp.where(offset == float(tap), weight, value)
     hi, mid, lo = split3(value)
-    source = jnp.concatenate([low, img_ref[...], high], axis=0)
+    source = jnp.concatenate([low, img_ref[...].astype(F32), high], axis=0).astype(BF16)
     total = jnp.zeros((EXT, 1024), F32)
     for piece in (lo, mid, hi):
         total = total + jnp.dot(piece.astype(BF16), source, preferred_element_type=F32)

time: 51.1 us -> 50.9 us (level)
  no operation moved by 1% of the time
where the time goes in v6:
time: 50.9 us; the launch traced here: 50.6 us
  starting transfers between devices  26.5 us (52%)
  Pallas kernels  17.2 us (34%)
  waiting for transfers between devices  3.88 us (8%)
  between operations  2.34 us (5%)
  local copies, waits for them, and re-layouts  0.75 us (1%)
    ppermute x6, starting transfers between devices, send(): return lax.ppermute(value, 'sec', [p for p in pairs if 0 <= p[1] < 16])  21.8 us
    pallas_call x5, Pallas kernels, add_pairs(): pl.pallas_call(functools.partial(pair_kernel, turns), out_shape=(FIELD,)...  7.45 us
    pallas_call x1, Pallas kernels, per_device(): pl.pallas_call(functools.partial(last_kernel, (5,)), out_shape=(shape((12...  5.01 us
    ppermute x2, starting transfers between devices, swap(): return lax.ppermute(value, 'strip', [p for p in pairs if 0 <= p[1] < 16])  4.63 us
    ppermute x2, waiting for transfers between devices, swap(): return lax.ppermute(value, 'strip', [p for p in pairs if 0 <= p[1] < 16])  3.87 us
    pallas_call x1, Pallas kernels, per_device(): pl.pallas_call(halo_kernel, out_shape=(block, block), in_specs=[SMEM, HBM...  1.86 us
    pallas_call x1, Pallas kernels, per_device(): pl.pallas_call(warp_kernel, out_shape=shape((TILES, EXT, 128), BF16), in_...  1.18 us
  transfers between devices with their start and end apart: 8, of which 1 were waited for; matrix products, arithmetic and copies ran while one was open for 0% of the time, Pallas kernels for 18%

profile of v6, /device:TPU:131, one launch (start us, length us, event | category | flops | bytes accessed | tf_op | source)
XLA Modules:
  0.0 50.6 jit_solution(14640906640003876752)
XLA Ops:
  0.6 0.0 copy-start
  1.3 0.0 copy-start.2
  1.3 1.9 %halo.1 = (bf16[24,1024]{1,0:T(8,128)(2,1)}, bf16[24,1024]{1,0:T(8,128)(2,1)}) custom-call(s32[1,1]{1,0:T(1,128)S(6)} %copy.39.shift_ref, bf16[1,128,1024]{2,1,0:T(8,128)(2,1)} %img_hbm.1, f32[1,4,128]{2,1,0:T(4,128)} %weights_hbm.1), custom_call_target="tpu_custom_call" | custom-call | tf_op jit(solution)/shard_map/halo/pallas_call | solution.py:551
  3.2 1.9 %collective-permute-start = (bf16[24,1024]{1,0:T(8,128)(2,1)}, bf16[24,1024]{1,0:T(8,128)(2,1)S(1)}, u32[]{:S(2)}, u32[]{:S(2)}) collective-permute-start(bf16[24,1024]{1,0:T(8,128)(2,1)} %get-tuple-element.32), channel_id=1, source_target_pairs={{0,1},{1,0},{2,3},{3,2},{4,5},{5,4},{6,7},{7,6},{8,9},{9,8},{10,11... | collective-permute-start | bytes 147464 | tf_op jit(solution)/shard_map/ppermute | solution.py:570
  5.1 0.0 copy-start.3
  5.1 2.7 %collective-permute-start.1 = (bf16[24,1024]{1,0:T(8,128)(2,1)}, bf16[24,1024]{1,0:T(8,128)(2,1)S(1)}, u32[]{:S(2)}, u32[]{:S(2)}) collective-permute-start(bf16[24,1024]{1,0:T(8,128)(2,1)} %get-tuple-element.33), channel_id=1, source_target_pairs={{1,2},{2,1},{3,4},{4,3},{5,6},{6,5},{7,8},{8,7},{9,10},{10,9},{11,... | collective-permute-start | bytes 147464 | tf_op jit(solution)/shard_map/ppermute | solution.py:570
  7.8 0.0 copy-done.2
  7.9 0.0 copy-done.3
  8.5 0.0 copy-start.1
  8.6 0.7 %copy-done.1 = f32[1,4,128]{2,1,0:T(4,128)S(1)} copy-done((f32[1,4,128]{2,1,0:T(4,128)S(1)}, f32[1,4,128]{2,1,0:T(4,128)}, u32[]{:S(2)}) %copy-start.1) | copy-done | bytes 2072
  9.2 0.1 concatenate.3.small_ref.small
  9.3 0.0 copy-done
  9.3 0.7 %prep.1 = (bf16[8,1024]{1,0:T(8,128)(2,1)S(1)}, bf16[128,1024]{1,0:T(8,128)(2,1)S(1)}, f32[8,8,128]{2,1,0:T(8,128)S(1)}, bf16[512,512]{1,0:T(8,128)(2,1)S(1)}) custom-call(bf16[128,1024]{1,0:T(8,128)(2,1)S(1)} %bitcast.12, f32[16,1024]{1,0:T(8,128)S(1)} %concatenate.3.small_ref.small), custom_call_target="tpu_custom_call" | custom-call | flops 4000000 | bytes 1000000 | tf_op jit(solution)/shard_map/prep/pallas_call | solution.py:574
  10.0 0.0 collective-permute-done.first_ref
  10.1 3.9 %collective-permute-done.1.second_ref = bf16[24,1024]{1,0:T(8,128)(2,1)S(1)} collective-permute-done((bf16[24,1024]{1,0:T(8,128)(2,1)}, bf16[24,1024]{1,0:T(8,128)(2,1)S(1)}, u32[]{:S(2)}, u32[]{:S(2)}) %collective-permute-start.1) | collective-permute-done | bytes 49184 | tf_op jit(solution)/shard_map/ppermute | solution.py:570
  13.9 1.2 %warp.1.x = bf16[8,152,128]{2,1,0:T(8,128)(2,1)S(1)} custom-call(s32[1]{0:T(128)S(6)} %copy.40.shift_ref, bf16[128,1024]{1,0:T(8,128)(2,1)S(1)} %get-tuple-element.31.img_ref, bf16[24,1024]{1,0:T(8,128)(2,1)S(1)} %collective-permute-done.first_ref, bf16[24,1024]{1,0:T(8,128)(2,1)S(1)} %collective-permute-done.1.second_ref, ...), custom_call_target="tpu_custom_call" | custom-call | tf_op jit(solution)/shard_map/warp/pallas_call | solution.py:589
  15.1 3.2 %collective-permute-start.4 = (bf16[8,152,128]{2,1,0:T(8,128)(2,1)S(1)}, bf16[8,152,128]{2,1,0:T(8,128)(2,1)S(1)}, u32[]{:S(2)}, u32[]{:S(2)}) collective-permute-start(bf16[8,152,128]{2,1,0:T(8,128)(2,1)S(1)} %warp.1.x), channel_id=1, source_target_pairs={{16,48},{32,0},{48,80},{64,32},{80,112},{96,64},{112,144},{128,96}... | collective-permute-start | bytes 933896 | tf_op jit(solution)/shard_map/ppermute | solution.py:602
  18.3 4.2 %collective-permute-start.2 = (bf16[8,152,128]{2,1,0:T(8,128)(2,1)S(1)}, bf16[8,152,128]{2,1,0:T(8,128)(2,1)S(1)}, u32[]{:S(2)}, u32[]{:S(2)}) collective-permute-start(bf16[8,152,128]{2,1,0:T(8,128)(2,1)S(1)} %warp.1.x), channel_id=1, source_target_pairs={{0,32},{32,64},{48,16},{64,96},{80,48},{96,128},{112,80},{128,160}... | collective-permute-start | bytes 933896 | tf_op jit(solution)/shard_map/ppermute | solution.py:602
  22.5 2.5 %collective-permute-start.7 = (bf16[8,152,128]{2,1,0:T(8,128)(2,1)S(1)}, bf16[8,152,128]{2,1,0:T(8,128)(2,1)S(1)}, u32[]{:S(2)}, u32[]{:S(2)}) collective-permute-start(bf16[8,152,128]{2,1,0:T(8,128)(2,1)S(1)} %warp.1.x), channel_id=1, source_target_pairs={{0,16},{16,0},{32,48},{48,32},{64,80},{80,64},{96,112},{112,96},{1... | collective-permute-start | bytes 933896 | tf_op jit(solution)/shard_map/ppermute | solution.py:602
  25.0 0.0 collective-permute-done.4.refs_0_
  25.0 5.1 %collective-permute-start.6 = (bf16[8,152,128]{2,1,0:T(8,128)(2,1)S(1)}, bf16[8,152,128]{2,1,0:T(8,128)(2,1)S(1)}, u32[]{:S(2)}, u32[]{:S(2)}) collective-permute-start(bf16[8,152,128]{2,1,0:T(8,128)(2,1)S(1)} %collective-permute-done.4.refs_0_), channel_id=1, source_target_pairs={{0,16},{16,0},{32,48},{48,32},{64,80},{80,64},{96,112},{112,96},{1... | collective-permute-start | bytes 933896 | tf_op jit(solution)/shard_map/ppermute | solution.py:602
  30.1 1.9 %collective-permute-start.5 = (bf16[8,152,128]{2,1,0:T(8,128)(2,1)S(1)}, bf16[8,152,128]{2,1,0:T(8,128)(2,1)S(1)}, u32[]{:S(2)}, u32[]{:S(2)}) collective-permute-start(bf16[8,152,128]{2,1,0:T(8,128)(2,1)S(1)} %collective-permute-done.4.refs_0_), channel_id=1, source_target_pairs={{16,32},{32,16},{48,64},{64,48},{80,96},{96,80},{112,128},{128,112... | collective-permute-start | bytes 933896 | tf_op jit(solution)/shard_map/ppermute | solution.py:602
  32.0 0.0 collective-permute-done.2.refs_0_
  32.0 5.0 %collective-permute-start.3 = (bf16[8,152,128]{2,1,0:T(8,128)(2,1)S(1)}, bf16[8,152,128]{2,1,0:T(8,128)(2,1)S(1)}, u32[]{:S(2)}, u32[]{:S(2)}) collective-permute-start(bf16[8,152,128]{2,1,0:T(8,128)(2,1)S(1)} %collective-permute-done.2.refs_0_), channel_id=1, source_target_pairs={{0,16},{16,0},{32,48},{48,32},{64,80},{80,64},{96,112},{112,96},{1... | collective-permute-start | bytes 933896 | tf_op jit(solution)/shard_map/ppermute | solution.py:602
  37.0 0.9 %own.1 = (f32[8,152,128]{2,1,0:T(8,128)S(1)}, f32[8,152,128]{2,1,0:T(8,128)S(1)}, f32[8,152,128]{2,1,0:T(8,128)S(1)}, f32[8,152,128]{2,1,0:T(8,128)S(1)}, f32[8,...) custom-call(f32[16,1024]{1,0:T(8,128)S(1)} %concatenate.3.small_ref.small, bf16[8,152,128]{2,1,0:T(8,128)(2,1)S(1)} %warp.1.x), custom_call_target="tpu_custom_call" | custom-call | flops 5200000 | bytes 1000000 | tf_op jit(solution)/shard_map/own/pallas_call | solution.py:610
  37.9 0.0 collective-permute-done.7.refs_0_
  37.9 1.4 %pair.5 = (f32[8,152,128]{2,1,0:T(8,128)S(1)}, f32[8,152,128]{2,1,0:T(8,128)S(1)}, f32[8,152,128]{2,1,0:T(8,128)S(1)}) custom-call(f32[8,128]{1,0:T(8,128)S(1)} %get-tuple-element.36.plan, bf16[8,152,128]{2,1,0:T(8,128)(2,1)S(1)} %collective-permute-done.7.refs_0_, f32[8,152,128]{2,1,0:T(8,128)S(1)} %get-tuple-element.37.refs_1_, ...), custom_call_target="tpu_custom_call" | custom-call | flops 6000000 | bytes 1000000 | tf_op jit(solution)/shard_map/pair/pallas_call | solution.py:523
  39.3 1.5 %pair.6 = (f32[8,152,128]{2,1,0:T(8,128)S(1)}, f32[8,152,128]{2,1,0:T(8,128)S(1)}, f32[8,152,128]{2,1,0:T(8,128)S(1)}) custom-call(f32[8,128]{1,0:T(8,128)S(1)} %get-tuple-element.36.plan, bf16[8,152,128]{2,1,0:T(8,128)(2,1)S(1)} %collective-permute-done.4.refs_0_, ...), custom_call_target="tpu_custom_call", output_to_operand_aliasing={{0}: (5, {}), {1}: (6, {}), {2}: (7, {})} | custom-call | flops 6000000 | bytes 1000000 | tf_op jit(solution)/shard_map/pair/pallas_call | solution.py:523
  40.9 0.0 collective-permute-done.6.refs_0_
  40.9 1.5 %pair.7 = (f32[8,152,128]{2,1,0:T(8,128)S(1)}, f32[8,152,128]{2,1,0:T(8,128)S(1)}, f32[8,152,128]{2,1,0:T(8,128)S(1)}) custom-call(f32[8,128]{1,0:T(8,128)S(1)} %get-tuple-element.36.plan, bf16[8,152,128]{2,1,0:T(8,128)(2,1)S(1)} %collective-permute-done.6.refs_0_, ...), custom_call_target="tpu_custom_call", output_to_operand_aliasing={{0}: (5, {}), {1}: (6, {}), {2}: (7, {})} | custom-call | flops 6000000 | bytes 1000000 | tf_op jit(solution)/shard_map/pair/pallas_call | solution.py:523
  42.4 1.5 %pair.8 = (f32[8,152,128]{2,1,0:T(8,128)S(1)}, f32[8,152,128]{2,1,0:T(8,128)S(1)}, f32[8,152,128]{2,1,0:T(8,128)S(1)}) custom-call(f32[8,128]{1,0:T(8,128)S(1)} %get-tuple-element.36.plan, bf16[8,152,128]{2,1,0:T(8,128)(2,1)S(1)} %collective-permute-done.2.refs_0_, ...), custom_call_target="tpu_custom_call", output_to_operand_aliasing={{0}: (5, {}), {1}: (6, {}), {2}: (7, {})} | custom-call | flops 6000000 | bytes 1000000 | tf_op jit(solution)/shard_map/pair/pallas_call | solution.py:523
  43.9 0.0 collective-permute-done.5.refs_0_
  43.9 1.5 %pair.9 = (f32[8,152,128]{2,1,0:T(8,128)S(1)}, f32[8,152,128]{2,1,0:T(8,128)S(1)}, f32[8,152,128]{2,1,0:T(8,128)S(1)}) custom-call(f32[8,128]{1,0:T(8,128)S(1)} %get-tuple-element.36.plan, bf16[8,152,128]{2,1,0:T(8,128)(2,1)S(1)} %collective-permute-done.5.refs_0_, ...), custom_call_target="tpu_custom_call", output_to_operand_aliasing={{0}: (5, {}), {1}: (6, {}), {2}: (7, {})} | custom-call | flops 6000000 | bytes 1000000 | tf_op jit(solution)/shard_map/pair/pallas_call | solution.py:523
  45.4 0.0 collective-permute-done.3.refs_0_
  45.4 5.0 %last.1 = (f32[128,1024]{1,0:T(8,128)}, f32[2,128,1024]{2,1,0:T(8,128)}, f32[8,152,128]{2,1,0:T(8,128)S(1)}, f32[8,152,128]{2,1,0:T(8,128)S(1)}, f32[8,152,128]{2,1,0:T(8,128)S(1)}) custom-call(f32[8,128]{1,0:T(8,128)S(1)} %get-tuple-element.36.plan, ...), custom_call_target="tpu_custom_call", output_to_operand_aliasing={{2}: (8, {}), {3}: (9, {}), {4}: (10, {})} | custom-call | flops 20000000 | bytes 1000000 | tf_op jit(solution)/shard_map/last/pallas_call | solution.py:624
  (6 shorter events, 0.0 us)
Async XLA Ops:
  0.6 8.7 %copy-start = (bf16[1,128,1024]{2,1,0:T(8,128)(2,1)S(1)}, bf16[1,128,1024]{2,1,0:T(8,128)(2,1)}, u32[]{:S(2)}) copy-start(bf16[1,128,1024]{2,1,0:T(8,128)(2,1)} %img_hbm.1) | copy-start | bytes 786436
  1.3 6.5 %copy-start.2 = (bf16[1,4,1024]{2,1,0:T(4,128)(2,1)S(1)}, bf16[1,4,1024]{2,1,0:T(4,128)(2,1)}, u32[]{:S(2)}) copy-start(bf16[1,4,1024]{2,1,0:T(4,128)(2,1)} %param.9) | copy-start | bytes 24580
  3.2 6.8 %collective-permute-start = (bf16[24,1024]{1,0:T(8,128)(2,1)}, bf16[24,1024]{1,0:T(8,128)(2,1)S(1)}, u32[]{:S(2)}, u32[]{:S(2)}) collective-permute-start(bf16[24,1024]{1,0:T(8,128)(2,1)} %get-tuple-element.32), channel_id=1, source_target_pairs={{0,1},{1,0},{2,3},{3,2},{4,5},{5,4},{6,7},{7,6},{8,9},{9,8},{10,11... | collective-permute-start | bytes 147464 | tf_op jit(solution)/shard_map/ppermute | solution.py:570
  5.1 2.7 %copy-start.3 = (s32[16,3]{0,1:T(4,128)S(1)}, s32[16,3]{0,1:T(4,128)}, u32[]{:S(2)}) copy-start(s32[16,3]{0,1:T(4,128)} %param.11) | copy-start | bytes 580
  5.1 8.8 %collective-permute-start.1 = (bf16[24,1024]{1,0:T(8,128)(2,1)}, bf16[24,1024]{1,0:T(8,128)(2,1)S(1)}, u32[]{:S(2)}, u32[]{:S(2)}) collective-permute-start(bf16[24,1024]{1,0:T(8,128)(2,1)} %get-tuple-element.33), channel_id=1, source_target_pairs={{1,2},{2,1},{3,4},{4,3},{5,6},{6,5},{7,8},{8,7},{9,10},{10,9},{11,... | collective-permute-start | bytes 147464 | tf_op jit(solution)/shard_map/ppermute | solution.py:570
  8.5 0.7 %copy-start.1 = (f32[1,4,128]{2,1,0:T(4,128)S(1)}, f32[1,4,128]{2,1,0:T(4,128)}, u32[]{:S(2)}) copy-start(f32[1,4,128]{2,1,0:T(4,128)} %weights_hbm.1) | copy-start | bytes 6148
  15.1 9.9 %collective-permute-start.4 = (bf16[8,152,128]{2,1,0:T(8,128)(2,1)S(1)}, bf16[8,152,128]{2,1,0:T(8,128)(2,1)S(1)}, u32[]{:S(2)}, u32[]{:S(2)}) collective-permute-start(bf16[8,152,128]{2,1,0:T(8,128)(2,1)S(1)} %warp.1.x), channel_id=1, source_target_pairs={{16,48},{32,0},{48,80},{64,32},{80,112},{96,64},{112,144},{128,96}... | collective-permute-start | bytes 933896 | tf_op jit(solution)/shard_map/ppermute | solution.py:602
  18.3 13.7 %collective-permute-start.2 = (bf16[8,152,128]{2,1,0:T(8,128)(2,1)S(1)}, bf16[8,152,128]{2,1,0:T(8,128)(2,1)S(1)}, u32[]{:S(2)}, u32[]{:S(2)}) collective-permute-start(bf16[8,152,128]{2,1,0:T(8,128)(2,1)S(1)} %warp.1.x), channel_id=1, source_target_pairs={{0,32},{32,64},{48,16},{64,96},{80,48},{96,128},{112,80},{128,160}... | collective-permute-start | bytes 933896 | tf_op jit(solution)/shard_map/ppermute | solution.py:602
  22.5 15.4 %collective-permute-start.7 = (bf16[8,152,128]{2,1,0:T(8,128)(2,1)S(1)}, bf16[8,152,128]{2,1,0:T(8,128)(2,1)S(1)}, u32[]{:S(2)}, u32[]{:S(2)}) collective-permute-start(bf16[8,152,128]{2,1,0:T(8,128)(2,1)S(1)} %warp.1.x), channel_id=1, source_target_pairs={{0,16},{16,0},{32,48},{48,32},{64,80},{80,64},{96,112},{112,96},{1... | collective-permute-start | bytes 933896 | tf_op jit(solution)/shard_map/ppermute | solution.py:602
  25.0 15.8 %collective-permute-start.6 = (bf16[8,152,128]{2,1,0:T(8,128)(2,1)S(1)}, bf16[8,152,128]{2,1,0:T(8,128)(2,1)S(1)}, u32[]{:S(2)}, u32[]{:S(2)}) collective-permute-start(bf16[8,152,128]{2,1,0:T(8,128)(2,1)S(1)} %collective-permute-done.4.refs_0_), channel_id=1, source_target_pairs={{0,16},{16,0},{32,48},{48,32},{64,80},{80,64},{96,112},{112,96},{1... | collective-permute-start | bytes 933896 | tf_op jit(solution)/shard_map/ppermute | solution.py:602
  30.1 13.8 %collective-permute-start.5 = (bf16[8,152,128]{2,1,0:T(8,128)(2,1)S(1)}, bf16[8,152,128]{2,1,0:T(8,128)(2,1)S(1)}, u32[]{:S(2)}, u32[]{:S(2)}) collective-permute-start(bf16[8,152,128]{2,1,0:T(8,128)(2,1)S(1)} %collective-permute-done.4.refs_0_), channel_id=1, source_target_pairs={{16,32},{32,16},{48,64},{64,48},{80,96},{96,80},{112,128},{128,112... | collective-permute-start | bytes 933896 | tf_op jit(solution)/shard_map/ppermute | solution.py:602
  32.0 13.4 %collective-permute-start.3 = (bf16[8,152,128]{2,1,0:T(8,128)(2,1)S(1)}, bf16[8,152,128]{2,1,0:T(8,128)(2,1)S(1)}, u32[]{:S(2)}, u32[]{:S(2)}) collective-permute-start(bf16[8,152,128]{2,1,0:T(8,128)(2,1)S(1)} %collective-permute-done.2.refs_0_), channel_id=1, source_target_pairs={{0,16},{16,0},{32,48},{48,32},{64,80},{80,64},{96,112},{112,96},{1... | collective-permute-start | bytes 933896 | tf_op jit(solution)/shard_map/ppermute | solution.py:602
